TPU v7x, 128 devices: a whole 4x4x4 slice. The times are simulated.
128 devices in a mesh: rows: 32 (over z, y, core), vecs: 4 (over x).
Axes of the slice: x: 4, y: 4, z: 4, core: 2. Of those that a mesh axis runs over, the one named last changes fastest.
Arguments:
- basis: bfloat16 [100, 2097152], P('vecs', 'rows'), may hold values from -6 to 6
- coefficients: bfloat16 [100, 40], replicated, may hold values from -0.625 to 0.625
- eigen_values: float32 [40], P('vecs'), may hold values from -3 to 1
- stiffness: float32 [2097152], P('rows'), may hold values from 6.5 to 10
- damping: float32 [2097152], P('rows'), may hold values from 0.2 to 2
- mass: float32 [2097152], P('rows'), may hold values from 0.5 to 2
- link_count: int32 [32], P('rows'), may hold values from 1024 to 4096, as said below
- lower_cells: int32 [32, 4096], P('rows'), may hold values from 0 to 4095
- upper_cells: int32 [32, 4096], P('rows'), may hold values from 0 to 4095
Outputs:
- eigvecs: bfloat16 [40, 2097152], P('vecs', 'rows')
- residuals: bfloat16 [40, 2097152], P('vecs', 'rows')
- relative_norms: float32 [40], P('vecs')
Inputs may be any that keep to these rules, and one draw needn't show every extreme that they name: Interface s joins subdomain s to subdomain (s + 1) mod 32; only its first link_count[s] slots are used, the others are to be ignored. Some interface uses all 4096 slots in every draw. `lower_cells`: slots beyond link_count[s] hold values that are not used. `upper_cells`: slots beyond link_count[s] hold values that are not used.
All inputs are finite; a program needn't handle non-finite values.
Results may differ from a plain program's by a relative error of at most 0.0037.
The roundings to bfloat16 on the way count: a program that leaves them out, or rounds other values in their place, can miss the bound.
Values may be sent and summed in bfloat16 or wider, within the bound.
No kernel may reach another device: no remote copies, remote signals or barrier semaphores. Data moves between devices by JAX's collectives and lax.ppermute only.
A program may use at most 320 MiB of HBM per device.

v0:
```python
import jax
import jax.numpy as jnp
from jax import lax
from jax.sharding import PartitionSpec as P

WID = 64


def from_behind(value, axis, steps):
    count = lax.axis_size(axis)
    pairs = [(source, (source + steps) % count) for source in range(count)]
    return lax.ppermute(value, axis, pairs)


def sent_to_all(value, axis):
    devices = lax.axis_size(axis)
    return lax.all_to_all(
        jnp.broadcast_to(value[None], (devices, *value.shape)), axis, 0, 0, tiled=True
    )


def taken_together(value, axis):
    return sent_to_all(value, axis).sum(axis=0)


def packed_total(arrays, axis):
    vector, at, finished = (jnp.concatenate([a.reshape(-1) for a in arrays]), 0, [])
    subtotal = taken_together(vector, axis)
    for a in arrays:
        finished.append(subtotal[at : at + a.size].reshape(a.shape))
        at += a.size
    return tuple(finished)


def neighbours(values, width_cells):
    depth_pad = jnp.pad(values, ((0, 0), (1, 1), (0, 0)))
    total = depth_pad[:, 2:] + depth_pad[:, :-2]
    across = jnp.pad(values, ((0, 0), (0, 0), (width_cells, width_cells)))
    total = total + across[:, :, 2 * width_cells :] + across[:, :, : -2 * width_cells]
    column = jnp.arange(values.shape[2]) % width_cells
    shifted = jnp.pad(values, ((0, 0), (0, 0), (1, 1)))
    total = total + jnp.where(column < width_cells - 1, shifted[:, :, 2:], 0.0)
    total = total + jnp.where(column > 0, shifted[:, :, :-2], 0.0)
    return total


def on_device(
    basis,
    coefficients,
    eigen_values,
    stiffness,
    damping,
    mass,
    link_count,
    lower_cells,
    upper_cells,
):
    vector_part = eigen_values.shape[0]
    rows_local = basis.shape[1]
    plane_cells = WID * WID
    plane_count = rows_local // plane_cells
    quarter = lax.all_to_all(basis, "vecs", split_axis=1, concat_axis=0, tiled=True)
    quarter_vecs = jnp.dot(coefficients.T, quarter, preferred_element_type=jnp.float32).astype(
        jnp.bfloat16
    )
    eigvecs = lax.all_to_all(quarter_vecs, "vecs", split_axis=0, concat_axis=1, tiled=True)
    vectors = eigvecs.astype(jnp.float32)
    down_lower, down_upper, down_count = from_behind(
        (lower_cells, upper_cells, link_count), "rows", 1
    )
    slot_index = jnp.arange(lower_cells.shape[1], dtype=jnp.int32)
    own_used = slot_index < link_count[0]
    down_used = slot_index < down_count[0]
    planes = eigvecs.reshape(vector_part, plane_count, plane_cells)
    last_plane = planes[:, plane_count - 1, :]
    first_plane = planes[:, 0, :]
    zero_value = jnp.zeros((), jnp.bfloat16)
    send_up = jnp.where(own_used[None, :], last_plane[:, lower_cells[0]], zero_value)
    send_down = jnp.where(down_used[None, :], first_plane[:, down_upper[0]], zero_value)
    from_below = from_behind(send_up, "rows", 1)
    from_above = from_behind(send_down, "rows", -1)
    link_first = (
        jnp.zeros((vector_part, plane_cells), jnp.float32)
        .at[:, down_upper[0]]
        .add(from_below.astype(jnp.float32))
    )
    link_last = (
        jnp.zeros((vector_part, plane_cells), jnp.float32)
        .at[:, lower_cells[0]]
        .add(from_above.astype(jnp.float32))
    )
    link_sum = jnp.zeros((vector_part, plane_count, plane_cells), jnp.float32)
    link_sum = link_sum.at[:, 0, :].add(link_first).at[:, plane_count - 1, :].add(link_last)
    neighbour_sum = neighbours(vectors.reshape(vector_part, plane_count, plane_cells), WID)
    total_coupled = (neighbour_sum + link_sum).reshape(vector_part, rows_local)
    eigen_col = eigen_values[:, None]
    diagonal = (
        eigen_col * eigen_col * mass[None, :] + eigen_col * damping[None, :] + stiffness[None, :]
    )
    coupling = eigen_col * eigen_col * 0.1 + eigen_col * 0.3 + 1.0
    residual_full = diagonal * vectors - coupling * total_coupled
    local_residual = jnp.sum(residual_full * residual_full, axis=1)
    vector_sq, residual_sq = packed_total(
        (jnp.sum(vectors * vectors, axis=1), local_residual), "rows"
    )
    relative_norms = jnp.sqrt(residual_sq) / jnp.sqrt(vector_sq + 1.0)
    return (eigvecs, residual_full.astype(jnp.bfloat16), relative_norms)


def solution(mesh):
    placed = (
        P("vecs", "rows"),
        P(),
        P("vecs"),
        P("rows"),
        P("rows"),
        P("rows"),
        P("rows"),
        P("rows", None),
        P("rows", None),
    )
    return jax.shard_map(
        on_device,
        mesh=mesh,
        in_specs=placed,
        out_specs=(P("vecs", "rows"), P("vecs", "rows"), P("vecs")),
        check_vma=False,
    )
```

profile of v0, /device:TPU:1, one launch (start us, length us, event | category | flops | bytes accessed | tf_op | source)
XLA Modules:
  0.0 387.3 jit_solution(10114052916482525448)
XLA Ops:
  0.6 6.3 %all_to_all.34 = bf16[25,4,16384]{2,1,0:T(4,128)(2,1)S(1)} reshape(bf16[25,65536]{1,0:T(8,128)(2,1)} %param.13) | data formatting | bytes 6553600 | tf_op jit(solution)/shard_map/all_to_all | solution.py:62
  7.0 3.8 copy.53
  10.8 5.0 %all-to-all-start = ((bf16[25,4,16384]{2,0,1:T(8,128)(2,1)}), bf16[25,4,16384]{2,0,1:T(8,128)(2,1)}, u32[]{:S(2)}, u32[]{:S(2)}) async-start(bf16[25,4,16384]{2,0,1:T(8,128)(2,1)} %copy.53), calls=%async_computation | async-start | bytes 8388608 | tf_op jit(solution)/shard_map/all_to_all | solution.py:62
  15.8 2.7 collective-permute-start
  24.8 39.8 %all-to-all-done = bf16[25,4,16384]{2,0,1:T(8,128)(2,1)} async-done(((bf16[25,4,16384]{2,0,1:T(8,128)(2,1)}), bf16[25,4,16384]{2,0,1:T(8,128)(2,1)}, u32[]{:S(2)}, u32[]{:S(2)}) %all-to-all-start) | async-done | bytes 3276832 | tf_op jit(solution)/shard_map/all_to_all | solution.py:62
  64.6 3.3 all_to_all.37
  67.9 1.9 convolution_convert_fusion
  69.8 3.1 all_to_all.38
  73.0 3.6 all-to-all-start.1
  76.7 24.7 %all-to-all-done.1 = bf16[4,10,16384]{2,1,0:T(8,128)(2,1)S(1)} async-done(((bf16[4,10,16384]{2,1,0:T(8,128)(2,1)}), bf16[4,10,16384]{2,1,0:T(8,128)(2,1)S(1)}, u32[]{:S(2)}, u32[]{:S(2)}) %all-to-all-start.1) | async-done | bytes 1310752 | tf_op jit(solution)/shard_map/all_to_all | solution.py:66
  101.3 10.9 %copy.55 = bf16[10,4,16384]{0,2,1:T(8,128)(2,1)} copy(bf16[10,4,16384]{2,0,1:T(8,128)(2,1)S(1)} %bitcast.40) | data formatting | bytes 2621440 | tf_op jit(solution)/shard_map/all_to_all | solution.py:66
  112.3 2.6 slice_bitcast_fusion
  114.9 15.0 %gather_fusion = bf16[4096,10]{1,0:T(8,128)(2,1)} fusion(bf16[10,4096]{0,1:T(8,128)(2,1)S(1)} %get-tuple-element.30, s32[4096]{0:T(1024)S(1)} %broadcast_clamp_fusion.1), kind=kCustom, calls=%fused_computation | custom fusion | bytes 180224 | tf_op jit(solution)/shard_map/gather | solution.py:78
  130.0 3.4 select_bitcast_fusion.1
  133.7 4.3 %collective-permute-start.1 = (bf16[10,4096]{1,0:T(8,128)(2,1)S(1)}, bf16[10,4096]{1,0:T(8,128)(2,1)}, u32[]{:S(2)}, u32[]{:S(2)}) collective-permute-start(bf16[10,4096]{1,0:T(8,128)(2,1)S(1)} %copy.56), channel_id=1, source_target_pairs={{0,4},{4,8},{8,12},{12,16},{16,20},{20,24},{24,28},{28,32},{32,36}... | collective-permute-start | bytes 245768 | tf_op jit(solution)/shard_map/ppermute | solution.py:12
  138.0 12.4 %gather_fusion.1 = bf16[4096,10]{1,0:T(8,128)(2,1)S(1)} fusion(bf16[10,4096]{0,1:T(8,128)(2,1)} %get-tuple-element.29, s32[4096]{0:T(1024)S(1)} %broadcast_clamp_fusion), kind=kCustom, calls=%fused_computation.1 | custom fusion | bytes 180224 | tf_op jit(solution)/shard_map/gather | solution.py:79
  150.4 2.9 select_bitcast_fusion
  153.3 18.2 %convert_element_type.30 = f32[10,16,4096]{0,2,1:T(8,128)} convert(bf16[10,16,4096]{0,2,1:T(8,128)(2,1)} %bitcast.39) | non-fusion elementwise | flops 655360 | bytes 3932160 | tf_op jit(solution)/shard_map/convert_element_type | solution.py:67
  172.5 2.3 copy.58
  175.6 2.5 copy.66
  179.0 2.0 copy.57
  180.9 24.0 %scatter_custom_fusion = f32[10,4096]{0,1:T(8,128)} fusion(s32[4096]{0:T(1024)} %bitcast.49, f32[4096,10]{1,0:T(8,128)} %copy.57, f32[]{:T(128)} %constant.81.clone.1), kind=kCustom, calls=%fused_computation.27 | custom fusion | flops 40960 | bytes 164352 | tf_op jit(solution)/shard_map/scatter-add | solution.py:85
  205.0 12.1 %scatter-add.25 = f32[10,16,4096]{0,2,1:T(8,128)} pad(f32[10,1,4096]{0,2,1:T(8,128)} %bitcast.44, f32[]{:T(128)} %constant.81.clone.1), padding=0_0x0_15x0_0 | pad | bytes 2785284 | tf_op jit(solution)/shard_map/scatter-add | solution.py:93
  218.0 2.0 copy.59
  220.0 24.0 %scatter_custom_fusion.1 = f32[10,4096]{0,1:T(8,128)} fusion(s32[4096]{0:T(1024)} %bitcast.47, f32[4096,10]{1,0:T(8,128)} %copy.59, f32[]{:T(128)} %constant.81.clone.1), kind=kCustom, calls=%fused_computation.25 | custom fusion | flops 40960 | bytes 164352 | tf_op jit(solution)/shard_map/scatter-add | solution.py:90
  244.0 3.0 bitcast_dynamic-update-slice_fusion
  247.0 82.5 %fusion.5 = f32[10,16,4096]{0,2,1:T(8,128)} fusion(f32[10,16,4096]{0,2,1:T(8,128)} %bitcast_dynamic-update-slice_fusion, f32[10,16,4096]{0,2,1:T(8,128)} %convert_element_type.30, pred[4096]{0:T(1024)(128)(4,1)S(1)} %get-tuple-element.33, pred[4096]{0:T(1024)(128)(4,1)S(1)} %copy-done.14), kind=kLoop, calls=%fused_computation.11 | loop fusion | flops 5242880 | bytes 7872512 | tf_op jit(solution)/shard_map/add | solution.py:95
  329.6 19.5 %copy.61 = f32[10,4,16384]{2,0,1:T(8,128)} copy(f32[10,4,16384]{0,2,1:T(8,128)} %bitcast.36) | data formatting | bytes 5242880 | tf_op jit(solution)/shard_map/reshape | solution.py:95
  349.1 3.6 fusion.6
  353.5 8.7 %all-to-all-start.2 = ((f32[32,1,20]{2,1,0:T(1,128)}), f32[32,1,20]{2,1,0:T(1,128)S(1)}, u32[]{:S(2)}, u32[]{:S(2)}) async-start(f32[32,1,20]{2,1,0:T(1,128)} %broadcast_in_dim.53), calls=%async_computation.2 | async-start | bytes 32768 | tf_op jit(solution)/shard_map/all_to_all | solution.py:17
  362.2 19.6 %copy.60 = f32[10,65536]{1,0:T(8,128)} copy(f32[10,65536]{0,1:T(8,128)} %bitcast.37) | data formatting | bytes 5242880 | tf_op jit(solution)/shard_map/reshape | solution.py:95
  381.8 4.8 %subtract_convert_fusion = bf16[10,65536]{1,0:T(8,128)(2,1)} fusion(f32[10,65536]{1,0:T(8,128)} %copy.60, bf16[10,65536]{1,0:T(8,128)(2,1)S(1)} %bitcast.43, f32[10]{0:T(128)S(1)} %copy-done.19, f32[65536]{0:T(1024)S(1)} %copy-done.4, f32[65536]{0:T(1024)S(1)} %copy-done.6, f32[10]{0:T(128)S(1)} %copy-done.18, f32[65536]{0:T(1024)S(1)} %copy-done.8, ...), kind=kLoop, calls=%fused_computation.19 | loop fusion | flops 5898240 | bytes 6029432 | tf_op jit(solution)/shard_map/convert_element_type | solution.py:107
  (71 shorter events, 11.0 us)
Async XLA Ops:
  0.6 67.3 %copy-start = (bf16[100,40]{0,1:T(8,128)(2,1)S(1)}, bf16[100,40]{0,1:T(8,128)(2,1)}, u32[]{:S(2)}) copy-start(bf16[100,40]{0,1:T(8,128)(2,1)} %param.14) | copy-start | bytes 24004
  10.8 5.0 %copy-start.21 = (s32[1,4096]{1,0:T(1,128)S(1)}, s32[1,4096]{1,0:T(1,128)}, u32[]{:S(2)}) copy-start(s32[1,4096]{1,0:T(1,128)} %param.21) | copy-start | bytes 49156
  10.8 8.6 %copy-start.3 = (f32[65536]{0:T(1024)S(1)}, f32[65536]{0:T(1024)}, u32[]{:S(2)}) copy-start(f32[65536]{0:T(1024)} %param.16) | copy-start | bytes 786436
  10.8 9.4 %copy-start.5 = (f32[65536]{0:T(1024)S(1)}, f32[65536]{0:T(1024)}, u32[]{:S(2)}) copy-start(f32[65536]{0:T(1024)} %param.17) | copy-start | bytes 786436
  10.8 10.2 %copy-start.7 = (f32[65536]{0:T(1024)S(1)}, f32[65536]{0:T(1024)}, u32[]{:S(2)}) copy-start(f32[65536]{0:T(1024)} %param.18) | copy-start | bytes 786436
  10.8 11.6 %copy-start.17 = (f32[10]{0:T(128)S(1)}, f32[10]{0:T(128)}, u32[]{:S(2)}) copy-start(f32[10]{0:T(128)} %param.15) | copy-start | bytes 124
  10.8 12.1 %copy-start.16 = (s32[1,4096]{1,0:T(1,128)S(1)}, s32[1,4096]{1,0:T(1,128)}, u32[]{:S(2)}) copy-start(s32[1,4096]{1,0:T(1,128)} %param.20) | copy-start | bytes 49156
  10.8 53.8 %all-to-all-start = ((bf16[25,4,16384]{2,0,1:T(8,128)(2,1)}), bf16[25,4,16384]{2,0,1:T(8,128)(2,1)}, u32[]{:S(2)}, u32[]{:S(2)}) async-start(bf16[25,4,16384]{2,0,1:T(8,128)(2,1)} %copy.53), calls=%async_computation | async-start | bytes 8388608 | tf_op jit(solution)/shard_map/all_to_all | solution.py:62
  15.8 60.8 %collective-permute-start = (s32[1,4096]{1,0:T(1,128)S(1)}, s32[1,4096]{1,0:T(1,128)S(1)}, u32[]{:S(2)}, u32[]{:S(2)}) collective-permute-start(s32[1,4096]{1,0:T(1,128)S(1)} %copy-done.21), channel_id=1, source_target_pairs={{0,4},{4,8},{8,12},{12,16},{16,20},{20,24},{24,28},{28,32},{32,36}... | collective-permute-start | bytes 49160 | tf_op jit(solution)/shard_map/ppermute | solution.py:12
  18.6 5.0 %collective-permute-start.2 = (s32[1]{0:T(128)}, s32[1]{0:T(128)}, u32[]{:S(2)}, u32[]{:S(2)}) collective-permute-start(s32[1]{0:T(128)} %param.19), channel_id=1, source_target_pairs={{0,4},{4,8},{8,12},{12,16},{16,20},{20,24},{24,28},{28,32},{32,36}... | collective-permute-start | bytes 20 | tf_op jit(solution)/shard_map/ppermute | solution.py:12
  23.0 0.6 copy-start.12
  73.0 28.4 %all-to-all-start.1 = ((bf16[4,10,16384]{2,1,0:T(8,128)(2,1)}), bf16[4,10,16384]{2,1,0:T(8,128)(2,1)S(1)}, u32[]{:S(2)}, u32[]{:S(2)}) async-start(bf16[4,10,16384]{2,1,0:T(8,128)(2,1)} %all_to_all.38), calls=%async_computation.1 | async-start | bytes 4194304 | tf_op jit(solution)/shard_map/all_to_all | solution.py:66
  76.6 35.6 %copy-start.13 = (s32[4096,1]{0,1:T(1,128)}, s32[4096,1]{0,1:T(1,128)S(1)}, u32[]{:S(2)}) copy-start(s32[4096,1]{0,1:T(1,128)S(1)} %compare_select_fusion.1) | copy-start | bytes 49156
  112.3 38.2 %copy-start.15 = (pred[4096]{0:T(1024)(128)(4,1)S(1)}, pred[4096]{0:T(1024)(128)(4,1)}, u32[]{:S(2)}) copy-start(pred[4096]{0:T(1024)(128)(4,1)} %iota_compare_fusion) | copy-start | bytes 12292
  133.7 44.3 %collective-permute-start.1 = (bf16[10,4096]{1,0:T(8,128)(2,1)S(1)}, bf16[10,4096]{1,0:T(8,128)(2,1)}, u32[]{:S(2)}, u32[]{:S(2)}) collective-permute-start(bf16[10,4096]{1,0:T(8,128)(2,1)S(1)} %copy.56), channel_id=1, source_target_pairs={{0,4},{4,8},{8,12},{12,16},{16,20},{20,24},{24,28},{28,32},{32,36}... | collective-permute-start | bytes 245768 | tf_op jit(solution)/shard_map/ppermute | solution.py:12
  174.8 42.3 %collective-permute-start.3 = (bf16[10,4096]{1,0:T(8,128)(2,1)}, bf16[10,4096]{1,0:T(8,128)(2,1)}, u32[]{:S(2)}, u32[]{:S(2)}) collective-permute-start(bf16[10,4096]{1,0:T(8,128)(2,1)} %copy.58), channel_id=1, source_target_pairs={{0,124},{4,0},{8,4},{12,8},{16,12},{20,16},{24,20},{28,24},{32,28}... | collective-permute-start | bytes 245768 | tf_op jit(solution)/shard_map/ppermute | solution.py:12
  218.0 29.1 %copy-start.14 = (pred[4096]{0:T(1024)(128)(4,1)S(1)}, pred[4096]{0:T(1024)(128)(4,1)}, u32[]{:S(2)}) copy-start(pred[4096]{0:T(1024)(128)(4,1)} %get-tuple-element.34) | copy-start | bytes 12292
  329.6 19.5 %copy-start.9 = (f32[4,16384]{1,0:T(4,128)S(1)}, f32[4,16384]{1,0:T(4,128)}, u32[]{:S(2)}) copy-start(f32[4,16384]{1,0:T(4,128)} %add.120) | copy-start | bytes 786436
  329.6 19.5 %copy-start.10 = (f32[4,16384]{1,0:T(4,128)S(1)}, f32[4,16384]{1,0:T(4,128)}, u32[]{:S(2)}) copy-start(f32[4,16384]{1,0:T(4,128)} %mul.102) | copy-start | bytes 786436
  329.6 19.5 %copy-start.11 = (f32[4,16384]{1,0:T(4,128)S(1)}, f32[4,16384]{1,0:T(4,128)}, u32[]{:S(2)}) copy-start(f32[4,16384]{1,0:T(4,128)} %mul.98) | copy-start | bytes 786436
  329.6 19.5 %copy-start.18 = (f32[10]{0:T(128)S(1)}, f32[10]{0:T(128)}, u32[]{:S(2)}) copy-start(f32[10]{0:T(128)} %param.15) | copy-start | bytes 124
  329.6 19.5 %copy-start.19 = (f32[10]{0:T(128)S(1)}, f32[10]{0:T(128)}, u32[]{:S(2)}) copy-start(f32[10]{0:T(128)} %get-tuple-element.31) | copy-start | bytes 124
  329.6 19.5 %copy-start.20 = (f32[10]{0:T(128)S(1)}, f32[10]{0:T(128)}, u32[]{:S(2)}) copy-start(f32[10]{0:T(128)} %get-tuple-element.32) | copy-start | bytes 124
  353.5 33.1 %all-to-all-start.2 = ((f32[32,1,20]{2,1,0:T(1,128)}), f32[32,1,20]{2,1,0:T(1,128)S(1)}, u32[]{:S(2)}, u32[]{:S(2)}) async-start(f32[32,1,20]{2,1,0:T(1,128)} %broadcast_in_dim.53), calls=%async_computation.2 | async-start | bytes 32768 | tf_op jit(solution)/shard_map/all_to_all | solution.py:17
  362.2 19.6 %copy-start.2 = (bf16[2,8,4,16384]{3,1,2,0:T(8,128)(2,1)S(1)}, bf16[2,8,4,16384]{3,1,2,0:T(8,128)(2,1)}, u32[]{:S(2)}) copy-start(bf16[2,8,4,16384]{3,1,2,0:T(8,128)(2,1)} %copy.66) | copy-start | bytes 6291460
  362.2 19.6 %copy-start.4 = (f32[65536]{0:T(1024)S(1)}, f32[65536]{0:T(1024)}, u32[]{:S(2)}) copy-start(f32[65536]{0:T(1024)} %param.16) | copy-start | bytes 786436
  362.2 19.6 %copy-start.6 = (f32[65536]{0:T(1024)S(1)}, f32[65536]{0:T(1024)}, u32[]{:S(2)}) copy-start(f32[65536]{0:T(1024)} %param.17) | copy-start | bytes 786436
  362.2 19.6 %copy-start.8 = (f32[65536]{0:T(1024)S(1)}, f32[65536]{0:T(1024)}, u32[]{:S(2)}) copy-start(f32[65536]{0:T(1024)} %param.18) | copy-start | bytes 786436
  381.8 5.5 %copy-start.1 = (bf16[100,40]{0,1:T(8,128)(2,1)S(1)}, bf16[100,40]{0,1:T(8,128)(2,1)}, u32[]{:S(2)}) copy-start(bf16[100,40]{0,1:T(8,128)(2,1)} %param.14) | copy-start | bytes 24004
where the time goes:
time: 389 us; the launch traced here: 387 us
  other arithmetic  168 us (43%)
  local copies, waits for them, and re-layouts  126 us (32%)
  waiting for transfers between devices  64.5 us (17%)
  starting transfers between devices  24.4 us (6%)
    add x1, other arithmetic, on_device(): total_coupled = (neighbour_sum + link_sum).reshape(vector_part, rows_local)  82.5 us
    all_to_all x1, waiting for transfers between devices, on_device(): lax.all_to_all(basis, 'vecs', split_axis=1, concat_axis=0, tiled=True)  39.8 us
    reshape x2, local copies, waits for them, and re-layouts, on_device(): total_coupled = (neighbour_sum + link_sum).reshape(vector_part, rows_local)  39 us
    all_to_all x1, waiting for transfers between devices, on_device(): lax.all_to_all(quarter_vecs, 'vecs', split_axis=0, concat_axis=1, tiled=T...  24.7 us
    scatter-add x1, other arithmetic, on_device(): link_last = jnp.zeros((vector_part, plane_cells), jnp.float32).at[:, lowe...  24 us
    scatter-add x1, other arithmetic, on_device(): link_first = jnp.zeros((vector_part, plane_cells), jnp.float32).at[:, dow...  24 us
    convert_element_type x1, other arithmetic, on_device(): vectors = eigvecs.astype(jnp.float32)  18.2 us
    scatter-add x2, local copies, waits for them, and re-layouts, on_device(): link_sum.at[:, 0, :].add(link_first).at[:, plane_count - 1, :]  15.1 us
  transfers between devices with their start and end apart: 7, of which 2 were waited for; matrix products, arithmetic and copies ran while one was open for 28% of the time, Pallas kernels for 0%

commit v1 on v0

v1 whole, which is shorter than its diff:
```python
import functools

import jax
import jax.numpy as jnp
import numpy as np
from jax import lax
from jax.experimental import pallas as pl
from jax.experimental.pallas import tpu as pltpu
from jax.sharding import PartitionSpec as P

WID = 64
LANES = 128
SEGS = 8
NP = 16
BF = jnp.bfloat16
F32 = jnp.float32


def from_behind(value, axis, steps):
    count = lax.axis_size(axis)
    pairs = [(source, (source + steps) % count) for source in range(count)]
    return lax.ppermute(value, axis, pairs)


def cost(flops, nbytes):
    return pl.CostEstimate(flops=int(flops), bytes_accessed=int(nbytes), transcendentals=0)


def pack_kernel(starts, width, basis_ref, out_ref, buf, obuf, sem_in, sem_out):
    ranks = basis_ref.shape[0]
    full = ranks // 8 * 8
    rest = ranks - full
    seg = width // SEGS
    reads = [
        pltpu.make_async_copy(basis_ref.at[:, pl.ds(st, width)], buf.at[v], sem_in.at[v])
        for v, st in enumerate(starts)
    ]
    writes = [
        pltpu.make_async_copy(obuf.at[v], out_ref.at[v], sem_out.at[v]) for v in range(len(starts))
    ]
    for r in reads:
        r.start()
    for v in range(len(starts)):
        reads[v].wait()
        for c in range(SEGS):
            obuf[v, c * full : (c + 1) * full, :] = buf[v, 0:full, c * seg : (c + 1) * seg]
        tail = [buf[v, full:ranks, c * seg : (c + 1) * seg] for c in range(SEGS)]
        obuf[v, SEGS * full : SEGS * ranks, :] = jnp.concatenate(tail, axis=0)
        if v > 0:
            writes[v - 1].start()
    writes[-1].start()
    for w in writes:
        w.wait()


def pack(basis, starts, width):
    ranks = basis.shape[0]
    n = len(starts)
    seg = width // SEGS
    return pl.pallas_call(
        functools.partial(pack_kernel, starts, width),
        out_shape=jax.ShapeDtypeStruct((n, SEGS * ranks, seg), BF),
        in_specs=[pl.BlockSpec(memory_space=pl.ANY)],
        out_specs=pl.BlockSpec(memory_space=pl.ANY),
        scratch_shapes=[
            pltpu.VMEM((n, ranks, width), BF),
            pltpu.VMEM((n, SEGS * ranks, seg), BF),
            pltpu.SemaphoreType.DMA((n,)),
            pltpu.SemaphoreType.DMA((n,)),
        ],
        cost_estimate=cost(0, 4 * n * ranks * width),
        name="pack",
    )(basis)


def row_orders(parts, ranks, vecs):
    full = ranks // 8 * 8
    rest = ranks - full
    vfull = vecs // 8 * 8
    vrest = vecs - vfull
    col_rank, col_seg = [], []
    for s in range(parts):
        for c in range(SEGS):
            for r in range(full):
                col_rank.append(s * ranks + r)
                col_seg.append(c)
        for c in range(SEGS):
            for r in range(rest):
                col_rank.append(s * ranks + full + r)
                col_seg.append(c)
    row_vec, row_seg = [], []
    for v in range(parts):
        for c in range(SEGS):
            for j in range(vfull):
                row_vec.append(v * vecs + j)
                row_seg.append(c)
        for c in range(SEGS):
            for j in range(vrest):
                row_vec.append(v * vecs + vfull + j)
                row_seg.append(c)
    return [np.array(a, np.int32) for a in (col_rank, col_seg, row_vec, row_seg)]


def spread_kernel(coef_ref, cr_ref, cs_ref, rv_ref, rs_ref, out_ref):
    total, vecs = coef_ref.shape
    cols, rows = cr_ref.shape[1], rv_ref.shape[0]
    pick_rank = (lax.broadcasted_iota(jnp.int32, (total, cols), 0) == cr_ref[...]).astype(F32).astype(BF)
    pick_vec = (lax.broadcasted_iota(jnp.int32, (rows, vecs), 1) == rv_ref[...]).astype(F32).astype(BF)
    by_row = lax.dot_general(
        pick_vec, coef_ref[...], (((1,), (1,)), ((), ())), preferred_element_type=F32
    ).astype(BF)
    spread = jnp.dot(by_row, pick_rank, preferred_element_type=F32)
    out_ref[...] = jnp.where(rs_ref[...] == cs_ref[...], spread, 0.0).astype(BF)


def spread_coefficients(coefficients, parts, ranks, vecs):
    cr, cs, rv, rs = row_orders(parts, ranks, vecs)
    return pl.pallas_call(
        spread_kernel,
        out_shape=jax.ShapeDtypeStruct((rv.size, cr.size), BF),
        cost_estimate=cost(2 * rv.size * cr.size * parts * ranks, 2 * rv.size * cr.size),
        name="spread",
    )(
        coefficients,
        jnp.asarray(cr)[None, :],
        jnp.asarray(cs)[None, :],
        jnp.asarray(rv)[:, None],
        jnp.asarray(rs)[:, None],
    )


def mix_kernel(l_ref, y_ref, out_ref):
    out_ref[...] = jnp.dot(l_ref[...], y_ref[...], preferred_element_type=F32).astype(BF)


def mix(spread, packed):
    rows, depth = spread.shape
    lanes = packed.shape[1]
    step = 256
    return pl.pallas_call(
        mix_kernel,
        out_shape=jax.ShapeDtypeStruct((rows, lanes), BF),
        grid=(lanes // step,),
        in_specs=[
            pl.BlockSpec((rows, depth), lambda i: (0, 0)),
            pl.BlockSpec((depth, step), lambda i: (0, i)),
        ],
        out_specs=pl.BlockSpec((rows, step), lambda i: (0, i)),
        cost_estimate=cost(2 * rows * depth * lanes, 2 * (rows + depth) * lanes),
        name="mix",
    )(spread, packed)


def link_kernel(plane_ref, g_ref, s_ref, n_ref, out_ref, hot_s, put):
    nd, rows2, low = plane_ref.shape
    slots = g_ref.shape[2]
    half_rows = rows2 // 2
    vfull, vrest = 8, half_rows // SEGS - 8
    step = 512
    for d in range(nd):

        def build(i, _):
            at = pl.ds(pl.multiple_of(i * step, step), step)
            lane = lax.broadcasted_iota(jnp.int32, (low, step), 0)
            g = g_ref[d, :, at]
            s = s_ref[d, :, at]
            slot = lax.broadcasted_iota(jnp.int32, (1, step), 1) + i * step
            used = slot < n_ref[d]
            hot_g = jnp.where(lane == jnp.bitwise_and(g, low - 1), 1.0, 0.0).astype(BF)
            got = jnp.dot(plane_ref[d], hot_g, preferred_element_type=F32)
            gh = lax.shift_right_logical(g, 8)
            sh = jnp.where(used, lax.shift_right_logical(s, 8), -1)
            main = jnp.zeros((vfull, step), F32)
            tail = jnp.zeros((SEGS * vrest, step), F32)
            tail_seg = lax.broadcasted_iota(jnp.int32, (SEGS * vrest, step), 0) // vrest
            for h in range(2):
                base = h * half_rows
                for c in range(SEGS):
                    part = got[base + c * vfull : base + (c + 1) * vfull]
                    main = main + jnp.where(gh == h * SEGS + c, part, 0.0)
                part = got[base + SEGS * vfull : base + half_rows]
                tail = tail + jnp.where(gh == tail_seg + h * SEGS, part, 0.0)
            same = lax.broadcasted_iota(jnp.int32, (SEGS * vrest, SEGS * vrest), 0) % vrest == (
                lax.broadcasted_iota(jnp.int32, (SEGS * vrest, SEGS * vrest), 1) % vrest
            )
            tail = jnp.dot(
                jnp.where(same, 1.0, 0.0).astype(BF), tail.astype(BF), preferred_element_type=F32
            )
            pieces = []
            for h in range(2):
                for c in range(SEGS):
                    pieces.append(jnp.where(sh == h * SEGS + c, main, 0.0))
                pieces.append(jnp.where(sh == tail_seg + h * SEGS, tail, 0.0))
            put[:, at] = jnp.concatenate(pieces, axis=0).astype(BF)
            hot_s[:, at] = jnp.where(lane == jnp.bitwise_and(s, low - 1), 1.0, 0.0).astype(BF)
            return 0

        lax.fori_loop(0, slots // step, build, 0)
        total = lax.dot_general(
            put[...], hot_s[...], (((1,), (1,)), ((), ())), preferred_element_type=F32
        )
        for h in range(2):
            base = h * half_rows
            for c in range(SEGS):
                for k in range(low // LANES):
                    t = d * 32 + (h * SEGS + c) * (low // LANES) + k
                    at = slice(k * LANES, (k + 1) * LANES)
                    out_ref[t, 0:8, :] = total[base + c * 8 : base + (c + 1) * 8, at]
                    first = base + SEGS * 8 + c * vrest
                    out_ref[t, 8 : 8 + vrest, :] = total[first : first + vrest, at]


def link_terms(plane, g, s, n):
    nd, rows2, low = plane.shape
    slots = g.shape[2]
    return pl.pallas_call(
        link_kernel,
        out_shape=jax.ShapeDtypeStruct((nd * 32, NP, LANES), F32),
        in_specs=[
            pl.BlockSpec(memory_space=pltpu.VMEM),
            pl.BlockSpec(memory_space=pltpu.VMEM),
            pl.BlockSpec(memory_space=pltpu.VMEM),
            pl.BlockSpec(memory_space=pltpu.SMEM),
        ],
        out_specs=pl.BlockSpec(memory_space=pltpu.VMEM),
        scratch_shapes=[
            pltpu.VMEM((low, slots), BF),
            pltpu.VMEM((rows2, slots), BF),
        ],
        cost_estimate=cost(nd * 4 * rows2 * low * slots, nd * 4 * rows2 * low),
        name="links",
    )(plane, g, s, n)


def residual_kernel(
    chunks, planes, z_refs, link_ref, eig_ref, stiff_ref, damp_ref, mass_ref,
    vec_ref, res_ref, sum_ref, cells
):
    tiles = WID * WID // LANES
    vecs = vec_ref.shape[0]
    vrest = vecs - 8
    lane = lax.broadcasted_iota(jnp.int32, (1, LANES), 1)
    low_half = lane < WID
    column = jnp.bitwise_and(lane, WID - 1)
    not_first, not_last = column > 0, column < WID - 1
    blank = jnp.zeros((tiles, NP, LANES), F32)
    cells[0:tiles] = blank
    cells[(planes + 1) * tiles : (planes + 2) * tiles] = blank
    for (starts, width), z_ref in zip(chunks, z_refs):
        seg = width // SEGS
        for v, st in enumerate(starts):
            for c in range(SEGS):
                for k in range(seg // LANES):
                    t = (st + c * seg) // LANES + k
                    at = slice(k * LANES, (k + 1) * LANES)
                    top = z_ref[v, c * 8 : (c + 1) * 8, at]
                    first = SEGS * 8 + c * vrest
                    low = z_ref[v, first : first + vrest, at]
                    cells[tiles + t, 0:8, :] = top.astype(F32)
                    cells[tiles + t, 8 : 8 + vrest, :] = low.astype(F32)
    eig = jnp.concatenate([eig_ref[...], jnp.zeros((NP - vecs, 1), F32)], axis=0)
    eig = jnp.broadcast_to(eig, (NP, LANES))
    eig_sq = eig * eig
    coupling = eig_sq * 0.1 + eig * 0.3 + 1.0

    def plane(z, carry, link):
        vsum, rsum = carry
        base = pl.multiple_of((z + 1) * tiles, tiles)
        for i in range(tiles):
            x = cells[base + i]
            ahead = cells[base + i + 1] if i + 1 < tiles else None
            behind = cells[base + i - 1] if i > 0 else None
            if behind is None:
                across = jnp.where(low_half, ahead, 0.0)
            elif ahead is None:
                across = jnp.where(low_half, 0.0, behind)
            else:
                across = jnp.where(low_half, ahead, behind)
            total = pltpu.roll(x + across, WID, 1)
            total = total + jnp.where(not_first, pltpu.roll(x, 1, 1), 0.0)
            total = total + jnp.where(not_last, pltpu.roll(x, LANES - 1, 1), 0.0)
            total = total + (cells[base + i - tiles] + cells[base + i + tiles])
            if link is not None:
                total = total + link_ref[link * tiles + i]
            row = pl.ds(z * tiles + i, 1)
            diagonal = eig_sq * mass_ref[row, :] + eig * damp_ref[row, :] + stiff_ref[row, :]
            res = diagonal * x - coupling * total
            at = pl.ds(pl.multiple_of(z * WID * WID + i * LANES, LANES), LANES)
            vec_ref[:, at] = x[:vecs].astype(BF)
            res_ref[:, at] = res[:vecs].astype(BF)
            vsum = vsum + x * x
            rsum = rsum + res * res
        return vsum, rsum

    zero = jnp.zeros((NP, LANES), F32)
    carry = plane(0, (zero, zero), 0)
    carry = lax.fori_loop(1, planes - 1, lambda z, c: plane(z, c, None), carry)
    vsum, rsum = plane(planes - 1, carry, 1)
    vrow = jnp.broadcast_to(jnp.sum(vsum, axis=1, keepdims=True), (NP, LANES))
    rrow = jnp.broadcast_to(jnp.sum(rsum, axis=1, keepdims=True), (NP, LANES))
    sub = lax.broadcasted_iota(jnp.int32, (NP, LANES), 0)
    wide = lax.broadcasted_iota(jnp.int32, (NP, LANES), 1)
    both = jnp.where((sub == wide) & (sub < vecs), vrow, 0.0)
    both = both + jnp.where((sub + NP == wide) & (sub < vecs), rrow, 0.0)
    line = jnp.sum(both, axis=0, keepdims=True)
    sum_ref[...] = jnp.broadcast_to(line[None], sum_ref.shape)


def residual(chunks, zs, link, eig, stiff, damp, mass, vecs, rows_local, copies):
    planes = rows_local // (WID * WID)
    nz = len(zs)
    tiles = WID * WID // LANES

    def kernel(*refs):
        residual_kernel(chunks, planes, refs[:nz], *refs[nz:])

    return pl.pallas_call(
        kernel,
        out_shape=(
            jax.ShapeDtypeStruct((vecs, rows_local), BF),
            jax.ShapeDtypeStruct((vecs, rows_local), BF),
            jax.ShapeDtypeStruct((copies, 1, LANES), F32),
        ),
        in_specs=[pl.BlockSpec(memory_space=pltpu.VMEM)] * (nz + 5),
        out_specs=(pl.BlockSpec(memory_space=pltpu.VMEM),) * 3,
        scratch_shapes=[pltpu.VMEM(((planes + 2) * tiles, NP, LANES), F32)],
        cost_estimate=cost(40 * NP * rows_local, 8 * NP * rows_local),
        name="residual",
    )(*zs, link, eig, stiff, damp, mass)


def on_device(
    basis,
    coefficients,
    eigen_values,
    stiffness,
    damping,
    mass,
    link_count,
    lower_cells,
    upper_cells,
):
    parts = lax.axis_size("vecs")
    subdomains = lax.axis_size("rows")
    vecs = eigen_values.shape[0]
    ranks, rows_local = basis.shape
    plane = WID * WID
    planes = rows_local // plane
    half = plane // 2
    inner = (planes - 2) * plane // parts
    chunks = [
        ((0, half, (planes - 1) * plane, (planes - 1) * plane + half), half),
        (tuple(plane + v * inner for v in range(parts)), inner),
    ]
    down_lower, down_upper, down_count = from_behind(
        (lower_cells, upper_cells, link_count), "rows", 1
    )
    spread = spread_coefficients(coefficients, parts, ranks, vecs)
    packed = [pack(basis, starts, width) for starts, width in chunks]
    arrived = [lax.all_to_all(p, "vecs", 0, 0, tiled=True) for p in packed]
    mixed = [
        mix(spread, a.reshape(parts * SEGS * ranks, -1)).reshape(parts, SEGS * vecs, -1)
        for a in arrived
    ]
    back = [lax.all_to_all(m, "vecs", 0, 0, tiled=True) for m in mixed]
    ends = back[0].reshape(2, 2 * SEGS * vecs, -1)
    from_below = from_behind(ends[1:2], "rows", 1)
    from_above = from_behind(ends[0:1], "rows", -1)
    link = link_terms(
        jnp.concatenate([from_below, from_above], axis=0),
        jnp.stack([down_lower, upper_cells]),
        jnp.stack([down_upper, lower_cells]),
        jnp.concatenate([down_count, link_count]),
    )
    as_tiles = lambda a: a.reshape(rows_local // LANES, LANES)
    eigvecs, residuals, sums = residual(
        chunks, back, link, eigen_values[:, None], as_tiles(stiffness), as_tiles(damping),
        as_tiles(mass), vecs, rows_local, subdomains,
    )
    total = lax.all_to_all(sums, "rows", 0, 0, tiled=True).sum(axis=(0, 1))
    vector_sq, residual_sq = total[:vecs], total[NP : NP + vecs]
    relative_norms = jnp.sqrt(residual_sq) / jnp.sqrt(vector_sq + 1.0)
    return (eigvecs, residuals, relative_norms)


def solution(mesh):
    placed = (
        P("vecs", "rows"),
        P(),
        P("vecs"),
        P("rows"),
        P("rows"),
        P("rows"),
        P("rows"),
        P("rows", None),
        P("rows", None),
    )
    return jax.shard_map(
        on_device,
        mesh=mesh,
        in_specs=placed,
        out_specs=(P("vecs", "rows"), P("vecs", "rows"), P("vecs")),
        check_vma=False,
    )
```

time: 389 us -> 111 us (0.29)
  other arithmetic: 168 us -> 3.8 us
  local copies, waits for them, and re-layouts: 126 us -> 3.23 us
  waiting for transfers between devices: 64.5 us -> 25.3 us
  Pallas kernels: 0 us -> 34 us
  blocking collectives: 0 us -> 16.9 us
    add x2 -> x0, other arithmetic: 83.1 us -> none  [the longest x1 82.5 us: on_device(): total_coupled = (neighbour_sum + link_sum).reshape(vector_part, rows_local)]
    scatter-add x2 -> x0, other arithmetic: 48.1 us -> none  [the longest x1 24 us: on_device(): link_last = jnp.zeros((vector_part, plane_cells), jnp.float32).at[:, lowe...]
    all_to_all x3 -> x4, waiting for transfers between devices: 64.4 us -> 23.4 us  [the longest x2 23.3 us: on_device(): arrived = [lax.all_to_all(p, 'vecs', 0, 0, tiled=True) for p in packed]]
    reshape x2 -> x0, local copies, waits for them, and re-layouts: 39 us -> none  [on_device(): total_coupled = (neighbour_sum + link_sum).reshape(vector_part, rows_local)]
    pallas_call x0 -> x7, Pallas kernels: none -> 34 us  [the longest x1 9.5 us: link_terms(): pl.pallas_call(link_kernel, out_shape=jax.ShapeDtypeStruct((nd * 32, NP,...]
    all_to_all x6 -> x0, local copies, waits for them, and re-layouts: 28.6 us -> none  [the longest x3 15.1 us: on_device(): lax.all_to_all(quarter_vecs, 'vecs', split_axis=0, concat_axis=1, tiled=T...]
    gather x2 -> x0, local copies, waits for them, and re-layouts: 27.4 us -> none  [the longest x1 15 us: on_device(): last_plane[:, lower_cells[0]]]
    convert_element_type x4 -> x0, other arithmetic: 24.8 us -> none  [the longest x1 18.2 us: on_device(): vectors = eigvecs.astype(jnp.float32)]
  transfers between devices with their start and end apart: 7 -> 9, of which waited for: 2 -> 4; matrix products, arithmetic and copies ran while one was open for 28% -> 4% of each run, Pallas kernels for 0% -> 22%
where the time goes in v1:
time: 111 us
  Pallas kernels  34 us (31%)
  starting transfers between devices  26 us (23%)
  waiting for transfers between devices  25.3 us (23%)
  blocking collectives  16.9 us (15%)
  other arithmetic  3.8 us (3%)
  local copies, waits for them, and re-layouts  3.23 us (3%)
  between operations  1.43 us (1%)
    all_to_all x2, waiting for transfers between devices, on_device(): arrived = [lax.all_to_all(p, 'vecs', 0, 0, tiled=True) for p in packed]  23.3 us
    all_to_all x1, blocking collectives, on_device(): total = lax.all_to_all(sums, 'rows', 0, 0, tiled=True).sum(axis=(0, 1))  16.9 us
    ppermute x5, starting transfers between devices, from_behind(): return lax.ppermute(value, axis, pairs)  9.9 us
    pallas_call x1, Pallas kernels, link_terms(): pl.pallas_call(link_kernel, out_shape=jax.ShapeDtypeStruct((nd * 32, NP,...  9.5 us
    pallas_call x2, Pallas kernels, mix(): pl.pallas_call(mix_kernel, out_shape=jax.ShapeDtypeStruct((rows, lanes),...  8.67 us
    all_to_all x2, starting transfers between devices, on_device(): arrived = [lax.all_to_all(p, 'vecs', 0, 0, tiled=True) for p in packed]  8.52 us
    pallas_call x1, Pallas kernels, residual(): pl.pallas_call(kernel, out_shape=(jax.ShapeDtypeStruct((vecs, rows_local)...  8.32 us
    all_to_all x2, starting transfers between devices, on_device(): back = [lax.all_to_all(m, 'vecs', 0, 0, tiled=True) for m in mixed]  7.54 us
  transfers between devices with their start and end apart: 9, of which 4 were waited for; matrix products, arithmetic and copies ran while one was open for 4% of the time, Pallas kernels for 22%

profile of v1, /device:TPU:1, one launch (start us, length us, event | category | flops | bytes accessed | tf_op | source)
XLA Modules:
  0.0 110.7 jit_solution(6551132345530835935)
XLA Ops:
  0.6 1.9 %pack.2 = bf16[4,200,256]{2,1,0:T(8,128)(2,1)} custom-call(bf16[25,65536]{1,0:T(8,128)(2,1)} %basis_ref.3), custom_call_target="tpu_custom_call" | custom-call | bytes 819200 | tf_op jit(solution)/shard_map/pack/pallas_call | solution.py:60
  2.5 4.8 %all-to-all-start = ((bf16[4,200,256]{2,1,0:T(8,128)(2,1)}), bf16[4,200,256]{2,1,0:T(8,128)(2,1)S(1)}, u32[]{:S(2)}, u32[]{:S(2)}) async-start(bf16[4,200,256]{2,1,0:T(8,128)(2,1)} %pack.2), calls=%async_computation | async-start | bytes 819200 | tf_op jit(solution)/shard_map/all_to_all | solution.py:360
  7.3 3.3 %pack.3 = bf16[4,200,1792]{2,1,0:T(8,128)(2,1)} custom-call(bf16[25,65536]{1,0:T(8,128)(2,1)} %basis_ref.3), custom_call_target="tpu_custom_call" | custom-call | bytes 5734400 | tf_op jit(solution)/shard_map/pack/pallas_call | solution.py:60
  10.6 0.0 copy-start.5
  10.7 3.8 %all-to-all-done = bf16[4,200,256]{2,1,0:T(8,128)(2,1)S(1)} async-done(((bf16[4,200,256]{2,1,0:T(8,128)(2,1)}), bf16[4,200,256]{2,1,0:T(8,128)(2,1)S(1)}, u32[]{:S(2)}, u32[]{:S(2)}) %all-to-all-start) | async-done | bytes 409632 | tf_op jit(solution)/shard_map/all_to_all | solution.py:360
  14.4 0.7 copy-done.2
  15.2 3.7 %all-to-all-start.2 = ((bf16[4,200,1792]{2,1,0:T(8,128)(2,1)}), bf16[4,200,1792]{2,1,0:T(8,128)(2,1)S(1)}, u32[]{:S(2)}, u32[]{:S(2)}) async-start(bf16[4,200,1792]{2,1,0:T(8,128)(2,1)} %pack.3), calls=%async_computation.2 | async-start | bytes 5734400 | tf_op jit(solution)/shard_map/all_to_all | solution.py:360
  18.9 3.4 %collective-permute-start.2 = (s32[1,4096]{1,0:T(1,128)S(1)}, s32[1,4096]{1,0:T(1,128)S(1)}, u32[]{:S(2)}, u32[]{:S(2)}) collective-permute-start(s32[1,4096]{1,0:T(1,128)S(1)} %copy-done.5), channel_id=1, source_target_pairs={{0,4},{4,8},{8,12},{12,16},{16,20},{20,24},{24,28},{28,32},{32,36}... | collective-permute-start | bytes 49160 | tf_op jit(solution)/shard_map/ppermute | solution.py:22
  22.2 0.1 collective-permute-start.3
  22.3 1.6 %collective-permute-start.4 = (s32[1]{0:T(128)}, s32[1]{0:T(128)}, u32[]{:S(2)}, u32[]{:S(2)}) collective-permute-start(s32[1]{0:T(128)} %param.19), channel_id=1, source_target_pairs={{0,4},{4,8},{8,12},{12,16},{16,20},{20,24},{24,28},{28,32},{32,36}... | collective-permute-start | bytes 20 | tf_op jit(solution)/shard_map/ppermute | solution.py:22
  24.6 0.7 copy.16.coef_ref
  25.3 0.7 copy.17.refs_3_
  26.0 2.4 %spread.1.l_ref = bf16[320,800]{1,0:T(8,128)(2,1)} custom-call(bf16[100,40]{1,0:T(8,128)(2,1)} %copy.16.coef_ref, s32[1,800]{1,0:T(1,128)} %constant.21.cr_ref, s32[1,800]{1,0:T(1,128)} %constant.22.cs_ref, s32[320,1]{1,0:T(8,128)} %constant.23.rv_ref, s32[320,1]{1,0:T(8,128)} %constant.24.rs_ref), custom_call_target="tpu_custom_call" | custom-call | flops 51200000 | bytes 512000 | tf_op jit(solution)/shard_map/spread/pallas_call | solution.py:118
  28.4 1.3 %pad_add_fusion.2.n_ref = s32[2]{0:T(128)} fusion(s32[1]{0:T(128)S(6)} %copy.18, s32[1]{0:T(128)} %collective-permute-done.4), kind=kLoop, calls=%fused_computation.3 | loop fusion | flops 2 | bytes 16 | tf_op jit(solution)/shard_map/concatenate | solution.py:373
  29.6 2.2 %mix.2 = bf16[320,256]{1,0:T(8,128)(2,1)} custom-call(bf16[320,800]{1,0:T(8,128)(2,1)} %spread.1.l_ref, bf16[800,256]{1,0:T(8,128)(2,1)} %bitcast.16), custom_call_target="tpu_custom_call" | custom-call | flops 131072000 | bytes 573440 | tf_op jit(solution)/shard_map/mix/pallas_call | solution.py:140
  31.8 19.6 %all-to-all-done.2 = bf16[4,200,1792]{2,1,0:T(8,128)(2,1)S(1)} async-done(((bf16[4,200,1792]{2,1,0:T(8,128)(2,1)}), bf16[4,200,1792]{2,1,0:T(8,128)(2,1)S(1)}, u32[]{:S(2)}, u32[]{:S(2)}) %all-to-all-start.2) | async-done | bytes 2867232 | tf_op jit(solution)/shard_map/all_to_all | solution.py:360
  51.4 3.3 %all-to-all-start.1 = ((bf16[4,80,256]{2,1,0:T(8,128)(2,1)}), bf16[4,80,256]{2,1,0:T(8,128)(2,1)S(1)}, u32[]{:S(2)}, u32[]{:S(2)}) async-start(bf16[4,80,256]{2,1,0:T(8,128)(2,1)} %bitcast.17), calls=%async_computation.1 | async-start | bytes 327680 | tf_op jit(solution)/shard_map/all_to_all | solution.py:365
  54.8 0.6 pad_add_fusion.g_ref
  55.4 6.5 %mix.3 = bf16[320,1792]{1,0:T(8,128)(2,1)} custom-call(bf16[320,800]{1,0:T(8,128)(2,1)} %spread.1.l_ref, bf16[800,1792]{1,0:T(8,128)(2,1)} %bitcast.14), custom_call_target="tpu_custom_call" | custom-call | flops 917504000 | bytes 4014080 | tf_op jit(solution)/shard_map/mix/pallas_call | solution.py:140
  61.9 4.2 %all-to-all-start.3 = ((bf16[4,80,1792]{2,1,0:T(8,128)(2,1)}), bf16[4,80,1792]{2,1,0:T(8,128)(2,1)S(1)}, u32[]{:S(2)}, u32[]{:S(2)}) async-start(bf16[4,80,1792]{2,1,0:T(8,128)(2,1)} %bitcast.15), calls=%async_computation.3 | async-start | bytes 2293760 | tf_op jit(solution)/shard_map/all_to_all | solution.py:365
  66.1 3.6 %collective-permute-start.1 = (bf16[1,160,256]{2,1,0:T(8,128)(2,1)S(1)}, bf16[1,160,256]{2,1,0:T(8,128)(2,1)S(1)}, u32[]{:S(2)}, u32[]{:S(2)}) collective-permute-start(bf16[1,160,256]{2,1,0:T(8,128)(2,1)S(1)} %bitcast.22), channel_id=1, source_target_pairs={{0,124},{4,0},{8,4},{12,8},{16,12},{20,16},{24,20},{28,24},{32,28}... | collective-permute-start | bytes 245768 | tf_op jit(solution)/shard_map/ppermute | solution.py:22
  69.7 1.3 %collective-permute-start = (bf16[1,160,256]{2,1,0:T(8,128)(2,1)S(1)}, bf16[1,160,256]{2,1,0:T(8,128)(2,1)S(1)}, u32[]{:S(2)}, u32[]{:S(2)}) collective-permute-start(bf16[1,160,256]{2,1,0:T(8,128)(2,1)S(1)} %bitcast.21), channel_id=1, source_target_pairs={{0,4},{4,8},{8,12},{12,16},{16,20},{20,24},{24,28},{28,32},{32,36}... | collective-permute-start | bytes 245768 | tf_op jit(solution)/shard_map/ppermute | solution.py:22
  71.0 0.6 pad_add_fusion.1.s_ref
  71.6 1.7 %collective-permute-done.1 = bf16[1,160,256]{2,1,0:T(8,128)(2,1)S(1)} collective-permute-done((bf16[1,160,256]{2,1,0:T(8,128)(2,1)S(1)}, bf16[1,160,256]{2,1,0:T(8,128)(2,1)S(1)}, u32[]{:S(2)}, u32[]{:S(2)}) %collective-permute-start.1) | collective-permute-done | bytes 81952 | tf_op jit(solution)/shard_map/ppermute | solution.py:22
  73.3 0.2 collective-permute-done
  73.5 0.7 pad_maximum_fusion.plane_ref
  74.2 9.5 %links.1.refs_2_ = f32[64,16,128]{2,1,0:T(8,128)} custom-call(bf16[2,160,256]{2,1,0:T(8,128)(2,1)} %pad_maximum_fusion.plane_ref, s32[2,1,4096]{2,1,0:T(1,128)} %pad_add_fusion.g_ref, s32[2,1,4096]{2,1,0:T(1,128)} %pad_add_fusion.1.s_ref, s32[2]{0:T(128)} %pad_add_fusion.2.n_ref), custom_call_target="tpu_custom_call" | custom-call | flops 1342177280 | bytes 327680 | tf_op jit(solution)/shard_map/links/pallas_call | solution.py:216
  83.7 1.0 copy-done.1
  84.8 8.3 %residual.1 = (bf16[10,65536]{1,0:T(8,128)(2,1)}, bf16[10,65536]{1,0:T(8,128)(2,1)}, f32[32,1,128]{2,1,0:T(1,128)}) custom-call(bf16[4,80,256]{2,1,0:T(8,128)(2,1)} %copy-done.3, bf16[4,80,1792]{2,1,0:T(8,128)(2,1)} %copy-done.1, f32[64,16,128]{2,1,0:T(8,128)} %links.1.refs_2_, f32[10,1]{1,0:T(8,128)} %copy.17.refs_3_, f32[512,128]{1,0:T(8,128)} %bitcast.18, ...), custom_call_target="tpu_custom_call" | custom-call | flops 41943040 | bytes 8388608 | tf_op jit(solution)/shard_map/residual/pallas_call | solution.py:317
  93.1 16.9 %all_to_all.25 = f32[32,1,128]{2,1,0:T(1,128)S(1)} all-to-all(f32[32,1,128]{2,1,0:T(1,128)} %get-tuple-element.8), channel_id=1, replica_groups=mesh['rows'=32,'vecs'=4] {'rows'}, dimensions={0} | all-to-all | bytes 32768 | tf_op jit(solution)/shard_map/all_to_all | solution.py:380
  110.0 0.1 reduce_sum.9
  110.1 0.6 rsqrt_multiply_fusion
  (19 shorter events, 0.1 us)
Async XLA Ops:
  2.5 11.9 %all-to-all-start = ((bf16[4,200,256]{2,1,0:T(8,128)(2,1)}), bf16[4,200,256]{2,1,0:T(8,128)(2,1)S(1)}, u32[]{:S(2)}, u32[]{:S(2)}) async-start(bf16[4,200,256]{2,1,0:T(8,128)(2,1)} %pack.2), calls=%async_computation | async-start | bytes 819200 | tf_op jit(solution)/shard_map/all_to_all | solution.py:360
  10.6 8.2 %copy-start.5 = (s32[1,4096]{1,0:T(1,128)S(1)}, s32[1,4096]{1,0:T(1,128)}, u32[]{:S(2)}) copy-start(s32[1,4096]{1,0:T(1,128)} %param.20) | copy-start | bytes 49156
  10.6 11.6 %copy-start.4 = (s32[1,4096]{1,0:T(1,128)S(1)}, s32[1,4096]{1,0:T(1,128)}, u32[]{:S(2)}) copy-start(s32[1,4096]{1,0:T(1,128)} %param.21) | copy-start | bytes 49156
  10.7 14.0 %copy-start.6 = (bf16[100,40]{0,1:T(8,128)(2,1)S(1)}, bf16[100,40]{0,1:T(8,128)(2,1)}, u32[]{:S(2)}) copy-start(bf16[100,40]{0,1:T(8,128)(2,1)} %param.14) | copy-start | bytes 24004
  10.7 14.7 %copy-start.7 = (f32[10]{0:T(128)S(1)}, f32[10]{0:T(128)}, u32[]{:S(2)}) copy-start(f32[10]{0:T(128)} %param.15) | copy-start | bytes 124
  14.4 0.8 copy-start.2
  15.2 36.2 %all-to-all-start.2 = ((bf16[4,200,1792]{2,1,0:T(8,128)(2,1)}), bf16[4,200,1792]{2,1,0:T(8,128)(2,1)S(1)}, u32[]{:S(2)}, u32[]{:S(2)}) async-start(bf16[4,200,1792]{2,1,0:T(8,128)(2,1)} %pack.3), calls=%async_computation.2 | async-start | bytes 5734400 | tf_op jit(solution)/shard_map/all_to_all | solution.py:360
  18.9 35.9 %collective-permute-start.2 = (s32[1,4096]{1,0:T(1,128)S(1)}, s32[1,4096]{1,0:T(1,128)S(1)}, u32[]{:S(2)}, u32[]{:S(2)}) collective-permute-start(s32[1,4096]{1,0:T(1,128)S(1)} %copy-done.5), channel_id=1, source_target_pairs={{0,4},{4,8},{8,12},{12,16},{16,20},{20,24},{24,28},{28,32},{32,36}... | collective-permute-start | bytes 49160 | tf_op jit(solution)/shard_map/ppermute | solution.py:22
  22.2 48.7 %collective-permute-start.3 = (s32[1,4096]{1,0:T(1,128)S(1)}, s32[1,4096]{1,0:T(1,128)S(1)}, u32[]{:S(2)}, u32[]{:S(2)}) collective-permute-start(s32[1,4096]{1,0:T(1,128)S(1)} %copy-done.4), channel_id=1, source_target_pairs={{0,4},{4,8},{8,12},{12,16},{16,20},{20,24},{24,28},{28,32},{32,36}... | collective-permute-start | bytes 49160 | tf_op jit(solution)/shard_map/ppermute | solution.py:22
  22.3 6.1 %collective-permute-start.4 = (s32[1]{0:T(128)}, s32[1]{0:T(128)}, u32[]{:S(2)}, u32[]{:S(2)}) collective-permute-start(s32[1]{0:T(128)} %param.19), channel_id=1, source_target_pairs={{0,4},{4,8},{8,12},{12,16},{16,20},{20,24},{24,28},{28,32},{32,36}... | collective-permute-start | bytes 20 | tf_op jit(solution)/shard_map/ppermute | solution.py:22
  51.4 4.0 %copy-start = (bf16[4,200,1792]{2,1,0:T(8,128)(2,1)}, bf16[4,200,1792]{2,1,0:T(8,128)(2,1)S(1)}, u32[]{:S(2)}) copy-start(bf16[4,200,1792]{2,1,0:T(8,128)(2,1)S(1)} %all-to-all-done.2) | copy-start | bytes 8601604
  51.4 10.5 %all-to-all-start.1 = ((bf16[4,80,256]{2,1,0:T(8,128)(2,1)}), bf16[4,80,256]{2,1,0:T(8,128)(2,1)S(1)}, u32[]{:S(2)}, u32[]{:S(2)}) async-start(bf16[4,80,256]{2,1,0:T(8,128)(2,1)} %bitcast.17), calls=%async_computation.1 | async-start | bytes 327680 | tf_op jit(solution)/shard_map/all_to_all | solution.py:365
  61.9 21.8 %copy-start.3 = (bf16[4,80,256]{2,1,0:T(8,128)(2,1)}, bf16[4,80,256]{2,1,0:T(8,128)(2,1)S(1)}, u32[]{:S(2)}) copy-start(bf16[4,80,256]{2,1,0:T(8,128)(2,1)S(1)} %all-to-all-done.1.refs_0_) | copy-start | bytes 491524
  61.9 21.8 %all-to-all-start.3 = ((bf16[4,80,1792]{2,1,0:T(8,128)(2,1)}), bf16[4,80,1792]{2,1,0:T(8,128)(2,1)S(1)}, u32[]{:S(2)}, u32[]{:S(2)}) async-start(bf16[4,80,1792]{2,1,0:T(8,128)(2,1)} %bitcast.15), calls=%async_computation.3 | async-start | bytes 2293760 | tf_op jit(solution)/shard_map/all_to_all | solution.py:365
  66.1 7.2 %collective-permute-start.1 = (bf16[1,160,256]{2,1,0:T(8,128)(2,1)S(1)}, bf16[1,160,256]{2,1,0:T(8,128)(2,1)S(1)}, u32[]{:S(2)}, u32[]{:S(2)}) collective-permute-start(bf16[1,160,256]{2,1,0:T(8,128)(2,1)S(1)} %bitcast.22), channel_id=1, source_target_pairs={{0,124},{4,0},{8,4},{12,8},{16,12},{20,16},{24,20},{28,24},{32,28}... | collective-permute-start | bytes 245768 | tf_op jit(solution)/shard_map/ppermute | solution.py:22
  69.7 3.9 %collective-permute-start = (bf16[1,160,256]{2,1,0:T(8,128)(2,1)S(1)}, bf16[1,160,256]{2,1,0:T(8,128)(2,1)S(1)}, u32[]{:S(2)}, u32[]{:S(2)}) collective-permute-start(bf16[1,160,256]{2,1,0:T(8,128)(2,1)S(1)} %bitcast.21), channel_id=1, source_target_pairs={{0,4},{4,8},{8,12},{12,16},{16,20},{20,24},{24,28},{28,32},{32,36}... | collective-permute-start | bytes 245768 | tf_op jit(solution)/shard_map/ppermute | solution.py:22
  83.7 1.0 copy-start.1

commit v2 on v0

v2 whole, which is shorter than its diff:
```python
import functools

import jax
import jax.numpy as jnp
from jax import lax
from jax.experimental import pallas as pl
from jax.experimental.pallas import tpu as pltpu
from jax.sharding import PartitionSpec as P


WID = 64
LANES = 128
SEGS = 8
NP = 16
BF = jnp.bfloat16
F32 = jnp.float32


def from_behind(value, axis, steps):
    count = lax.axis_size(axis)
    pairs = [(source, (source + steps) % count) for source in range(count)]
    return lax.ppermute(value, axis, pairs)


ANY = pl.BlockSpec(memory_space=pl.ANY)
VMEM = pl.BlockSpec(memory_space=pltpu.VMEM)
SMEM = pl.BlockSpec(memory_space=pltpu.SMEM)


def params(mib):
    return pltpu.CompilerParams(vmem_limit_bytes=mib * 1024 * 1024)


def cost(flops, nbytes):
    return pl.CostEstimate(flops=int(flops), bytes_accessed=int(nbytes), transcendentals=0)


class Chunk:
    def __init__(self, first, count, parts, planes):
        self.first = first or 0
        self.width = count * WID * WID // parts
        self.seg = self.width // SEGS
        self.jump = (planes - count) * WID * WID if first is None else 0
        self.parts = parts

    def start(self, v):
        base = self.first * WID * WID + v * self.width
        return base + jnp.where(2 * v >= self.parts, self.jump, 0) if self.jump else base


class Packing:
    def __init__(self, chunk, parts, me, basis_ref, outs, buf, sem):
        self.chunk, self.outs, self.buf, self.reads = chunk, outs, buf, []
        for k in range(parts):
            st = pl.multiple_of(chunk.start(lax.rem(me + k, parts)), LANES)
            read = pltpu.make_async_copy(
                basis_ref.at[:, pl.ds(st, chunk.width)], buf.at[k], sem.at[k]
            )
            read.start()
            self.reads.append(read)

    def finish(self):
        ranks, seg = self.buf.shape[1], self.chunk.seg
        full = ranks // 8 * 8
        for read, out, k in zip(self.reads, self.outs, range(len(self.outs))):
            read.wait()
            tail = []
            for c in range(SEGS):
                cut = slice(c * seg, (c + 1) * seg)
                out[c * full : (c + 1) * full, :] = self.buf[k, 0:full, cut]
                tail.append(self.buf[k, full:ranks, cut])
            out[SEGS * full : SEGS * ranks, :] = jnp.concatenate(tail, axis=0)


def packed_shape(chunk, ranks):
    return jax.ShapeDtypeStruct((SEGS * ranks, chunk.seg), BF)


def pack_scratch(chunk, ranks, parts):
    return [pltpu.VMEM((parts, ranks, chunk.width), BF), pltpu.SemaphoreType.DMA((parts,))]


def pack_kernel(chunk, parts, me_ref, basis_ref, *rest):
    Packing(chunk, parts, me_ref[0], basis_ref, rest[:parts], *rest[parts:]).finish()


def pack(me, basis, chunk, parts):
    ranks = basis.shape[0]
    return list(
        pl.pallas_call(
            functools.partial(pack_kernel, chunk, parts),
            out_shape=[packed_shape(chunk, ranks)] * parts,
            in_specs=[SMEM, ANY],
            out_specs=[VMEM] * parts,
            scratch_shapes=pack_scratch(chunk, ranks, parts),
            compiler_params=params(60),
            cost_estimate=cost(1, 4 * parts * ranks * chunk.width),
            name="pack",
        )(me, basis)
    )


def orders(shape, axis, main, rest):
    i = lax.broadcasted_iota(jnp.int32, shape, axis)
    body, tail = i < main * SEGS, i - main * SEGS
    entry = jnp.where(body, lax.rem(i, main), main + lax.rem(tail, rest))
    return entry, jnp.where(body, lax.div(i, main), lax.div(tail, rest))


def spread(parts, me, coef_ref, out_ref):
    wide, total = coef_ref.shape
    ranks, vecs = total // parts, wide // parts
    rows, cols = out_ref.shape[1] // parts, out_ref.shape[2]
    full, vfull = ranks // 8 * 8, vecs // 8 * 8
    col_rank, col_seg = orders((1, cols), 1, full, ranks - full)
    row_vec, row_seg = orders((rows, 1), 0, vfull, vecs - vfull)
    coef = coef_ref[...]
    same = row_seg == col_seg
    for k in range(parts):
        source = lax.rem(me - k + parts, parts) * ranks
        pick = lax.broadcasted_iota(jnp.int32, (total, cols), 0) == col_rank + source
        by_col = jnp.dot(
            coef, jnp.where(pick, 1.0, 0.0).astype(BF), preferred_element_type=F32
        ).astype(BF)
        for o in range(parts):
            owner = lax.rem(me + o, parts) * vecs
            pick = lax.broadcasted_iota(jnp.int32, (rows, wide), 1) == row_vec + owner
            block = jnp.dot(
                jnp.where(pick, 1.0, 0.0).astype(BF), by_col, preferred_element_type=F32
            )
            out_ref[k, o * rows : (o + 1) * rows, :] = jnp.where(same, block, 0.0).astype(BF)


def spread_coefficients(me, coefficients, parts, ranks, vecs):
    nc, nr = SEGS * ranks, SEGS * vecs
    return pl.pallas_call(
        lambda me_ref, coef_ref, out_ref: spread(parts, me_ref[0], coef_ref, out_ref),
        out_shape=jax.ShapeDtypeStruct((parts, parts * nr, nc), BF),
        in_specs=[SMEM, VMEM],
        out_specs=VMEM,
        compiler_params=params(8),
        cost_estimate=cost(20 * parts * parts * nr * nc, 2 * parts * parts * nr * nc),
        name="spread",
    )(me, coefficients.T)


def mix_kernel(parts, lane, seg, l_ref, *rest):
    ys, outs = rest[:parts], rest[parts:]
    rows = outs[0].shape[0]
    step = 256

    def body(at, step):
        total = None
        for k in range(parts):
            part = jnp.dot(
                l_ref[k], ys[k][:, pl.ds(lane + at, step)], preferred_element_type=F32
            )
            total = part if total is None else total + part
        for o in range(parts):
            outs[o][:, pl.ds(at, step)] = total[o * rows : (o + 1) * rows].astype(BF)

    @pl.loop(0, seg // step)
    def _(i):
        body(pl.multiple_of(i * step, step), step)

    if seg % step:
        body(seg // step * step, seg % step)


def mix(matrix, packed, lane, seg, vecs):
    parts, rows, depth = matrix.shape
    return pl.pallas_call(
        functools.partial(mix_kernel, parts, lane, seg),
        out_shape=[jax.ShapeDtypeStruct((SEGS * vecs, seg), BF)] * parts,
        in_specs=[VMEM] * (1 + parts),
        out_specs=[VMEM] * parts,
        compiler_params=params(12),
        cost_estimate=cost(2 * rows * parts * depth * seg, 2 * (rows + parts * depth) * seg),
        name="mix",
    )(matrix, *packed)


def one_hot_kernel(low, down_ref, lower_ref, upper_ref, count_ref, g_ref, s_ref, seg_ref):
    slots = lower_ref.shape[1]
    shift = low.bit_length() - 1
    step = 256
    lane = lax.broadcasted_iota(jnp.int32, (low, 1), 0)
    across = lax.broadcasted_iota(jnp.int32, (1, low), 1)
    ways = (
        (down_ref, 0, down_ref, slots, down_ref[:, 2 * slots : 2 * slots + 1]),
        (upper_ref, 0, lower_ref, 0, count_ref[...]),
    )

    @pl.loop(0, slots // step)
    def _(i):
        at = pl.ds(pl.multiple_of(i * step, step), step)
        slot = lax.broadcasted_iota(jnp.int32, (1, step), 1) + i * step
        for d, (from_ref, f0, to_ref, t0, count) in enumerate(ways):
            g = from_ref[:, pl.ds(pl.multiple_of(f0 + i * step, step), step)]
            s = to_ref[:, pl.ds(pl.multiple_of(t0 + i * step, step), step)]
            g_low, s_low = jnp.bitwise_and(g, low - 1), jnp.bitwise_and(s, low - 1)
            g_ref[d, :, at] = jnp.where(lane == g_low, 1.0, 0.0).astype(BF)
            for j in range(0, step, LANES):
                down_sub = jnp.broadcast_to(s_low[:, j : j + LANES], (LANES, LANES)).T
                down_sub = jnp.concatenate([down_sub] * (low // LANES), axis=1)
                rows = pl.ds(pl.multiple_of(i * step + j, LANES), LANES)
                s_ref[d, rows, :] = jnp.where(down_sub == across, 1.0, 0.0).astype(BF)
            seg_ref[2 * d : 2 * d + 1, at] = lax.shift_right_logical(g, shift)
            seg_ref[2 * d + 1 : 2 * d + 2, at] = jnp.where(
                slot < count, lax.shift_right_logical(s, shift), -1
            )


def one_hots(low, down, lower, upper, count):
    slots = lower.shape[1]
    hot = jax.ShapeDtypeStruct((2, low, slots), BF)
    hot_down = jax.ShapeDtypeStruct((2, slots, low), BF)
    return pl.pallas_call(
        functools.partial(one_hot_kernel, low),
        out_shape=(hot, hot_down, jax.ShapeDtypeStruct((4, slots), jnp.int32)),
        in_specs=[VMEM] * 4,
        out_specs=[VMEM] * 3,
        compiler_params=params(20),
        cost_estimate=cost(40 * low * slots, 8 * low * slots),
        name="one_hots",
    )(down, lower, upper, count)


def link_kernel(below_ref, above_ref, g_ref, s_ref, seg_ref, out_ref, put):
    rows, low = below_ref.shape
    slots = g_ref.shape[2]
    vfull = 8
    vrest = rows // SEGS - vfull
    step = 512
    tail_rows = SEGS * vrest
    tail_seg = lax.broadcasted_iota(jnp.int32, (tail_rows, 1), 0) // vrest
    for i in range(slots // step):
        at = slice(i * step, (i + 1) * step)
        for d, plane_ref in enumerate((below_ref, above_ref)):
            got = jnp.dot(plane_ref[...], g_ref[d, :, at], preferred_element_type=F32)
            gh, sh = seg_ref[2 * d : 2 * d + 1, at], seg_ref[2 * d + 1 : 2 * d + 2, at]
            main = got[0:vfull]
            for c in range(1, SEGS):
                main = jnp.where(gh == c, got[c * vfull : (c + 1) * vfull], main)
            tail = jnp.where(gh == tail_seg, got[SEGS * vfull : rows], 0.0)
            shift = vrest
            while shift < tail_rows:
                tail = tail + pltpu.roll(tail, shift, 0)
                shift *= 2
            pieces = [jnp.where(sh == c, main, 0.0) for c in range(SEGS)]
            pieces.append(jnp.where(sh == tail_seg, tail, 0.0))
            put[d, :, at] = jnp.concatenate(pieces, axis=0).astype(BF)

    for d in range(2):
        total = jnp.dot(put[d], s_ref[d], preferred_element_type=F32)
        for c in range(SEGS):
            for k in range(low // LANES):
                t = d * 32 + c * (low // LANES) + k
                at = slice(k * LANES, (k + 1) * LANES)
                out_ref[t, 0:8, :] = total[c * 8 : (c + 1) * 8, at]
                first = SEGS * 8 + c * vrest
                out_ref[t, 8 : 8 + vrest, :] = total[first : first + vrest, at]


def link_terms(below, above, hots):
    rows, low = below.shape
    slots = hots[0].shape[2]
    return pl.pallas_call(
        link_kernel,
        out_shape=jax.ShapeDtypeStruct((64, NP, LANES), F32),
        in_specs=[VMEM] * 5,
        out_specs=VMEM,
        scratch_shapes=[pltpu.VMEM((2, rows, slots), BF)],
        compiler_params=params(10),
        cost_estimate=cost(8 * rows * low * slots, 8 * rows * low),
        name="links",
    )(below, above, *hots)


def ends_kernel(parts, me_ref, *rest):
    z_refs, (low_ref, high_ref) = rest[:parts], rest[parts:]
    for k in range(parts):
        v = lax.rem(me_ref[0] - k + parts, parts)

        @pl.when(v == 0)
        def _():
            low_ref[...] = z_refs[k][...]

        @pl.when(v == parts - 1)
        def _():
            high_ref[...] = z_refs[k][...]


def end_planes(me, zs):
    parts = len(zs)
    shape = jax.ShapeDtypeStruct(zs[0].shape, BF)
    return pl.pallas_call(
        functools.partial(ends_kernel, parts),
        out_shape=(shape, shape),
        in_specs=[SMEM] + [VMEM] * parts,
        out_specs=(VMEM, VMEM),
        compiler_params=params(8),
        cost_estimate=cost(1, 8 * zs[0].size * parts),
        name="ends",
    )(me, *zs)


def unpack(cells, tile0, chunk, me, parts, z_refs, vrest):
    for k in range(parts):
        first = chunk.start(lax.rem(me - k + parts, parts)) // LANES - tile0
        per = chunk.seg // LANES
        for c in range(SEGS):
            for i in range(per):
                at = slice(i * LANES, (i + 1) * LANES)
                t = first + c * per + i
                low = SEGS * 8 + c * vrest
                cells[t, 0:8, :] = z_refs[k][c * 8 : (c + 1) * 8, at].astype(F32)
                cells[t, 8 : 8 + vrest, :] = z_refs[k][low : low + vrest, at].astype(F32)


class Output:
    def __init__(self, refs, bufs, sem, low):
        self.refs, self.bufs, self.sem, self.low = refs, bufs, sem, low
        self.copies = []

    def send(self, first, last):
        lanes = (last - first) * WID * WID
        to = pl.ds(first * WID * WID, lanes)
        at = pl.ds((first - self.low) * WID * WID, lanes)
        for i in range(2):
            copy = pltpu.make_async_copy(
                self.bufs[i].at[:, at], self.refs[i].at[:, to], self.sem.at[len(self.copies)]
            )
            copy.start()
            self.copies.append(copy)

    def wait(self):
        for copy in self.copies:
            copy.wait()


def cuts(low, high, step=3):
    marks = list(range(low, high, step))
    return list(zip(marks, marks[1:] + [high]))


class Terms:
    def __init__(self, eig_ref, stiff_ref, damp_ref, mass_ref):
        vecs = eig_ref.shape[1]
        sub = lax.broadcasted_iota(jnp.int32, (NP, vecs), 0)
        own = sub == lax.broadcasted_iota(jnp.int32, (NP, vecs), 1)
        eig = jnp.sum(jnp.where(own, eig_ref[...], 0.0), axis=1, keepdims=True)
        self.eig = jnp.broadcast_to(eig, (NP, LANES))
        self.eig_sq = self.eig * self.eig
        self.coupling = self.eig_sq * 0.1 + self.eig * 0.3 + 1.0
        self.diagonals = (stiff_ref, damp_ref, mass_ref)
        lane = lax.broadcasted_iota(jnp.int32, (1, LANES), 1)
        self.low_half = lane < WID
        column = jnp.bitwise_and(lane, WID - 1)
        self.not_first, self.not_last = column > 0, column < WID - 1


def one_plane(terms, cells, z, z0, carry, link, outs):
    tiles = WID * WID // LANES
    vsum, rsum = carry
    base = (z - z0) * tiles
    stiff_ref, damp_ref, mass_ref = terms.diagonals
    for i in range(tiles):
        x = cells[base + i]
        ahead = cells[base + i + 1] if i + 1 < tiles else None
        behind = cells[base + i - 1] if i > 0 else None
        if behind is None:
            across = jnp.where(terms.low_half, ahead, 0.0)
        elif ahead is None:
            across = jnp.where(terms.low_half, 0.0, behind)
        else:
            across = jnp.where(terms.low_half, ahead, behind)
        total = pltpu.roll(x + across, WID, 1)
        total = total + jnp.where(terms.not_first, pltpu.roll(x, 1, 1), 0.0)
        total = total + jnp.where(terms.not_last, pltpu.roll(x, LANES - 1, 1), 0.0)
        if link is None:
            total = total + (cells[base + i - tiles] + cells[base + i + tiles])
        else:
            link_ref, offset, side = link
            total = total + (link_ref[offset + i] + cells[base + i + side * tiles])
        row = pl.ds(z * tiles + i, 1)
        diagonal = (
            terms.eig_sq * mass_ref[row, :] + terms.eig * damp_ref[row, :] + stiff_ref[row, :]
        )
        res = diagonal * x - terms.coupling * total
        if outs is not None:
            vec_ref, res_ref, o0 = outs
            vecs = vec_ref.shape[0]
            at = pl.ds(pl.multiple_of(z * WID * WID - o0 + i * LANES, LANES), LANES)
            vec_ref[:, at] = x[:vecs].astype(BF)
            res_ref[:, at] = res[:vecs].astype(BF)
        vsum = vsum + x * x
        rsum = rsum + res * res
    return vsum, rsum


def residual_kernel(chunks, parts, planes, me_ref, *rest):
    nz = parts * len(chunks)
    z_refs, rest = rest[:nz], rest[nz:]
    link_ref, eig_ref, stiff_ref, damp_ref, mass_ref = rest[:5]
    vec_ref, res_ref, out_ref, cells, vec_buf, res_buf, sem = rest[5:]
    vecs = vec_ref.shape[0]
    tiles = WID * WID // LANES
    for i, chunk in enumerate(chunks):
        unpack(cells, 0, chunk, me_ref[0], parts, z_refs[i * parts : (i + 1) * parts], vecs - 8)
    terms = Terms(eig_ref, stiff_ref, damp_ref, mass_ref)
    outs = (vec_buf, res_buf, 0)
    out = Output((vec_ref, res_ref), (vec_buf, res_buf), sem, 0)
    zero = jnp.zeros((NP, LANES), F32)
    carry = one_plane(terms, cells, 0, 0, (zero, zero), (link_ref, 0, 1), outs)
    carry = one_plane(terms, cells, planes - 1, 0, carry, (link_ref, tiles, -1), outs)
    ready = [(0, 1), (planes - 1, planes)]
    for first, end in cuts(1, planes - 1):
        carry = lax.fori_loop(
            first, end, lambda z, c: one_plane(terms, cells, z, 0, c, None, outs), carry
        )
        for cut in ready:
            out.send(*cut)
        ready = [(first, end)]
    vsum, rsum = carry
    vrow = jnp.broadcast_to(jnp.sum(vsum, axis=1, keepdims=True), (NP, LANES))
    rrow = jnp.broadcast_to(jnp.sum(rsum, axis=1, keepdims=True), (NP, LANES))
    sub = lax.broadcasted_iota(jnp.int32, (NP, LANES), 0)
    wide = lax.broadcasted_iota(jnp.int32, (NP, LANES), 1)
    both = jnp.where((sub == wide) & (sub < vecs), vrow, 0.0)
    both = both + jnp.where((sub + NP == wide) & (sub < vecs), rrow, 0.0)
    line = jnp.sum(both, axis=0, keepdims=True)
    out_ref[...] = jnp.broadcast_to(line[None], out_ref.shape)
    for cut in ready:
        out.send(*cut)
    out.wait()


def residual(me, chunks, zs, link, eig, diagonals, vecs, rows_local, parts, copies):
    planes = rows_local // (WID * WID)
    tiles = WID * WID // LANES
    whole = jax.ShapeDtypeStruct((vecs, rows_local), BF)
    return pl.pallas_call(
        functools.partial(residual_kernel, chunks, parts, planes),
        out_shape=(whole, whole, jax.ShapeDtypeStruct((copies, 1, LANES), F32)),
        in_specs=[SMEM] + [VMEM] * (len(zs) + 5),
        out_specs=(ANY, ANY, VMEM),
        scratch_shapes=[
            pltpu.VMEM((planes * tiles, NP, LANES), F32),
            pltpu.VMEM((vecs, rows_local), BF),
            pltpu.VMEM((vecs, rows_local), BF),
            pltpu.SemaphoreType.DMA((32,)),
        ],
        compiler_params=params(24),
        cost_estimate=cost(4000 * NP * rows_local, 8 * NP * rows_local),
        name="residual",
    )(me, *zs, link, eig, *diagonals)


def kept(value):
    def kernel(from_ref, to_ref):
        to_ref[...] = from_ref[...]

    return pl.pallas_call(
        kernel,
        out_shape=jax.ShapeDtypeStruct(value.shape, value.dtype),
        in_specs=[VMEM],
        out_specs=VMEM,
        compiler_params=params(4),
        cost_estimate=cost(1, 4 * value.size),
        name="kept",
    )(value)


def exchanged(arrays, axis):
    return [arrays[0]] + [from_behind(arrays[k], axis, k) for k in range(1, len(arrays))]


def on_device(
    basis,
    coefficients,
    eigen_values,
    stiffness,
    damping,
    mass,
    link_count,
    lower_cells,
    upper_cells,
):
    parts = lax.axis_size("vecs")
    subdomains = lax.axis_size("rows")
    vecs = eigen_values.shape[0]
    ranks, rows_local = basis.shape
    planes = rows_local // (WID * WID)
    me = lax.axis_index("vecs").astype(jnp.int32)[None]
    ends = Chunk(None, 4, parts, planes)
    inner = Chunk(2, planes - 4, parts, planes)
    wide_count = jnp.broadcast_to(link_count[:, None], (1, LANES))
    lists = jnp.concatenate([lower_cells, upper_cells, wide_count], axis=1)
    ends_out = pack(me, basis, ends, parts)
    ends_out = exchanged(ends_out, "vecs")
    inner_out = pack(me, basis, inner, parts)
    inner_out = exchanged(inner_out, "vecs")
    down = from_behind(lists, "rows", 1)
    matrix = spread_coefficients(me, coefficients, parts, ranks, vecs)
    hots = one_hots(ends.seg, down, lower_cells, upper_cells, wide_count[:, :1])
    inner_out[0] = kept(inner_out[0])
    z_ends = mix(matrix, ends_out, 0, ends.seg, vecs)
    z_ends = exchanged(z_ends, "vecs")
    z_inner = mix(matrix, inner_out, 0, inner.seg, vecs)
    z_inner = exchanged(z_inner, "vecs")
    plane_low, plane_high = end_planes(me, z_ends)
    from_below = from_behind(plane_high, "rows", 1)
    from_above = from_behind(plane_low, "rows", -1)
    link = link_terms(from_below, from_above, hots)
    diagonals = [a.reshape(rows_local // LANES, LANES) for a in (stiffness, damping, mass)]
    eigvecs, residuals, sums = residual(
        me, [ends, inner], z_ends + z_inner, link, eigen_values[None, :], diagonals, vecs,
        rows_local, parts, subdomains,
    )
    total = lax.all_to_all(sums, "rows", 0, 0, tiled=True).sum(axis=(0, 1))
    vector_sq, residual_sq = total[:vecs], total[NP : NP + vecs]
    relative_norms = jnp.sqrt(residual_sq) / jnp.sqrt(vector_sq + 1.0)
    return (eigvecs, residuals, relative_norms)


def solution(mesh):
    placed = (
        P("vecs", "rows"),
        P(),
        P("vecs"),
        P("rows"),
        P("rows"),
        P("rows"),
        P("rows"),
        P("rows", None),
        P("rows", None),
    )
    return jax.shard_map(
        on_device,
        mesh=mesh,
        in_specs=placed,
        out_specs=(P("vecs", "rows"), P("vecs", "rows"), P("vecs")),
        check_vma=False,
    )
```

time: 389 us -> 95 us (0.24)
  other arithmetic: 168 us -> 0.68 us
  local copies, waits for them, and re-layouts: 126 us -> 0.99 us
  waiting for transfers between devices: 64.5 us -> 29.4 us
  Pallas kernels: 0 us -> 23.8 us
  blocking collectives: 0 us -> 11.7 us
    add x2 -> x0, other arithmetic: 83.1 us -> none  [the longest x1 82.5 us: on_device(): total_coupled = (neighbour_sum + link_sum).reshape(vector_part, rows_local)]
    all_to_all x3 -> x0, waiting for transfers between devices: 64.4 us -> none  [the longest x1 39.8 us: on_device(): lax.all_to_all(basis, 'vecs', split_axis=1, concat_axis=0, tiled=True)]
    scatter-add x2 -> x0, other arithmetic: 48.1 us -> none  [the longest x1 24 us: on_device(): link_last = jnp.zeros((vector_part, plane_cells), jnp.float32).at[:, lowe...]
    reshape x2 -> x0, local copies, waits for them, and re-layouts: 39 us -> none  [on_device(): total_coupled = (neighbour_sum + link_sum).reshape(vector_part, rows_local)]
    ppermute x4 -> x15, waiting for transfers between devices: 0.01 us -> 29.4 us  [from_behind(): return lax.ppermute(value, axis, pairs)]
    all_to_all x6 -> x0, local copies, waits for them, and re-layouts: 28.6 us -> none  [the longest x3 15.1 us: on_device(): lax.all_to_all(quarter_vecs, 'vecs', split_axis=0, concat_axis=1, tiled=T...]
    gather x2 -> x0, local copies, waits for them, and re-layouts: 27.4 us -> none  [the longest x1 15 us: on_device(): last_plane[:, lower_cells[0]]]
    convert_element_type x4 -> x0, other arithmetic: 24.8 us -> none  [the longest x1 18.2 us: on_device(): vectors = eigvecs.astype(jnp.float32)]
  transfers between devices with their start and end apart: 7 -> 15, of which waited for: 2 -> 3; matrix products, arithmetic and copies ran while one was open for 28% -> 0% of each run, Pallas kernels for 0% -> 15%
where the time goes in v2:
time: 95 us; the launch traced here: 94.8 us
  waiting for transfers between devices  29.4 us (31%)
  starting transfers between devices  26.8 us (28%)
  Pallas kernels  23.8 us (25%)
  blocking collectives  11.7 us (12%)
  between operations  1.54 us (2%)
  local copies, waits for them, and re-layouts  0.99 us (1%)
    ppermute x15, waiting for transfers between devices, from_behind(): return lax.ppermute(value, axis, pairs)  29.4 us
    ppermute x15, starting transfers between devices, from_behind(): return lax.ppermute(value, axis, pairs)  26.8 us
    all_to_all x1, blocking collectives, on_device(): total = lax.all_to_all(sums, 'rows', 0, 0, tiled=True).sum(axis=(0, 1))  11.7 us
    pallas_call x1, Pallas kernels, residual(): pl.pallas_call(functools.partial(residual_kernel, chunks, parts, planes),...  6.06 us
    pallas_call x1, Pallas kernels, one_hots(): pl.pallas_call(functools.partial(one_hot_kernel, low), out_shape=(hot, ho...  5.63 us
    pallas_call x2, Pallas kernels, pack(): pl.pallas_call(functools.partial(pack_kernel, chunk, parts), out_shape=[p...  5.44 us
    pallas_call x1, Pallas kernels, link_terms(): pl.pallas_call(link_kernel, out_shape=jax.ShapeDtypeStruct((64, NP, LANES...  3.06 us
    pallas_call x2, Pallas kernels, mix(): pl.pallas_call(functools.partial(mix_kernel, parts, lane, seg), out_shape...  2.65 us
  transfers between devices with their start and end apart: 15, of which 3 were waited for; matrix products, arithmetic and copies ran while one was open for 0% of the time, Pallas kernels for 15%

profile of v2, /device:TPU:1, one launch (start us, length us, event | category | flops | bytes accessed | tf_op | source)
XLA Modules:
  0.0 94.8 jit_solution(13781002369470980733)
XLA Ops:
  0.6 3.3 %pack.3 = (bf16[200,1536]{1,0:T(8,128)(2,1)}, bf16[200,1536]{1,0:T(8,128)(2,1)}, bf16[200,1536]{1,0:T(8,128)(2,1)}, bf16[200,1536]{1,0:T(8,128)(2,1)}) custom-call(s32[1]{0:T(128)} %bitcast.me_ref, bf16[25,65536]{1,0:T(8,128)(2,1)} %basis_ref.3), custom_call_target="tpu_custom_call" | custom-call | flops 1 | bytes 4915200 | tf_op jit(solution)/shard_map/pack/pallas_call | solution.py:90
  4.0 2.1 %collective-permute-start.6 = (bf16[200,1536]{1,0:T(8,128)(2,1)}, bf16[200,1536]{1,0:T(8,128)(2,1)S(1)}, u32[]{:S(2)}, u32[]{:S(2)}) collective-permute-start(bf16[200,1536]{1,0:T(8,128)(2,1)} %get-tuple-element.36), channel_id=1, source_target_pairs={{0,1},{1,2},{2,3},{3,0},{4,5},{5,6},{6,7},{7,4},{8,9},{9,10},{10,1... | collective-permute-start | bytes 1843208 | tf_op jit(solution)/shard_map/ppermute | solution.py:22
  6.1 2.5 %collective-permute-start.7 = (bf16[200,1536]{1,0:T(8,128)(2,1)}, bf16[200,1536]{1,0:T(8,128)(2,1)S(1)}, u32[]{:S(2)}, u32[]{:S(2)}) collective-permute-start(bf16[200,1536]{1,0:T(8,128)(2,1)} %get-tuple-element.37), channel_id=1, source_target_pairs={{0,2},{1,3},{2,0},{3,1},{4,6},{5,7},{6,4},{7,5},{8,10},{9,11},{10,... | collective-permute-start | bytes 1843208 | tf_op jit(solution)/shard_map/ppermute | solution.py:22
  8.5 1.2 %collective-permute-start.8 = (bf16[200,1536]{1,0:T(8,128)(2,1)}, bf16[200,1536]{1,0:T(8,128)(2,1)S(1)}, u32[]{:S(2)}, u32[]{:S(2)}) collective-permute-start(bf16[200,1536]{1,0:T(8,128)(2,1)} %get-tuple-element.38), channel_id=1, source_target_pairs={{0,3},{1,0},{2,1},{3,2},{4,7},{5,4},{6,5},{7,6},{8,11},{9,8},{10,9... | collective-permute-start | bytes 1843208 | tf_op jit(solution)/shard_map/ppermute | solution.py:22
  9.7 2.1 %pack.2 = (bf16[200,512]{1,0:T(8,128)(2,1)}, bf16[200,512]{1,0:T(8,128)(2,1)}, bf16[200,512]{1,0:T(8,128)(2,1)}, bf16[200,512]{1,0:T(8,128)(2,1)}) custom-call(s32[1]{0:T(128)} %bitcast.me_ref, bf16[25,65536]{1,0:T(8,128)(2,1)} %basis_ref.3), custom_call_target="tpu_custom_call" | custom-call | flops 1 | bytes 1638400 | tf_op jit(solution)/shard_map/pack/pallas_call | solution.py:90
  11.8 0.0 copy-start.2
  11.8 0.4 collective-permute-start
  12.2 0.9 collective-permute-start.1
  13.1 25.2 %collective-permute-done.rest_1_ = bf16[200,512]{1,0:T(8,128)(2,1)S(1)} collective-permute-done((bf16[200,512]{1,0:T(8,128)(2,1)}, bf16[200,512]{1,0:T(8,128)(2,1)S(1)}, u32[]{:S(2)}, u32[]{:S(2)}) %collective-permute-start) | collective-permute-done | bytes 204832 | tf_op jit(solution)/shard_map/ppermute | solution.py:22
  38.3 1.6 %collective-permute-start.2 = (bf16[200,512]{1,0:T(8,128)(2,1)}, bf16[200,512]{1,0:T(8,128)(2,1)S(1)}, u32[]{:S(2)}, u32[]{:S(2)}) collective-permute-start(bf16[200,512]{1,0:T(8,128)(2,1)} %get-tuple-element.30), channel_id=1, source_target_pairs={{0,3},{1,0},{2,1},{3,2},{4,7},{5,4},{6,5},{7,6},{8,11},{9,8},{10,9... | collective-permute-start | bytes 614408 | tf_op jit(solution)/shard_map/ppermute | solution.py:22
  39.9 0.9 spread.1.l_ref
  40.8 3.2 %collective-permute-done.1.rest_2_ = bf16[200,512]{1,0:T(8,128)(2,1)S(1)} collective-permute-done((bf16[200,512]{1,0:T(8,128)(2,1)}, bf16[200,512]{1,0:T(8,128)(2,1)S(1)}, u32[]{:S(2)}, u32[]{:S(2)}) %collective-permute-start.1) | collective-permute-done | bytes 204832 | tf_op jit(solution)/shard_map/ppermute | solution.py:22
  44.0 0.9 copy-done.1
  45.0 0.7 mix.2
  45.6 0.7 collective-permute-start.3
  47.1 2.5 %collective-permute-start.4 = (bf16[80,512]{1,0:T(8,128)(2,1)S(1)}, bf16[80,512]{1,0:T(8,128)(2,1)S(1)}, u32[]{:S(2)}, u32[]{:S(2)}) collective-permute-start(bf16[80,512]{1,0:T(8,128)(2,1)S(1)} %get-tuple-element.33), channel_id=1, source_target_pairs={{0,2},{1,3},{2,0},{3,1},{4,6},{5,7},{6,4},{7,5},{8,10},{9,11},{10,... | collective-permute-start | bytes 245768 | tf_op jit(solution)/shard_map/ppermute | solution.py:22
  49.6 0.2 collective-permute-start.5
  49.8 2.0 %mix.3 = (bf16[80,1536]{1,0:T(8,128)(2,1)S(1)}, bf16[80,1536]{1,0:T(8,128)(2,1)S(1)}, bf16[80,1536]{1,0:T(8,128)(2,1)S(1)}, bf16[80,1536]{1,0:T(8,128)(2,1)S(1)}) custom-call(bf16[4,320,200]{2,1,0:T(8,128)(2,1)S(1)} %spread.1.l_ref, bf16[200,1536]{1,0:T(8,128)(2,1)S(1)} %kept.1.rest_0_, bf16[200,1536]{1,0:T(8,128)(2,1)S(1)} %collective-permute-done.6.rest_1_, ...), custom_call_target="tpu_custom_call" | custom-call | flops 786432000 | bytes 3440640 | tf_op jit(solution)/shard_map/mix/pallas_call | solution.py:172
  51.8 1.8 %collective-permute-start.10 = (bf16[80,1536]{1,0:T(8,128)(2,1)S(1)}, bf16[80,1536]{1,0:T(8,128)(2,1)S(1)}, u32[]{:S(2)}, u32[]{:S(2)}) collective-permute-start(bf16[80,1536]{1,0:T(8,128)(2,1)S(1)} %get-tuple-element.41), channel_id=1, source_target_pairs={{0,2},{1,3},{2,0},{3,1},{4,6},{5,7},{6,4},{7,5},{8,10},{9,11},{10,... | collective-permute-start | bytes 737288 | tf_op jit(solution)/shard_map/ppermute | solution.py:22
  53.6 1.9 %collective-permute-start.11 = (bf16[80,1536]{1,0:T(8,128)(2,1)S(1)}, bf16[80,1536]{1,0:T(8,128)(2,1)S(1)}, u32[]{:S(2)}, u32[]{:S(2)}) collective-permute-start(bf16[80,1536]{1,0:T(8,128)(2,1)S(1)} %get-tuple-element.42), channel_id=1, source_target_pairs={{0,3},{1,0},{2,1},{3,2},{4,7},{5,4},{6,5},{7,6},{8,11},{9,8},{10,9... | collective-permute-start | bytes 737288 | tf_op jit(solution)/shard_map/ppermute | solution.py:22
  55.6 6.5 %collective-permute-start.14 = (s32[1,8320]{1,0:T(1,128)S(1)}, s32[1,8320]{1,0:T(1,128)S(1)}, u32[]{:S(2)}, u32[]{:S(2)}) collective-permute-start(s32[1,8320]{1,0:T(1,128)S(1)} %reshape_add_fusion), channel_id=1, source_target_pairs={{0,4},{4,8},{8,12},{12,16},{16,20},{20,24},{24,28},{28,32},{32,36}... | collective-permute-start | bytes 99848 | tf_op jit(solution)/shard_map/ppermute | solution.py:22
  62.1 0.1 ends.1
  62.1 0.1 collective-permute-start.12
  62.3 0.9 collective-permute-done.14.down_ref
  63.1 4.5 %collective-permute-start.13 = (bf16[80,512]{1,0:T(8,128)(2,1)S(1)}, bf16[80,512]{1,0:T(8,128)(2,1)S(1)}, u32[]{:S(2)}, u32[]{:S(2)}) collective-permute-start(bf16[80,512]{1,0:T(8,128)(2,1)S(1)} %get-tuple-element.44), channel_id=1, source_target_pairs={{0,124},{4,0},{8,4},{12,8},{16,12},{20,16},{24,20},{28,24},{32,28}... | collective-permute-start | bytes 245768 | tf_op jit(solution)/shard_map/ppermute | solution.py:22
  67.6 5.6 %one_hots.1 = (bf16[2,512,4096]{2,1,0:T(8,128)(2,1)S(1)}, bf16[2,4096,512]{2,1,0:T(8,128)(2,1)S(1)}, s32[4,4096]{1,0:T(4,128)S(1)}) custom-call(s32[1,8320]{1,0:T(1,128)S(1)} %collective-permute-done.14.down_ref, s32[1,4096]{1,0:T(1,128)S(1)} %copy-done.3, s32[1,4096]{1,0:T(1,128)S(1)} %copy-done.2, s32[1,1]{1,0:T(1,128)} %bitcast.9.count_ref), custom_call_target="tpu_custom_call" | custom-call | flops 83886080 | bytes 16777216 | tf_op jit(solution)/shard_map/one_hots/pallas_call | solution.py:218
  73.3 3.1 %links.1.rest_8_ = f32[64,16,128]{2,1,0:T(8,128)S(1)} custom-call(bf16[80,512]{1,0:T(8,128)(2,1)S(1)} %collective-permute-done.12.below_ref, bf16[80,512]{1,0:T(8,128)(2,1)S(1)} %collective-permute-done.13.above_ref, bf16[2,512,4096]{2,1,0:T(8,128)(2,1)S(1)} %get-tuple-element.45.g_ref, bf16[2,4096,512]{2,1,0:T(8,128)(2,1)S(1)} %get-tuple-element.46.s_ref, ...), custom_call_target="tpu_custom_call" | custom-call | flops 1342177280 | bytes 327680 | tf_op jit(solution)/shard_map/links/pallas_call | solution.py:268
  76.3 0.0 collective-permute-done.10.rest_6_
  76.4 6.1 %residual.1 = (bf16[10,65536]{1,0:T(8,128)(2,1)}, bf16[10,65536]{1,0:T(8,128)(2,1)}, f32[32,1,128]{2,1,0:T(1,128)S(1)}) custom-call(s32[1]{0:T(128)} %bitcast.me_ref, bf16[80,512]{1,0:T(8,128)(2,1)S(1)} %get-tuple-element.31.rest_0_, bf16[80,512]{1,0:T(8,128)(2,1)S(1)} %collective-permute-done.3.rest_1_, bf16[80,512]{1,0:T(8,128)(2,1)S(1)} %collective-permute-done.4.rest_2_, ...), custom_call_target="tpu_custom_call" | custom-call | flops 4194304000 | bytes 8388608 | tf_op jit(solution)/shard_map/residual/pallas_call | solution.py:443
  82.5 11.7 %all_to_all.5 = f32[32,1,128]{2,1,0:T(1,128)S(1)} all-to-all(f32[32,1,128]{2,1,0:T(1,128)S(1)} %get-tuple-element.50), channel_id=1, replica_groups=mesh['rows'=32,'vecs'=4] {'rows'}, dimensions={0} | all-to-all | bytes 32768 | tf_op jit(solution)/shard_map/all_to_all | solution.py:521
  94.1 0.1 reduce_sum.9
  94.2 0.6 rsqrt_multiply_fusion
  (32 shorter events, 0.2 us)
Async XLA Ops:
  0.6 39.3 %copy-start.4 = (bf16[100,40]{0,1:T(8,128)(2,1)S(1)}, bf16[100,40]{0,1:T(8,128)(2,1)}, u32[]{:S(2)}) copy-start(bf16[100,40]{0,1:T(8,128)(2,1)} %param.10) | copy-start | bytes 24004
  4.0 42.4 %copy-start = (bf16[200,1536]{1,0:T(8,128)(2,1)S(1)}, bf16[200,1536]{1,0:T(8,128)(2,1)}, u32[]{:S(2)}) copy-start(bf16[200,1536]{1,0:T(8,128)(2,1)} %get-tuple-element.35.from_ref) | copy-start | bytes 1843204
  4.0 45.6 %collective-permute-start.6 = (bf16[200,1536]{1,0:T(8,128)(2,1)}, bf16[200,1536]{1,0:T(8,128)(2,1)S(1)}, u32[]{:S(2)}, u32[]{:S(2)}) collective-permute-start(bf16[200,1536]{1,0:T(8,128)(2,1)} %get-tuple-element.36), channel_id=1, source_target_pairs={{0,1},{1,2},{2,3},{3,0},{4,5},{5,6},{6,7},{7,4},{8,9},{9,10},{10,1... | collective-permute-start | bytes 1843208 | tf_op jit(solution)/shard_map/ppermute | solution.py:22
  6.1 43.7 %collective-permute-start.7 = (bf16[200,1536]{1,0:T(8,128)(2,1)}, bf16[200,1536]{1,0:T(8,128)(2,1)S(1)}, u32[]{:S(2)}, u32[]{:S(2)}) collective-permute-start(bf16[200,1536]{1,0:T(8,128)(2,1)} %get-tuple-element.37), channel_id=1, source_target_pairs={{0,2},{1,3},{2,0},{3,1},{4,6},{5,7},{6,4},{7,5},{8,10},{9,11},{10,... | collective-permute-start | bytes 1843208 | tf_op jit(solution)/shard_map/ppermute | solution.py:22
  8.5 41.3 %collective-permute-start.8 = (bf16[200,1536]{1,0:T(8,128)(2,1)}, bf16[200,1536]{1,0:T(8,128)(2,1)S(1)}, u32[]{:S(2)}, u32[]{:S(2)}) collective-permute-start(bf16[200,1536]{1,0:T(8,128)(2,1)} %get-tuple-element.38), channel_id=1, source_target_pairs={{0,3},{1,0},{2,1},{3,2},{4,7},{5,4},{6,5},{7,6},{8,11},{9,8},{10,9... | collective-permute-start | bytes 1843208 | tf_op jit(solution)/shard_map/ppermute | solution.py:22
  11.8 43.7 %copy-start.2 = (s32[1,4096]{1,0:T(1,128)S(1)}, s32[1,4096]{1,0:T(1,128)}, u32[]{:S(2)}) copy-start(s32[1,4096]{1,0:T(1,128)} %upper_ref.1) | copy-start | bytes 49156
  11.8 43.7 %copy-start.3 = (s32[1,4096]{1,0:T(1,128)S(1)}, s32[1,4096]{1,0:T(1,128)}, u32[]{:S(2)}) copy-start(s32[1,4096]{1,0:T(1,128)} %lower_ref.1) | copy-start | bytes 49156
  11.8 26.5 %collective-permute-start = (bf16[200,512]{1,0:T(8,128)(2,1)}, bf16[200,512]{1,0:T(8,128)(2,1)S(1)}, u32[]{:S(2)}, u32[]{:S(2)}) collective-permute-start(bf16[200,512]{1,0:T(8,128)(2,1)} %get-tuple-element.28), channel_id=1, source_target_pairs={{0,1},{1,2},{2,3},{3,0},{4,5},{5,6},{6,7},{7,4},{8,9},{9,10},{10,1... | collective-permute-start | bytes 614408 | tf_op jit(solution)/shard_map/ppermute | solution.py:22
  12.2 31.8 %collective-permute-start.1 = (bf16[200,512]{1,0:T(8,128)(2,1)}, bf16[200,512]{1,0:T(8,128)(2,1)S(1)}, u32[]{:S(2)}, u32[]{:S(2)}) collective-permute-start(bf16[200,512]{1,0:T(8,128)(2,1)} %get-tuple-element.29), channel_id=1, source_target_pairs={{0,2},{1,3},{2,0},{3,1},{4,6},{5,7},{6,4},{7,5},{8,10},{9,11},{10,... | collective-permute-start | bytes 614408 | tf_op jit(solution)/shard_map/ppermute | solution.py:22
  38.3 5.7 %collective-permute-start.2 = (bf16[200,512]{1,0:T(8,128)(2,1)}, bf16[200,512]{1,0:T(8,128)(2,1)S(1)}, u32[]{:S(2)}, u32[]{:S(2)}) collective-permute-start(bf16[200,512]{1,0:T(8,128)(2,1)} %get-tuple-element.30), channel_id=1, source_target_pairs={{0,3},{1,0},{2,1},{3,2},{4,7},{5,4},{6,5},{7,6},{8,11},{9,8},{10,9... | collective-permute-start | bytes 614408 | tf_op jit(solution)/shard_map/ppermute | solution.py:22
  44.0 0.9 copy-start.1
  45.6 9.9 %collective-permute-start.3 = (bf16[80,512]{1,0:T(8,128)(2,1)S(1)}, bf16[80,512]{1,0:T(8,128)(2,1)S(1)}, u32[]{:S(2)}, u32[]{:S(2)}) collective-permute-start(bf16[80,512]{1,0:T(8,128)(2,1)S(1)} %get-tuple-element.32), channel_id=1, source_target_pairs={{0,1},{1,2},{2,3},{3,0},{4,5},{5,6},{6,7},{7,4},{8,9},{9,10},{10,1... | collective-permute-start | bytes 245768 | tf_op jit(solution)/shard_map/ppermute | solution.py:22
  47.1 8.5 %collective-permute-start.4 = (bf16[80,512]{1,0:T(8,128)(2,1)S(1)}, bf16[80,512]{1,0:T(8,128)(2,1)S(1)}, u32[]{:S(2)}, u32[]{:S(2)}) collective-permute-start(bf16[80,512]{1,0:T(8,128)(2,1)S(1)} %get-tuple-element.33), channel_id=1, source_target_pairs={{0,2},{1,3},{2,0},{3,1},{4,6},{5,7},{6,4},{7,5},{8,10},{9,11},{10,... | collective-permute-start | bytes 245768 | tf_op jit(solution)/shard_map/ppermute | solution.py:22
  49.6 12.5 %collective-permute-start.5 = (bf16[80,512]{1,0:T(8,128)(2,1)S(1)}, bf16[80,512]{1,0:T(8,128)(2,1)S(1)}, u32[]{:S(2)}, u32[]{:S(2)}) collective-permute-start(bf16[80,512]{1,0:T(8,128)(2,1)S(1)} %get-tuple-element.34), channel_id=1, source_target_pairs={{0,3},{1,0},{2,1},{3,2},{4,7},{5,4},{6,5},{7,6},{8,11},{9,8},{10,9... | collective-permute-start | bytes 245768 | tf_op jit(solution)/shard_map/ppermute | solution.py:22
  51.8 24.5 %collective-permute-start.10 = (bf16[80,1536]{1,0:T(8,128)(2,1)S(1)}, bf16[80,1536]{1,0:T(8,128)(2,1)S(1)}, u32[]{:S(2)}, u32[]{:S(2)}) collective-permute-start(bf16[80,1536]{1,0:T(8,128)(2,1)S(1)} %get-tuple-element.41), channel_id=1, source_target_pairs={{0,2},{1,3},{2,0},{3,1},{4,6},{5,7},{6,4},{7,5},{8,10},{9,11},{10,... | collective-permute-start | bytes 737288 | tf_op jit(solution)/shard_map/ppermute | solution.py:22
  53.6 22.7 %collective-permute-start.11 = (bf16[80,1536]{1,0:T(8,128)(2,1)S(1)}, bf16[80,1536]{1,0:T(8,128)(2,1)S(1)}, u32[]{:S(2)}, u32[]{:S(2)}) collective-permute-start(bf16[80,1536]{1,0:T(8,128)(2,1)S(1)} %get-tuple-element.42), channel_id=1, source_target_pairs={{0,3},{1,0},{2,1},{3,2},{4,7},{5,4},{6,5},{7,6},{8,11},{9,8},{10,9... | collective-permute-start | bytes 737288 | tf_op jit(solution)/shard_map/ppermute | solution.py:22
  55.5 20.8 %collective-permute-start.9 = (bf16[80,1536]{1,0:T(8,128)(2,1)S(1)}, bf16[80,1536]{1,0:T(8,128)(2,1)S(1)}, u32[]{:S(2)}, u32[]{:S(2)}) collective-permute-start(bf16[80,1536]{1,0:T(8,128)(2,1)S(1)} %get-tuple-element.40), channel_id=1, source_target_pairs={{0,1},{1,2},{2,3},{3,0},{4,5},{5,6},{6,7},{7,4},{8,9},{9,10},{10,1... | collective-permute-start | bytes 737288 | tf_op jit(solution)/shard_map/ppermute | solution.py:22
  55.6 7.5 %collective-permute-start.14 = (s32[1,8320]{1,0:T(1,128)S(1)}, s32[1,8320]{1,0:T(1,128)S(1)}, u32[]{:S(2)}, u32[]{:S(2)}) collective-permute-start(s32[1,8320]{1,0:T(1,128)S(1)} %reshape_add_fusion), channel_id=1, source_target_pairs={{0,4},{4,8},{8,12},{12,16},{16,20},{20,24},{24,28},{28,32},{32,36}... | collective-permute-start | bytes 99848 | tf_op jit(solution)/shard_map/ppermute | solution.py:22
  62.1 11.1 %collective-permute-start.12 = (bf16[80,512]{1,0:T(8,128)(2,1)S(1)}, bf16[80,512]{1,0:T(8,128)(2,1)S(1)}, u32[]{:S(2)}, u32[]{:S(2)}) collective-permute-start(bf16[80,512]{1,0:T(8,128)(2,1)S(1)} %get-tuple-element.43), channel_id=1, source_target_pairs={{0,4},{4,8},{8,12},{12,16},{16,20},{20,24},{24,28},{28,32},{32,36}... | collective-permute-start | bytes 245768 | tf_op jit(solution)/shard_map/ppermute | solution.py:22
  63.1 10.1 %collective-permute-start.13 = (bf16[80,512]{1,0:T(8,128)(2,1)S(1)}, bf16[80,512]{1,0:T(8,128)(2,1)S(1)}, u32[]{:S(2)}, u32[]{:S(2)}) collective-permute-start(bf16[80,512]{1,0:T(8,128)(2,1)S(1)} %get-tuple-element.44), channel_id=1, source_target_pairs={{0,124},{4,0},{8,4},{12,8},{16,12},{20,16},{24,20},{28,24},{32,28}... | collective-permute-start | bytes 245768 | tf_op jit(solution)/shard_map/ppermute | solution.py:22
  73.2 3.1 %copy-start.5 = (f32[65536]{0:T(1024)S(1)}, f32[65536]{0:T(1024)}, u32[]{:S(2)}) copy-start(f32[65536]{0:T(1024)} %param.12) | copy-start | bytes 786436
  73.2 3.1 %copy-start.6 = (f32[65536]{0:T(1024)S(1)}, f32[65536]{0:T(1024)}, u32[]{:S(2)}) copy-start(f32[65536]{0:T(1024)} %param.13) | copy-start | bytes 786436
  73.2 3.1 %copy-start.7 = (f32[65536]{0:T(1024)S(1)}, f32[65536]{0:T(1024)}, u32[]{:S(2)}) copy-start(f32[65536]{0:T(1024)} %param.14) | copy-start | bytes 786436
  73.3 3.1 %copy-start.8 = (f32[10]{0:T(128)S(1)}, f32[10]{0:T(128)}, u32[]{:S(2)}) copy-start(f32[10]{0:T(128)} %param.11) | copy-start | bytes 124

commit v3 on v2

--- a/solution.py
+++ b/solution.py
@@ -80,24 +80,37 @@
     return [pltpu.VMEM((parts, ranks, chunk.width), BF), pltpu.SemaphoreType.DMA((parts,))]
 
 
-def pack_kernel(chunk, parts, me_ref, basis_ref, *rest):
-    Packing(chunk, parts, me_ref[0], basis_ref, rest[:parts], *rest[parts:]).finish()
-
-
-def pack(me, basis, chunk, parts):
+def pack_kernel(chunks, parts, me_ref, basis_ref, *rest):
+    n = parts * len(chunks)
+    outs, scratch = rest[:n], rest[n:]
+    work = [
+        Packing(
+            chunk, parts, me_ref[0], basis_ref, outs[i * parts : (i + 1) * parts],
+            *scratch[2 * i : 2 * i + 2]
+        )
+        for i, chunk in enumerate(chunks)
+    ]
+    for w in work:
+        w.finish()
+
+
+def pack(me, basis, chunks, parts):
     ranks = basis.shape[0]
-    return list(
-        pl.pallas_call(
-            functools.partial(pack_kernel, chunk, parts),
-            out_shape=[packed_shape(chunk, ranks)] * parts,
-            in_specs=[SMEM, ANY],
-            out_specs=[VMEM] * parts,
-            scratch_shapes=pack_scratch(chunk, ranks, parts),
-            compiler_params=params(60),
-            cost_estimate=cost(1, 4 * parts * ranks * chunk.width),
-            name="pack",
-        )(me, basis)
-    )
+    shapes, scratch = [], []
+    for chunk in chunks:
+        shapes += [packed_shape(chunk, ranks)] * parts
+        scratch += pack_scratch(chunk, ranks, parts)
+    packed = pl.pallas_call(
+        functools.partial(pack_kernel, chunks, parts),
+        out_shape=shapes,
+        in_specs=[SMEM, ANY],
+        out_specs=[VMEM] * len(shapes),
+        scratch_shapes=scratch,
+        compiler_params=params(60),
+        cost_estimate=cost(1, 4 * parts * ranks * sum(chunk.width for chunk in chunks)),
+        name="pack",
+    )(me, basis)
+    return [list(packed[i * parts : (i + 1) * parts]) for i in range(len(chunks))]
 
 
 def orders(shape, axis, main, rest):
@@ -184,8 +197,10 @@
     slots = lower_ref.shape[1]
     shift = low.bit_length() - 1
     step = 256
-    lane = lax.broadcasted_iota(jnp.int32, (low, 1), 0)
-    across = lax.broadcasted_iota(jnp.int32, (1, low), 1)
+    centred = lambda cells: (jnp.bitwise_and(cells, low - 1) - low // 2).astype(F32).astype(BF)
+    lane = centred(lax.broadcasted_iota(jnp.int32, (low, step), 0))
+    across = centred(lax.broadcasted_iota(jnp.int32, (LANES, low), 1))
+    one, none = jnp.ones((), BF), jnp.zeros((), BF)
     ways = (
         (down_ref, 0, down_ref, slots, down_ref[:, 2 * slots : 2 * slots + 1]),
         (upper_ref, 0, lower_ref, 0, count_ref[...]),
@@ -198,13 +213,14 @@
         for d, (from_ref, f0, to_ref, t0, count) in enumerate(ways):
             g = from_ref[:, pl.ds(pl.multiple_of(f0 + i * step, step), step)]
             s = to_ref[:, pl.ds(pl.multiple_of(t0 + i * step, step), step)]
-            g_low, s_low = jnp.bitwise_and(g, low - 1), jnp.bitwise_and(s, low - 1)
-            g_ref[d, :, at] = jnp.where(lane == g_low, 1.0, 0.0).astype(BF)
+            wanted = jnp.broadcast_to(centred(g), (low, step))
+            g_ref[d, :, at] = jnp.where(lane == wanted, one, none)
+            s_low = (jnp.bitwise_and(s, low - 1) - low // 2).astype(F32)
             for j in range(0, step, LANES):
-                down_sub = jnp.broadcast_to(s_low[:, j : j + LANES], (LANES, LANES)).T
-                down_sub = jnp.concatenate([down_sub] * (low // LANES), axis=1)
+                turned = jnp.broadcast_to(s_low[:, j : j + LANES], (LANES, LANES)).T.astype(BF)
+                turned = jnp.concatenate([turned] * (low // LANES), axis=1)
                 rows = pl.ds(pl.multiple_of(i * step + j, LANES), LANES)
-                s_ref[d, rows, :] = jnp.where(down_sub == across, 1.0, 0.0).astype(BF)
+                s_ref[d, rows, :] = jnp.where(turned == across, one, none)
             seg_ref[2 * d : 2 * d + 1, at] = lax.shift_right_logical(g, shift)
             seg_ref[2 * d + 1 : 2 * d + 2, at] = jnp.where(
                 slot < count, lax.shift_right_logical(s, shift), -1
@@ -227,44 +243,56 @@
 
 
 def link_kernel(below_ref, above_ref, g_ref, s_ref, seg_ref, out_ref, put):
-    rows, low = below_ref.shape
-    slots = g_ref.shape[2]
+    rows, wide = below_ref.shape
+    low, slots = g_ref.shape[1:]
+    per = wide // low
     vfull = 8
     vrest = rows // SEGS - vfull
     step = 512
     tail_rows = SEGS * vrest
     tail_seg = lax.broadcasted_iota(jnp.int32, (tail_rows, 1), 0) // vrest
+    planes = [
+        jnp.concatenate([ref[:, h * low : (h + 1) * low] for h in range(per)], axis=0)
+        for ref in (below_ref, above_ref)
+    ]
     for i in range(slots // step):
         at = slice(i * step, (i + 1) * step)
-        for d, plane_ref in enumerate((below_ref, above_ref)):
-            got = jnp.dot(plane_ref[...], g_ref[d, :, at], preferred_element_type=F32)
+        for d, plane in enumerate(planes):
+            got = jnp.dot(plane, g_ref[d, :, at], preferred_element_type=F32)
             gh, sh = seg_ref[2 * d : 2 * d + 1, at], seg_ref[2 * d + 1 : 2 * d + 2, at]
-            main = got[0:vfull]
-            for c in range(1, SEGS):
-                main = jnp.where(gh == c, got[c * vfull : (c + 1) * vfull], main)
-            tail = jnp.where(gh == tail_seg, got[SEGS * vfull : rows], 0.0)
+            main, tail = got[0:vfull], jnp.zeros((tail_rows, step), F32)
+            for h in range(per):
+                for c in range(SEGS):
+                    part = got[h * rows + c * vfull : h * rows + (c + 1) * vfull]
+                    main = jnp.where(gh == c * per + h, part, main)
+                part = got[h * rows + SEGS * vfull : (h + 1) * rows]
+                tail = jnp.where(gh == tail_seg * per + h, part, tail)
             shift = vrest
             while shift < tail_rows:
                 tail = tail + pltpu.roll(tail, shift, 0)
                 shift *= 2
-            pieces = [jnp.where(sh == c, main, 0.0) for c in range(SEGS)]
-            pieces.append(jnp.where(sh == tail_seg, tail, 0.0))
+            pieces = []
+            for h in range(per):
+                pieces += [jnp.where(sh == c * per + h, main, 0.0) for c in range(SEGS)]
+                pieces.append(jnp.where(sh == tail_seg * per + h, tail, 0.0))
             put[d, :, at] = jnp.concatenate(pieces, axis=0).astype(BF)
 
     for d in range(2):
         total = jnp.dot(put[d], s_ref[d], preferred_element_type=F32)
-        for c in range(SEGS):
-            for k in range(low // LANES):
-                t = d * 32 + c * (low // LANES) + k
-                at = slice(k * LANES, (k + 1) * LANES)
-                out_ref[t, 0:8, :] = total[c * 8 : (c + 1) * 8, at]
-                first = SEGS * 8 + c * vrest
-                out_ref[t, 8 : 8 + vrest, :] = total[first : first + vrest, at]
+        for h in range(per):
+            for c in range(SEGS):
+                for k in range(low // LANES):
+                    t = d * 32 + (c * per + h) * (low // LANES) + k
+                    at = slice(k * LANES, (k + 1) * LANES)
+                    first = h * rows + c * 8
+                    out_ref[t, 0:8, :] = total[first : first + 8, at]
+                    first = h * rows + SEGS * 8 + c * vrest
+                    out_ref[t, 8 : 8 + vrest, :] = total[first : first + vrest, at]
 
 
 def link_terms(below, above, hots):
-    rows, low = below.shape
-    slots = hots[0].shape[2]
+    rows = below.size // hots[0].shape[1]
+    low, slots = hots[0].shape[1:]
     return pl.pallas_call(
         link_kernel,
         out_shape=jax.ShapeDtypeStruct((64, NP, LANES), F32),
@@ -319,14 +347,15 @@
 
 
 class Output:
-    def __init__(self, refs, bufs, sem, low):
-        self.refs, self.bufs, self.sem, self.low = refs, bufs, sem, low
+    def __init__(self, refs, bufs, sem, shifts):
+        self.refs, self.bufs, self.sem, self.shifts = refs, bufs, sem, shifts
         self.copies = []
 
     def send(self, first, last):
         lanes = (last - first) * WID * WID
         to = pl.ds(first * WID * WID, lanes)
-        at = pl.ds((first - self.low) * WID * WID, lanes)
+        shift = self.shifts.get(first, self.shifts.get(None, 0))
+        at = pl.ds((first - shift) * WID * WID, lanes)
         for i in range(2):
             copy = pltpu.make_async_copy(
                 self.bufs[i].at[:, at], self.refs[i].at[:, to], self.sem.at[len(self.copies)]
@@ -399,29 +428,62 @@
     return vsum, rsum
 
 
-def residual_kernel(chunks, parts, planes, me_ref, *rest):
+def finished_planes(terms, cells, z0, carry, links, outs, out, low, high, ends):
+    ready = []
+    for z in ends:
+        carry = one_plane(terms, cells, z, z0, carry, links.get(z), outs(z))
+        ready.append((z, z + 1))
+    for first, end in cuts(low, high):
+        carry = lax.fori_loop(
+            first, end, lambda z, c: one_plane(terms, cells, z, z0, c, None, outs(first)), carry
+        )
+        for cut in ready:
+            out.send(*cut)
+        ready = [(first, end)]
+    return carry, ready
+
+
+def part_one_kernel(chunks, parts, planes, split, me_ref, *rest):
     nz = parts * len(chunks)
     z_refs, rest = rest[:nz], rest[nz:]
     link_ref, eig_ref, stiff_ref, damp_ref, mass_ref = rest[:5]
-    vec_ref, res_ref, out_ref, cells, vec_buf, res_buf, sem = rest[5:]
+    vec_ref, res_ref, edge_ref, sum_ref, cells, vec_buf, res_buf, sem = rest[5:]
     vecs = vec_ref.shape[0]
     tiles = WID * WID // LANES
     for i, chunk in enumerate(chunks):
         unpack(cells, 0, chunk, me_ref[0], parts, z_refs[i * parts : (i + 1) * parts], vecs - 8)
     terms = Terms(eig_ref, stiff_ref, damp_ref, mass_ref)
-    outs = (vec_buf, res_buf, 0)
-    out = Output((vec_ref, res_ref), (vec_buf, res_buf), sem, 0)
+    moved = (planes - 1 - split) * WID * WID
+    outs = lambda z: (vec_buf, res_buf, moved if z == planes - 1 else 0)
+    out = Output((vec_ref, res_ref), (vec_buf, res_buf), sem, {planes - 1: planes - 1 - split})
     zero = jnp.zeros((NP, LANES), F32)
-    carry = one_plane(terms, cells, 0, 0, (zero, zero), (link_ref, 0, 1), outs)
-    carry = one_plane(terms, cells, planes - 1, 0, carry, (link_ref, tiles, -1), outs)
-    ready = [(0, 1), (planes - 1, planes)]
-    for first, end in cuts(1, planes - 1):
-        carry = lax.fori_loop(
-            first, end, lambda z, c: one_plane(terms, cells, z, 0, c, None, outs), carry
-        )
-        for cut in ready:
-            out.send(*cut)
-        ready = [(first, end)]
+    links = {0: (link_ref, 0, 1), planes - 1: (link_ref, tiles, -1)}
+    carry, ready = finished_planes(
+        terms, cells, 0, (zero, zero), links, outs, out, 1, split, (0, planes - 1)
+    )
+    edge_ref[0 : 2 * tiles] = cells[(split - 1) * tiles : (split + 1) * tiles]
+    edge_ref[2 * tiles : 4 * tiles] = cells[(planes - 2) * tiles : planes * tiles]
+    sum_ref[0], sum_ref[1] = carry
+    for cut in ready:
+        out.send(*cut)
+    out.wait()
+
+
+def part_two_kernel(chunk, parts, planes, split, me_ref, *rest):
+    z_refs, rest = rest[:parts], rest[parts:]
+    edge_ref, eig_ref, stiff_ref, damp_ref, mass_ref, early_ref, _, _ = rest[:8]
+    vec_ref, res_ref, out_ref, cells, vec_buf, res_buf, sem = rest[8:]
+    vecs = vec_ref.shape[0]
+    tiles = WID * WID // LANES
+    z0 = split - 1
+    cells[0 : 2 * tiles] = edge_ref[0 : 2 * tiles]
+    cells[(planes - 2 - z0) * tiles : (planes - z0) * tiles] = edge_ref[2 * tiles : 4 * tiles]
+    unpack(cells, z0 * tiles, chunk, me_ref[0], parts, z_refs, vecs - 8)
+    terms = Terms(eig_ref, stiff_ref, damp_ref, mass_ref)
+    outs = lambda z: (vec_buf, res_buf, split * WID * WID)
+    out = Output((vec_ref, res_ref), (vec_buf, res_buf), sem, {None: split})
+    carry = (early_ref[0], early_ref[1])
+    carry, ready = finished_planes(terms, cells, z0, carry, {}, outs, out, split, planes - 1, ())
     vsum, rsum = carry
     vrow = jnp.broadcast_to(jnp.sum(vsum, axis=1, keepdims=True), (NP, LANES))
     rrow = jnp.broadcast_to(jnp.sum(rsum, axis=1, keepdims=True), (NP, LANES))
@@ -436,25 +498,53 @@
     out.wait()
 
 
-def residual(me, chunks, zs, link, eig, diagonals, vecs, rows_local, parts, copies):
+def buffers(planes, kept_planes, vecs):
+    tiles = WID * WID // LANES
+    return [
+        pltpu.VMEM((planes * tiles, NP, LANES), F32),
+        pltpu.VMEM((vecs, kept_planes * WID * WID), BF),
+        pltpu.VMEM((vecs, kept_planes * WID * WID), BF),
+        pltpu.SemaphoreType.DMA((16,)),
+    ]
+
+
+def part_one(me, chunks, zs, link, eig, diagonals, vecs, rows_local, parts, split):
     planes = rows_local // (WID * WID)
     tiles = WID * WID // LANES
     whole = jax.ShapeDtypeStruct((vecs, rows_local), BF)
     return pl.pallas_call(
-        functools.partial(residual_kernel, chunks, parts, planes),
+        functools.partial(part_one_kernel, chunks, parts, planes, split),
+        out_shape=(
+            whole,
+            whole,
+            jax.ShapeDtypeStruct((4 * tiles, NP, LANES), F32),
+            jax.ShapeDtypeStruct((2, NP, LANES), F32),
+        ),
+        in_specs=[SMEM] + [VMEM] * (len(zs) + 5),
+        out_specs=(ANY, ANY, VMEM, VMEM),
+        scratch_shapes=buffers(planes, split + 1, vecs),
+        compiler_params=params(20),
+        cost_estimate=cost(2000 * NP * rows_local, 4 * NP * rows_local),
+        name="part_one",
+    )(me, *zs, link, eig, *diagonals)
+
+
+def part_two(me, chunk, zs, edge, eig, diagonals, early, vec, res, parts, split, copies):
+    vecs, rows_local = vec.shape
+    planes = rows_local // (WID * WID)
+    whole = jax.ShapeDtypeStruct((vecs, rows_local), BF)
+    first = 1 + parts + 6
+    return pl.pallas_call(
+        functools.partial(part_two_kernel, chunk, parts, planes, split),
         out_shape=(whole, whole, jax.ShapeDtypeStruct((copies, 1, LANES), F32)),
-        in_specs=[SMEM] + [VMEM] * (len(zs) + 5),
+        in_specs=[SMEM] + [VMEM] * (parts + 6) + [ANY, ANY],
         out_specs=(ANY, ANY, VMEM),
-        scratch_shapes=[
-            pltpu.VMEM((planes * tiles, NP, LANES), F32),
-            pltpu.VMEM((vecs, rows_local), BF),
-            pltpu.VMEM((vecs, rows_local), BF),
-            pltpu.SemaphoreType.DMA((32,)),
-        ],
-        compiler_params=params(24),
-        cost_estimate=cost(4000 * NP * rows_local, 8 * NP * rows_local),
-        name="residual",
-    )(me, *zs, link, eig, *diagonals)
+        scratch_shapes=buffers(planes - split + 1, planes - 1 - split, vecs),
+        input_output_aliases={first: 0, first + 1: 1},
+        compiler_params=params(20),
+        cost_estimate=cost(2000 * NP * rows_local, 4 * NP * rows_local),
+        name="part_two",
+    )(me, *zs, edge, eig, *diagonals, early, vec, res)
 
 
 def kept(value):
@@ -494,29 +584,40 @@
     planes = rows_local // (WID * WID)
     me = lax.axis_index("vecs").astype(jnp.int32)[None]
     ends = Chunk(None, 4, parts, planes)
-    inner = Chunk(2, planes - 4, parts, planes)
+    middle = (planes - 4) // 2 + 2
+    one = Chunk(2, middle - 2, parts, planes)
+    two = Chunk(middle, planes - 2 - middle, parts, planes)
     wide_count = jnp.broadcast_to(link_count[:, None], (1, LANES))
     lists = jnp.concatenate([lower_cells, upper_cells, wide_count], axis=1)
-    ends_out = pack(me, basis, ends, parts)
+    (ends_out,) = pack(me, basis, [ends], parts)
     ends_out = exchanged(ends_out, "vecs")
-    inner_out = pack(me, basis, inner, parts)
-    inner_out = exchanged(inner_out, "vecs")
+    one_out, two_out = pack(me, basis, [one, two], parts)
+    one_out = exchanged(one_out, "vecs")
     down = from_behind(lists, "rows", 1)
     matrix = spread_coefficients(me, coefficients, parts, ranks, vecs)
-    hots = one_hots(ends.seg, down, lower_cells, upper_cells, wide_count[:, :1])
-    inner_out[0] = kept(inner_out[0])
     z_ends = mix(matrix, ends_out, 0, ends.seg, vecs)
     z_ends = exchanged(z_ends, "vecs")
-    z_inner = mix(matrix, inner_out, 0, inner.seg, vecs)
-    z_inner = exchanged(z_inner, "vecs")
+    two_out = exchanged(two_out, "vecs")
+    hots = one_hots(min(ends.seg, 256), down, lower_cells, upper_cells, wide_count[:, :1])
+    one_out[0], two_out[0] = kept(one_out[0]), kept(two_out[0])
+    z_one = mix(matrix, one_out, 0, one.seg, vecs)
+    z_one = exchanged(z_one, "vecs")
     plane_low, plane_high = end_planes(me, z_ends)
     from_below = from_behind(plane_high, "rows", 1)
     from_above = from_behind(plane_low, "rows", -1)
     link = link_terms(from_below, from_above, hots)
+    z_two = mix(matrix, two_out, 0, two.seg, vecs)
+    z_two = exchanged(z_two, "vecs")
     diagonals = [a.reshape(rows_local // LANES, LANES) for a in (stiffness, damping, mass)]
-    eigvecs, residuals, sums = residual(
-        me, [ends, inner], z_ends + z_inner, link, eigen_values[None, :], diagonals, vecs,
-        rows_local, parts, subdomains,
+    eig = eigen_values[None, :]
+    split = middle - 1
+    eigvecs, residuals, edge, sums = part_one(
+        me, [ends, one], z_ends + z_one, link, eig, diagonals, vecs, rows_local, parts,
+        split,
+    )
+    eigvecs, residuals, sums = part_two(
+        me, two, z_two, edge, eig, diagonals, sums, eigvecs, residuals, parts, split,
+        subdomains,
     )
     total = lax.all_to_all(sums, "rows", 0, 0, tiled=True).sum(axis=(0, 1))
     vector_sq, residual_sq = total[:vecs], total[NP : NP + vecs]

time: 95 us -> 90.2 us (0.949)
  waiting for transfers between devices: 29.4 us -> 6.88 us
  starting transfers between devices: 26.8 us -> 40.8 us
  blocking collectives: 11.7 us -> 19.1 us
  Pallas kernels: 23.8 us -> 20.7 us
    ppermute x15 -> x21, waiting for transfers between devices: 29.4 us -> 6.88 us  [from_behind(): return lax.ppermute(value, axis, pairs)]
    ppermute x15 -> x21, starting transfers between devices: 26.8 us -> 40.8 us  [from_behind(): return lax.ppermute(value, axis, pairs)]
    all_to_all x1, blocking collectives: 11.7 us -> 19.1 us  [on_device(): total = lax.all_to_all(sums, 'rows', 0, 0, tiled=True).sum(axis=(0, 1))]
    pallas_call x1, Pallas kernels: 5.63 us -> 2.34 us  [one_hots(): pl.pallas_call(functools.partial(one_hot_kernel, low), out_shape=(hot, ho...]
    pallas_call x3 -> x4, Pallas kernels: 11.5 us -> 12.8 us  [the longest x2 5.5 us: pack(): pl.pallas_call(functools.partial(pack_kernel, chunks, parts), out_shape=s...]
    pallas_call x1, Pallas kernels: 3.06 us -> 1.91 us  [link_terms(): pl.pallas_call(link_kernel, out_shape=jax.ShapeDtypeStruct((64, NP, LANES...]
    pallas_call x2 -> x3, Pallas kernels: 2.65 us -> 2.65 us  [mix(): pl.pallas_call(functools.partial(mix_kernel, parts, lane, seg), out_shape...]
  transfers between devices with their start and end apart: 15 -> 21, of which waited for: 3 -> 4; matrix products, arithmetic and copies ran while one was open for 0% -> 0% of each run, Pallas kernels for 15% -> 17%
where the time goes in v3:
time: 90.2 us; the launch traced here: 90.1 us
  starting transfers between devices  40.8 us (45%)
  Pallas kernels  20.7 us (23%)
  blocking collectives  19.1 us (21%)
  waiting for transfers between devices  6.88 us (8%)
  between operations  1.8 us (2%)
    ppermute x21, starting transfers between devices, from_behind(): return lax.ppermute(value, axis, pairs)  40.8 us
    all_to_all x1, blocking collectives, on_device(): total = lax.all_to_all(sums, 'rows', 0, 0, tiled=True).sum(axis=(0, 1))  19.1 us
    ppermute x21, waiting for transfers between devices, from_behind(): return lax.ppermute(value, axis, pairs)  6.88 us
    pallas_call x2, Pallas kernels, pack(): pl.pallas_call(functools.partial(pack_kernel, chunks, parts), out_shape=s...  5.5 us
    pallas_call x1, Pallas kernels, part_one(): pl.pallas_call(functools.partial(part_one_kernel, chunks, parts, planes,...  3.68 us
    pallas_call x1, Pallas kernels, part_two(): pl.pallas_call(functools.partial(part_two_kernel, chunk, parts, planes, s...  3.63 us
    pallas_call x3, Pallas kernels, mix(): pl.pallas_call(functools.partial(mix_kernel, parts, lane, seg), out_shape...  2.65 us
    pallas_call x1, Pallas kernels, one_hots(): pl.pallas_call(functools.partial(one_hot_kernel, low), out_shape=(hot, ho...  2.34 us
  transfers between devices with their start and end apart: 21, of which 4 were waited for; matrix products, arithmetic and copies ran while one was open for 0% of the time, Pallas kernels for 17%

profile of v3, /device:TPU:1, one launch (start us, length us, event | category | flops | bytes accessed | tf_op | source)
XLA Modules:
  0.0 90.1 jit_solution(16107842488955225365)
XLA Ops:
  0.6 2.1 %pack.3 = (bf16[200,512]{1,0:T(8,128)(2,1)}, bf16[200,512]{1,0:T(8,128)(2,1)}, bf16[200,512]{1,0:T(8,128)(2,1)}, bf16[200,512]{1,0:T(8,128)(2,1)}) custom-call(s32[1]{0:T(128)} %bitcast.me_ref, bf16[25,65536]{1,0:T(8,128)(2,1)} %basis_ref.3), custom_call_target="tpu_custom_call" | custom-call | flops 1 | bytes 1638400 | tf_op jit(solution)/shard_map/pack/pallas_call | solution.py:103
  2.8 2.1 %collective-permute-start.6 = (bf16[200,512]{1,0:T(8,128)(2,1)}, bf16[200,512]{1,0:T(8,128)(2,1)S(1)}, u32[]{:S(2)}, u32[]{:S(2)}) collective-permute-start(bf16[200,512]{1,0:T(8,128)(2,1)} %get-tuple-element.48), channel_id=1, source_target_pairs={{0,1},{1,2},{2,3},{3,0},{4,5},{5,6},{6,7},{7,4},{8,9},{9,10},{10,1... | collective-permute-start | bytes 614408 | tf_op jit(solution)/shard_map/ppermute | solution.py:22
  4.9 2.5 %collective-permute-start.7 = (bf16[200,512]{1,0:T(8,128)(2,1)}, bf16[200,512]{1,0:T(8,128)(2,1)S(1)}, u32[]{:S(2)}, u32[]{:S(2)}) collective-permute-start(bf16[200,512]{1,0:T(8,128)(2,1)} %get-tuple-element.49), channel_id=1, source_target_pairs={{0,2},{1,3},{2,0},{3,1},{4,6},{5,7},{6,4},{7,5},{8,10},{9,11},{10,... | collective-permute-start | bytes 614408 | tf_op jit(solution)/shard_map/ppermute | solution.py:22
  7.3 1.2 %collective-permute-start.8 = (bf16[200,512]{1,0:T(8,128)(2,1)}, bf16[200,512]{1,0:T(8,128)(2,1)S(1)}, u32[]{:S(2)}, u32[]{:S(2)}) collective-permute-start(bf16[200,512]{1,0:T(8,128)(2,1)} %get-tuple-element.50), channel_id=1, source_target_pairs={{0,3},{1,0},{2,1},{3,2},{4,7},{5,4},{6,5},{7,6},{8,11},{9,8},{10,9... | collective-permute-start | bytes 614408 | tf_op jit(solution)/shard_map/ppermute | solution.py:22
  8.5 3.4 %pack.2 = (bf16[200,768]{1,0:T(8,128)(2,1)}, bf16[200,768]{1,0:T(8,128)(2,1)}, bf16[200,768]{1,0:T(8,128)(2,1)}, bf16[200,768]{1,0:T(8,128)(2,1)}, bf16[200,768]...) custom-call(s32[1]{0:T(128)} %bitcast.me_ref, ...), custom_call_target="tpu_custom_call" | custom-call | flops 1 | bytes 4915200 | tf_op jit(solution)/shard_map/pack/pallas_call | solution.py:103
  13.2 0.9 spread.1.l_ref
  14.1 2.3 %collective-permute-done.7.rest_2_ = bf16[200,512]{1,0:T(8,128)(2,1)S(1)} collective-permute-done((bf16[200,512]{1,0:T(8,128)(2,1)}, bf16[200,512]{1,0:T(8,128)(2,1)S(1)}, u32[]{:S(2)}, u32[]{:S(2)}) %collective-permute-start.7) | collective-permute-done | bytes 204832 | tf_op jit(solution)/shard_map/ppermute | solution.py:22
  16.4 0.7 mix.4
  17.1 2.2 %collective-permute-start.10 = (bf16[80,512]{1,0:T(8,128)(2,1)S(1)}, bf16[80,512]{1,0:T(8,128)(2,1)S(1)}, u32[]{:S(2)}, u32[]{:S(2)}) collective-permute-start(bf16[80,512]{1,0:T(8,128)(2,1)S(1)} %get-tuple-element.53), channel_id=1, source_target_pairs={{0,2},{1,3},{2,0},{3,1},{4,6},{5,7},{6,4},{7,5},{8,10},{9,11},{10,... | collective-permute-start | bytes 245768 | tf_op jit(solution)/shard_map/ppermute | solution.py:22
  19.3 1.5 %collective-permute-start.11 = (bf16[80,512]{1,0:T(8,128)(2,1)S(1)}, bf16[80,512]{1,0:T(8,128)(2,1)S(1)}, u32[]{:S(2)}, u32[]{:S(2)}) collective-permute-start(bf16[80,512]{1,0:T(8,128)(2,1)S(1)} %get-tuple-element.54), channel_id=1, source_target_pairs={{0,3},{1,0},{2,1},{3,2},{4,7},{5,4},{6,5},{7,6},{8,11},{9,8},{10,9... | collective-permute-start | bytes 245768 | tf_op jit(solution)/shard_map/ppermute | solution.py:22
  20.8 3.8 %collective-permute-start.20 = (s32[1,8320]{1,0:T(1,128)S(1)}, s32[1,8320]{1,0:T(1,128)S(1)}, u32[]{:S(2)}, u32[]{:S(2)}) collective-permute-start(s32[1,8320]{1,0:T(1,128)S(1)} %reshape_add_fusion), channel_id=1, source_target_pairs={{0,4},{4,8},{8,12},{12,16},{16,20},{20,24},{24,28},{28,32},{32,36}... | collective-permute-start | bytes 99848 | tf_op jit(solution)/shard_map/ppermute | solution.py:22
  24.7 1.0 %collective-permute-done.20.down_ref = s32[1,8320]{1,0:T(1,128)S(1)} collective-permute-done((s32[1,8320]{1,0:T(1,128)S(1)}, s32[1,8320]{1,0:T(1,128)S(1)}, u32[]{:S(2)}, u32[]{:S(2)}) %collective-permute-start.20) | collective-permute-done | bytes 33312 | tf_op jit(solution)/shard_map/ppermute | solution.py:22
  25.7 1.7 %collective-permute-start.13 = (bf16[200,768]{1,0:T(8,128)(2,1)S(1)}, bf16[200,768]{1,0:T(8,128)(2,1)S(1)}, u32[]{:S(2)}, u32[]{:S(2)}) collective-permute-start(bf16[200,768]{1,0:T(8,128)(2,1)S(1)} %copy-done.14), channel_id=1, source_target_pairs={{0,2},{1,3},{2,0},{3,1},{4,6},{5,7},{6,4},{7,5},{8,10},{9,11},{10,... | collective-permute-start | bytes 921608 | tf_op jit(solution)/shard_map/ppermute | solution.py:22
  27.5 0.9 collective-permute-start.14
  28.3 0.6 collective-permute-start
  28.9 1.6 %collective-permute-start.1 = (bf16[200,768]{1,0:T(8,128)(2,1)S(1)}, bf16[200,768]{1,0:T(8,128)(2,1)S(1)}, u32[]{:S(2)}, u32[]{:S(2)}) collective-permute-start(bf16[200,768]{1,0:T(8,128)(2,1)S(1)} %copy-done.11), channel_id=1, source_target_pairs={{0,2},{1,3},{2,0},{3,1},{4,6},{5,7},{6,4},{7,5},{8,10},{9,11},{10,... | collective-permute-start | bytes 921608 | tf_op jit(solution)/shard_map/ppermute | solution.py:22
  30.5 2.0 %collective-permute-start.2 = (bf16[200,768]{1,0:T(8,128)(2,1)S(1)}, bf16[200,768]{1,0:T(8,128)(2,1)S(1)}, u32[]{:S(2)}, u32[]{:S(2)}) collective-permute-start(bf16[200,768]{1,0:T(8,128)(2,1)S(1)} %copy-done.10), channel_id=1, source_target_pairs={{0,3},{1,0},{2,1},{3,2},{4,7},{5,4},{6,5},{7,6},{8,11},{9,8},{10,9... | collective-permute-start | bytes 921608 | tf_op jit(solution)/shard_map/ppermute | solution.py:22
  33.0 6.7 %collective-permute-start.18 = (bf16[80,512]{1,0:T(8,128)(2,1)S(1)}, bf16[80,512]{1,0:T(8,128)(2,1)S(1)}, u32[]{:S(2)}, u32[]{:S(2)}) collective-permute-start(bf16[80,512]{1,0:T(8,128)(2,1)S(1)} %get-tuple-element.63), channel_id=1, source_target_pairs={{0,4},{4,8},{8,12},{12,16},{16,20},{20,24},{24,28},{28,32},{32,36}... | collective-permute-start | bytes 245768 | tf_op jit(solution)/shard_map/ppermute | solution.py:22
  39.7 3.0 %collective-permute-done.14.rest_3_ = bf16[200,768]{1,0:T(8,128)(2,1)S(1)} collective-permute-done((bf16[200,768]{1,0:T(8,128)(2,1)S(1)}, bf16[200,768]{1,0:T(8,128)(2,1)S(1)}, u32[]{:S(2)}, u32[]{:S(2)}) %collective-permute-start.14) | collective-permute-done | bytes 307232 | tf_op jit(solution)/shard_map/ppermute | solution.py:22
  42.7 5.5 %collective-permute-start.19 = (bf16[80,512]{1,0:T(8,128)(2,1)S(1)}, bf16[80,512]{1,0:T(8,128)(2,1)S(1)}, u32[]{:S(2)}, u32[]{:S(2)}) collective-permute-start(bf16[80,512]{1,0:T(8,128)(2,1)S(1)} %get-tuple-element.64), channel_id=1, source_target_pairs={{0,124},{4,0},{8,4},{12,8},{16,12},{20,16},{24,20},{28,24},{32,28}... | collective-permute-start | bytes 245768 | tf_op jit(solution)/shard_map/ppermute | solution.py:22
  48.3 2.3 %one_hots.1 = (bf16[2,256,4096]{2,1,0:T(8,128)(2,1)S(1)}, bf16[2,4096,256]{2,1,0:T(8,128)(2,1)S(1)}, s32[4,4096]{1,0:T(4,128)S(1)}) custom-call(s32[1,8320]{1,0:T(1,128)S(1)} %collective-permute-done.20.down_ref, s32[1,4096]{1,0:T(1,128)S(1)} %copy-done.4, s32[1,4096]{1,0:T(1,128)S(1)} %copy-done.3, s32[1,1]{1,0:T(1,128)} %bitcast.9.count_ref), custom_call_target="tpu_custom_call" | custom-call | flops 41943040 | bytes 8388608 | tf_op jit(solution)/shard_map/one_hots/pallas_call | solution.py:234
  50.7 1.0 %mix.5 = (bf16[80,768]{1,0:T(8,128)(2,1)S(1)}, bf16[80,768]{1,0:T(8,128)(2,1)S(1)}, bf16[80,768]{1,0:T(8,128)(2,1)S(1)}, bf16[80,768]{1,0:T(8,128)(2,1)S(1)}) custom-call(bf16[4,320,200]{2,1,0:T(8,128)(2,1)S(1)} %spread.1.l_ref, bf16[200,768]{1,0:T(8,128)(2,1)S(1)} %kept.3.rest_0_, bf16[200,768]{1,0:T(8,128)(2,1)S(1)} %collective-permute-done.12.rest_1_, ...), custom_call_target="tpu_custom_call" | custom-call | flops 393216000 | bytes 1720320 | tf_op jit(solution)/shard_map/mix/pallas_call | solution.py:185
  51.7 1.7 %collective-permute-start.15 = (bf16[80,768]{1,0:T(8,128)(2,1)S(1)}, bf16[80,768]{1,0:T(8,128)(2,1)S(1)}, u32[]{:S(2)}, u32[]{:S(2)}) collective-permute-start(bf16[80,768]{1,0:T(8,128)(2,1)S(1)} %get-tuple-element.60), channel_id=1, source_target_pairs={{0,1},{1,2},{2,3},{3,0},{4,5},{5,6},{6,7},{7,4},{8,9},{9,10},{10,1... | collective-permute-start | bytes 368648 | tf_op jit(solution)/shard_map/ppermute | solution.py:22
  53.4 2.2 %collective-permute-start.16 = (bf16[80,768]{1,0:T(8,128)(2,1)S(1)}, bf16[80,768]{1,0:T(8,128)(2,1)S(1)}, u32[]{:S(2)}, u32[]{:S(2)}) collective-permute-start(bf16[80,768]{1,0:T(8,128)(2,1)S(1)} %get-tuple-element.61), channel_id=1, source_target_pairs={{0,2},{1,3},{2,0},{3,1},{4,6},{5,7},{6,4},{7,5},{8,10},{9,11},{10,... | collective-permute-start | bytes 368648 | tf_op jit(solution)/shard_map/ppermute | solution.py:22
  55.6 1.2 %collective-permute-start.17 = (bf16[80,768]{1,0:T(8,128)(2,1)S(1)}, bf16[80,768]{1,0:T(8,128)(2,1)S(1)}, u32[]{:S(2)}, u32[]{:S(2)}) collective-permute-start(bf16[80,768]{1,0:T(8,128)(2,1)S(1)} %get-tuple-element.62), channel_id=1, source_target_pairs={{0,3},{1,0},{2,1},{3,2},{4,7},{5,4},{6,5},{7,6},{8,11},{9,8},{10,9... | collective-permute-start | bytes 368648 | tf_op jit(solution)/shard_map/ppermute | solution.py:22
  56.8 1.0 %mix.3 = (bf16[80,768]{1,0:T(8,128)(2,1)S(1)}, bf16[80,768]{1,0:T(8,128)(2,1)S(1)}, bf16[80,768]{1,0:T(8,128)(2,1)S(1)}, bf16[80,768]{1,0:T(8,128)(2,1)S(1)}) custom-call(bf16[4,320,200]{2,1,0:T(8,128)(2,1)S(1)} %spread.1.l_ref, bf16[200,768]{1,0:T(8,128)(2,1)S(1)} %kept.2.rest_0_, bf16[200,768]{1,0:T(8,128)(2,1)S(1)} %collective-permute-done.rest_1_, ...), custom_call_target="tpu_custom_call" | custom-call | flops 393216000 | bytes 1720320 | tf_op jit(solution)/shard_map/mix/pallas_call | solution.py:185
  58.2 0.9 %collective-permute-start.4 = (bf16[80,768]{1,0:T(8,128)(2,1)S(1)}, bf16[80,768]{1,0:T(8,128)(2,1)S(1)}, u32[]{:S(2)}, u32[]{:S(2)}) collective-permute-start(bf16[80,768]{1,0:T(8,128)(2,1)S(1)} %get-tuple-element.45), channel_id=1, source_target_pairs={{0,2},{1,3},{2,0},{3,1},{4,6},{5,7},{6,4},{7,5},{8,10},{9,11},{10,... | collective-permute-start | bytes 368648 | tf_op jit(solution)/shard_map/ppermute | solution.py:22
  59.1 1.9 %links.1.rest_8_ = f32[64,16,128]{2,1,0:T(8,128)S(1)} custom-call(bf16[80,512]{1,0:T(8,128)(2,1)S(1)} %collective-permute-done.18.below_ref, bf16[80,512]{1,0:T(8,128)(2,1)S(1)} %collective-permute-done.19.above_ref, bf16[2,256,4096]{2,1,0:T(8,128)(2,1)S(1)} %get-tuple-element.65.g_ref, bf16[2,4096,256]{2,1,0:T(8,128)(2,1)S(1)} %get-tuple-element.66.s_ref, ...), custom_call_target="tpu_custom_call" | custom-call | flops 1342177280 | bytes 327680 | tf_op jit(solution)/shard_map/links/pallas_call | solution.py:296
  61.0 1.8 %collective-permute-start.5 = (bf16[80,768]{1,0:T(8,128)(2,1)S(1)}, bf16[80,768]{1,0:T(8,128)(2,1)S(1)}, u32[]{:S(2)}, u32[]{:S(2)}) collective-permute-start(bf16[80,768]{1,0:T(8,128)(2,1)S(1)} %get-tuple-element.46), channel_id=1, source_target_pairs={{0,3},{1,0},{2,1},{3,2},{4,7},{5,4},{6,5},{7,6},{8,11},{9,8},{10,9... | collective-permute-start | bytes 368648 | tf_op jit(solution)/shard_map/ppermute | solution.py:22
  62.9 3.7 %part_one.1 = (bf16[10,65536]{1,0:T(8,128)(2,1)}, bf16[10,65536]{1,0:T(8,128)(2,1)}, f32[128,16,128]{2,1,0:T(8,128)S(1)}, f32[2,16,128]{2,1,0:T(8,128)S(1)}) custom-call(s32[1]{0:T(128)} %bitcast.me_ref, bf16[80,512]{1,0:T(8,128)(2,1)S(1)} %get-tuple-element.51.rest_0_, bf16[80,512]{1,0:T(8,128)(2,1)S(1)} %collective-permute-done.9.rest_1_, ...), custom_call_target="tpu_custom_call" | custom-call | flops 2097152000 | bytes 4194304 | tf_op jit(solution)/shard_map/part_one/pallas_call | solution.py:515
  66.6 3.6 %part_two.1 = (bf16[10,65536]{1,0:T(8,128)(2,1)}, bf16[10,65536]{1,0:T(8,128)(2,1)}, f32[32,1,128]{2,1,0:T(1,128)S(1)}) custom-call(s32[1]{0:T(128)} %bitcast.me_ref, bf16[80,768]{1,0:T(8,128)(2,1)S(1)} %get-tuple-element.43.rest_0_, bf16[80,768]{1,0:T(8,128)(2,1)S(1)} %collective-permute-done.3.rest_1_, ...), custom_call_target="tpu_custom_call", output_to_operand_aliasing={{0}: (11, {}), {1}: (12, {})} | custom-call | flops 2097152000 | bytes 4194304 | tf_op jit(solution)/shard_map/part_two/pallas_call | solution.py:537
  70.3 19.1 %all_to_all.5 = f32[32,1,128]{2,1,0:T(1,128)S(1)} all-to-all(f32[32,1,128]{2,1,0:T(1,128)S(1)} %get-tuple-element.74), channel_id=1, replica_groups=mesh['rows'=32,'vecs'=4] {'rows'}, dimensions={0} | all-to-all | bytes 32768 | tf_op jit(solution)/shard_map/all_to_all | solution.py:622
  (59 shorter events, 2.1 us)
Async XLA Ops:
  2.8 11.3 %collective-permute-start.6 = (bf16[200,512]{1,0:T(8,128)(2,1)}, bf16[200,512]{1,0:T(8,128)(2,1)S(1)}, u32[]{:S(2)}, u32[]{:S(2)}) collective-permute-start(bf16[200,512]{1,0:T(8,128)(2,1)} %get-tuple-element.48), channel_id=1, source_target_pairs={{0,1},{1,2},{2,3},{3,0},{4,5},{5,6},{6,7},{7,4},{8,9},{9,10},{10,1... | collective-permute-start | bytes 614408 | tf_op jit(solution)/shard_map/ppermute | solution.py:22
  4.9 11.5 %collective-permute-start.7 = (bf16[200,512]{1,0:T(8,128)(2,1)}, bf16[200,512]{1,0:T(8,128)(2,1)S(1)}, u32[]{:S(2)}, u32[]{:S(2)}) collective-permute-start(bf16[200,512]{1,0:T(8,128)(2,1)} %get-tuple-element.49), channel_id=1, source_target_pairs={{0,2},{1,3},{2,0},{3,1},{4,6},{5,7},{6,4},{7,5},{8,10},{9,11},{10,... | collective-permute-start | bytes 614408 | tf_op jit(solution)/shard_map/ppermute | solution.py:22
  7.3 5.9 %copy-start.5 = (bf16[100,40]{0,1:T(8,128)(2,1)S(1)}, bf16[100,40]{0,1:T(8,128)(2,1)}, u32[]{:S(2)}) copy-start(bf16[100,40]{0,1:T(8,128)(2,1)} %param.10) | copy-start | bytes 24004
  7.3 9.1 %copy-start.2 = (bf16[200,512]{1,0:T(8,128)(2,1)S(1)}, bf16[200,512]{1,0:T(8,128)(2,1)}, u32[]{:S(2)}) copy-start(bf16[200,512]{1,0:T(8,128)(2,1)} %get-tuple-element.47.rest_0_) | copy-start | bytes 614404
  7.3 9.1 %collective-permute-start.8 = (bf16[200,512]{1,0:T(8,128)(2,1)}, bf16[200,512]{1,0:T(8,128)(2,1)S(1)}, u32[]{:S(2)}, u32[]{:S(2)}) collective-permute-start(bf16[200,512]{1,0:T(8,128)(2,1)} %get-tuple-element.50), channel_id=1, source_target_pairs={{0,3},{1,0},{2,1},{3,2},{4,7},{5,4},{6,5},{7,6},{8,11},{9,8},{10,9... | collective-permute-start | bytes 614408 | tf_op jit(solution)/shard_map/ppermute | solution.py:22
  11.9 8.9 %copy-start.3 = (s32[1,4096]{1,0:T(1,128)S(1)}, s32[1,4096]{1,0:T(1,128)}, u32[]{:S(2)}) copy-start(s32[1,4096]{1,0:T(1,128)} %upper_ref.1) | copy-start | bytes 49156
  11.9 8.9 %copy-start.4 = (s32[1,4096]{1,0:T(1,128)S(1)}, s32[1,4096]{1,0:T(1,128)}, u32[]{:S(2)}) copy-start(s32[1,4096]{1,0:T(1,128)} %lower_ref.1) | copy-start | bytes 49156
  11.9 13.8 %copy-start.14 = (bf16[200,768]{1,0:T(8,128)(2,1)S(1)}, bf16[200,768]{1,0:T(8,128)(2,1)}, u32[]{:S(2)}) copy-start(bf16[200,768]{1,0:T(8,128)(2,1)} %get-tuple-element.57) | copy-start | bytes 921604
  11.9 15.6 %copy-start.13 = (bf16[200,768]{1,0:T(8,128)(2,1)S(1)}, bf16[200,768]{1,0:T(8,128)(2,1)}, u32[]{:S(2)}) copy-start(bf16[200,768]{1,0:T(8,128)(2,1)} %get-tuple-element.58) | copy-start | bytes 921604
  11.9 16.4 %copy-start.12 = (bf16[200,768]{1,0:T(8,128)(2,1)S(1)}, bf16[200,768]{1,0:T(8,128)(2,1)}, u32[]{:S(2)}) copy-start(bf16[200,768]{1,0:T(8,128)(2,1)} %get-tuple-element.40) | copy-start | bytes 921604
  11.9 17.0 %copy-start.11 = (bf16[200,768]{1,0:T(8,128)(2,1)S(1)}, bf16[200,768]{1,0:T(8,128)(2,1)}, u32[]{:S(2)}) copy-start(bf16[200,768]{1,0:T(8,128)(2,1)} %get-tuple-element.41) | copy-start | bytes 921604
  11.9 18.6 %copy-start.10 = (bf16[200,768]{1,0:T(8,128)(2,1)S(1)}, bf16[200,768]{1,0:T(8,128)(2,1)}, u32[]{:S(2)}) copy-start(bf16[200,768]{1,0:T(8,128)(2,1)} %get-tuple-element.42) | copy-start | bytes 921604
  11.9 36.3 %copy-start.1 = (bf16[200,768]{1,0:T(8,128)(2,1)S(1)}, bf16[200,768]{1,0:T(8,128)(2,1)}, u32[]{:S(2)}) copy-start(bf16[200,768]{1,0:T(8,128)(2,1)} %get-tuple-element.55.from_ref) | copy-start | bytes 921604
  11.9 36.3 %copy-start = (bf16[200,768]{1,0:T(8,128)(2,1)S(1)}, bf16[200,768]{1,0:T(8,128)(2,1)}, u32[]{:S(2)}) copy-start(bf16[200,768]{1,0:T(8,128)(2,1)} %get-tuple-element.39.from_ref) | copy-start | bytes 921604
  12.0 18.5 %collective-permute-start.12 = (bf16[200,768]{1,0:T(8,128)(2,1)}, bf16[200,768]{1,0:T(8,128)(2,1)S(1)}, u32[]{:S(2)}, u32[]{:S(2)}) collective-permute-start(bf16[200,768]{1,0:T(8,128)(2,1)} %get-tuple-element.56), channel_id=1, source_target_pairs={{0,1},{1,2},{2,3},{3,0},{4,5},{5,6},{6,7},{7,4},{8,9},{9,10},{10,1... | collective-permute-start | bytes 921608 | tf_op jit(solution)/shard_map/ppermute | solution.py:22
  17.1 10.3 %collective-permute-start.10 = (bf16[80,512]{1,0:T(8,128)(2,1)S(1)}, bf16[80,512]{1,0:T(8,128)(2,1)S(1)}, u32[]{:S(2)}, u32[]{:S(2)}) collective-permute-start(bf16[80,512]{1,0:T(8,128)(2,1)S(1)} %get-tuple-element.53), channel_id=1, source_target_pairs={{0,2},{1,3},{2,0},{3,1},{4,6},{5,7},{6,4},{7,5},{8,10},{9,11},{10,... | collective-permute-start | bytes 245768 | tf_op jit(solution)/shard_map/ppermute | solution.py:22
  19.3 9.0 %collective-permute-start.11 = (bf16[80,512]{1,0:T(8,128)(2,1)S(1)}, bf16[80,512]{1,0:T(8,128)(2,1)S(1)}, u32[]{:S(2)}, u32[]{:S(2)}) collective-permute-start(bf16[80,512]{1,0:T(8,128)(2,1)S(1)} %get-tuple-element.54), channel_id=1, source_target_pairs={{0,3},{1,0},{2,1},{3,2},{4,7},{5,4},{6,5},{7,6},{8,11},{9,8},{10,9... | collective-permute-start | bytes 245768 | tf_op jit(solution)/shard_map/ppermute | solution.py:22
  20.8 8.1 %collective-permute-start.9 = (bf16[80,512]{1,0:T(8,128)(2,1)S(1)}, bf16[80,512]{1,0:T(8,128)(2,1)S(1)}, u32[]{:S(2)}, u32[]{:S(2)}) collective-permute-start(bf16[80,512]{1,0:T(8,128)(2,1)S(1)} %get-tuple-element.52), channel_id=1, source_target_pairs={{0,1},{1,2},{2,3},{3,0},{4,5},{5,6},{6,7},{7,4},{8,9},{9,10},{10,1... | collective-permute-start | bytes 245768 | tf_op jit(solution)/shard_map/ppermute | solution.py:22
  20.8 4.9 %collective-permute-start.20 = (s32[1,8320]{1,0:T(1,128)S(1)}, s32[1,8320]{1,0:T(1,128)S(1)}, u32[]{:S(2)}, u32[]{:S(2)}) collective-permute-start(s32[1,8320]{1,0:T(1,128)S(1)} %reshape_add_fusion), channel_id=1, source_target_pairs={{0,4},{4,8},{8,12},{12,16},{16,20},{20,24},{24,28},{28,32},{32,36}... | collective-permute-start | bytes 99848 | tf_op jit(solution)/shard_map/ppermute | solution.py:22
  25.7 7.3 %collective-permute-start.13 = (bf16[200,768]{1,0:T(8,128)(2,1)S(1)}, bf16[200,768]{1,0:T(8,128)(2,1)S(1)}, u32[]{:S(2)}, u32[]{:S(2)}) collective-permute-start(bf16[200,768]{1,0:T(8,128)(2,1)S(1)} %copy-done.14), channel_id=1, source_target_pairs={{0,2},{1,3},{2,0},{3,1},{4,6},{5,7},{6,4},{7,5},{8,10},{9,11},{10,... | collective-permute-start | bytes 921608 | tf_op jit(solution)/shard_map/ppermute | solution.py:22
  27.5 15.3 %collective-permute-start.14 = (bf16[200,768]{1,0:T(8,128)(2,1)S(1)}, bf16[200,768]{1,0:T(8,128)(2,1)S(1)}, u32[]{:S(2)}, u32[]{:S(2)}) collective-permute-start(bf16[200,768]{1,0:T(8,128)(2,1)S(1)} %copy-done.13), channel_id=1, source_target_pairs={{0,3},{1,0},{2,1},{3,2},{4,7},{5,4},{6,5},{7,6},{8,11},{9,8},{10,9... | collective-permute-start | bytes 921608 | tf_op jit(solution)/shard_map/ppermute | solution.py:22
  28.3 23.3 %collective-permute-start = (bf16[200,768]{1,0:T(8,128)(2,1)S(1)}, bf16[200,768]{1,0:T(8,128)(2,1)S(1)}, u32[]{:S(2)}, u32[]{:S(2)}) collective-permute-start(bf16[200,768]{1,0:T(8,128)(2,1)S(1)} %copy-done.12), channel_id=1, source_target_pairs={{0,1},{1,2},{2,3},{3,0},{4,5},{5,6},{6,7},{7,4},{8,9},{9,10},{10,1... | collective-permute-start | bytes 921608 | tf_op jit(solution)/shard_map/ppermute | solution.py:22
  28.9 24.5 %collective-permute-start.1 = (bf16[200,768]{1,0:T(8,128)(2,1)S(1)}, bf16[200,768]{1,0:T(8,128)(2,1)S(1)}, u32[]{:S(2)}, u32[]{:S(2)}) collective-permute-start(bf16[200,768]{1,0:T(8,128)(2,1)S(1)} %copy-done.11), channel_id=1, source_target_pairs={{0,2},{1,3},{2,0},{3,1},{4,6},{5,7},{6,4},{7,5},{8,10},{9,11},{10,... | collective-permute-start | bytes 921608 | tf_op jit(solution)/shard_map/ppermute | solution.py:22
  30.5 25.1 %collective-permute-start.2 = (bf16[200,768]{1,0:T(8,128)(2,1)S(1)}, bf16[200,768]{1,0:T(8,128)(2,1)S(1)}, u32[]{:S(2)}, u32[]{:S(2)}) collective-permute-start(bf16[200,768]{1,0:T(8,128)(2,1)S(1)} %copy-done.10), channel_id=1, source_target_pairs={{0,3},{1,0},{2,1},{3,2},{4,7},{5,4},{6,5},{7,6},{8,11},{9,8},{10,9... | collective-permute-start | bytes 921608 | tf_op jit(solution)/shard_map/ppermute | solution.py:22
  33.0 24.8 %collective-permute-start.18 = (bf16[80,512]{1,0:T(8,128)(2,1)S(1)}, bf16[80,512]{1,0:T(8,128)(2,1)S(1)}, u32[]{:S(2)}, u32[]{:S(2)}) collective-permute-start(bf16[80,512]{1,0:T(8,128)(2,1)S(1)} %get-tuple-element.63), channel_id=1, source_target_pairs={{0,4},{4,8},{8,12},{12,16},{16,20},{20,24},{24,28},{28,32},{32,36}... | collective-permute-start | bytes 245768 | tf_op jit(solution)/shard_map/ppermute | solution.py:22
  42.7 15.5 %collective-permute-start.19 = (bf16[80,512]{1,0:T(8,128)(2,1)S(1)}, bf16[80,512]{1,0:T(8,128)(2,1)S(1)}, u32[]{:S(2)}, u32[]{:S(2)}) collective-permute-start(bf16[80,512]{1,0:T(8,128)(2,1)S(1)} %get-tuple-element.64), channel_id=1, source_target_pairs={{0,124},{4,0},{8,4},{12,8},{16,12},{20,16},{24,20},{28,24},{32,28}... | collective-permute-start | bytes 245768 | tf_op jit(solution)/shard_map/ppermute | solution.py:22
  51.7 9.4 %collective-permute-start.15 = (bf16[80,768]{1,0:T(8,128)(2,1)S(1)}, bf16[80,768]{1,0:T(8,128)(2,1)S(1)}, u32[]{:S(2)}, u32[]{:S(2)}) collective-permute-start(bf16[80,768]{1,0:T(8,128)(2,1)S(1)} %get-tuple-element.60), channel_id=1, source_target_pairs={{0,1},{1,2},{2,3},{3,0},{4,5},{5,6},{6,7},{7,4},{8,9},{9,10},{10,1... | collective-permute-start | bytes 368648 | tf_op jit(solution)/shard_map/ppermute | solution.py:22
  53.4 9.5 %collective-permute-start.16 = (bf16[80,768]{1,0:T(8,128)(2,1)S(1)}, bf16[80,768]{1,0:T(8,128)(2,1)S(1)}, u32[]{:S(2)}, u32[]{:S(2)}) collective-permute-start(bf16[80,768]{1,0:T(8,128)(2,1)S(1)} %get-tuple-element.61), channel_id=1, source_target_pairs={{0,2},{1,3},{2,0},{3,1},{4,6},{5,7},{6,4},{7,5},{8,10},{9,11},{10,... | collective-permute-start | bytes 368648 | tf_op jit(solution)/shard_map/ppermute | solution.py:22
  55.6 7.2 %collective-permute-start.17 = (bf16[80,768]{1,0:T(8,128)(2,1)S(1)}, bf16[80,768]{1,0:T(8,128)(2,1)S(1)}, u32[]{:S(2)}, u32[]{:S(2)}) collective-permute-start(bf16[80,768]{1,0:T(8,128)(2,1)S(1)} %get-tuple-element.62), channel_id=1, source_target_pairs={{0,3},{1,0},{2,1},{3,2},{4,7},{5,4},{6,5},{7,6},{8,11},{9,8},{10,9... | collective-permute-start | bytes 368648 | tf_op jit(solution)/shard_map/ppermute | solution.py:22
  57.8 8.8 %collective-permute-start.3 = (bf16[80,768]{1,0:T(8,128)(2,1)S(1)}, bf16[80,768]{1,0:T(8,128)(2,1)S(1)}, u32[]{:S(2)}, u32[]{:S(2)}) collective-permute-start(bf16[80,768]{1,0:T(8,128)(2,1)S(1)} %get-tuple-element.44), channel_id=1, source_target_pairs={{0,1},{1,2},{2,3},{3,0},{4,5},{5,6},{6,7},{7,4},{8,9},{9,10},{10,1... | collective-permute-start | bytes 368648 | tf_op jit(solution)/shard_map/ppermute | solution.py:22
  58.2 8.4 %collective-permute-start.4 = (bf16[80,768]{1,0:T(8,128)(2,1)S(1)}, bf16[80,768]{1,0:T(8,128)(2,1)S(1)}, u32[]{:S(2)}, u32[]{:S(2)}) collective-permute-start(bf16[80,768]{1,0:T(8,128)(2,1)S(1)} %get-tuple-element.45), channel_id=1, source_target_pairs={{0,2},{1,3},{2,0},{3,1},{4,6},{5,7},{6,4},{7,5},{8,10},{9,11},{10,... | collective-permute-start | bytes 368648 | tf_op jit(solution)/shard_map/ppermute | solution.py:22
  61.0 5.6 %collective-permute-start.5 = (bf16[80,768]{1,0:T(8,128)(2,1)S(1)}, bf16[80,768]{1,0:T(8,128)(2,1)S(1)}, u32[]{:S(2)}, u32[]{:S(2)}) collective-permute-start(bf16[80,768]{1,0:T(8,128)(2,1)S(1)} %get-tuple-element.46), channel_id=1, source_target_pairs={{0,3},{1,0},{2,1},{3,2},{4,7},{5,4},{6,5},{7,6},{8,11},{9,8},{10,9... | collective-permute-start | bytes 368648 | tf_op jit(solution)/shard_map/ppermute | solution.py:22
  (4 other events, 15.1 us)

commit v4 on v3

--- a/solution.py
+++ b/solution.py
@@ -49,27 +49,42 @@
 
 
 class Packing:
-    def __init__(self, chunk, parts, me, basis_ref, outs, buf, sem):
-        self.chunk, self.outs, self.buf, self.reads = chunk, outs, buf, []
+    def __init__(self, chunk, parts, me, basis_ref, outs, buf, laid, sem):
+        self.chunk, self.buf, self.laid, self.reads = chunk, buf, laid, []
+        self.turns = [*range(1, parts), 0]
+        self.writes = [
+            pltpu.make_async_copy(laid.at[k], outs[k], sem.at[1, k]) for k in range(parts)
+        ]
         for k in range(parts):
             st = pl.multiple_of(chunk.start(lax.rem(me + k, parts)), LANES)
-            read = pltpu.make_async_copy(
-                basis_ref.at[:, pl.ds(st, chunk.width)], buf.at[k], sem.at[k]
+            self.reads.append(
+                pltpu.make_async_copy(
+                    basis_ref.at[:, pl.ds(st, chunk.width)], buf.at[k], sem.at[0, k]
+                )
             )
-            read.start()
-            self.reads.append(read)
+        for k in self.turns:
+            self.reads[k].start()
 
     def finish(self):
         ranks, seg = self.buf.shape[1], self.chunk.seg
         full = ranks // 8 * 8
-        for read, out, k in zip(self.reads, self.outs, range(len(self.outs))):
-            read.wait()
+        before = None
+        for k in self.turns:
+            self.reads[k].wait()
             tail = []
             for c in range(SEGS):
                 cut = slice(c * seg, (c + 1) * seg)
-                out[c * full : (c + 1) * full, :] = self.buf[k, 0:full, cut]
+                self.laid[k, c * full : (c + 1) * full, :] = self.buf[k, 0:full, cut]
                 tail.append(self.buf[k, full:ranks, cut])
-            out[SEGS * full : SEGS * ranks, :] = jnp.concatenate(tail, axis=0)
+            self.laid[k, SEGS * full : SEGS * ranks, :] = jnp.concatenate(tail, axis=0)
+            if before is not None:
+                self.writes[before].start()
+            before = k
+        self.writes[before].start()
+
+    def wait(self):
+        for write in self.writes:
+            write.wait()
 
 
 def packed_shape(chunk, ranks):
@@ -77,7 +92,11 @@
 
 
 def pack_scratch(chunk, ranks, parts):
-    return [pltpu.VMEM((parts, ranks, chunk.width), BF), pltpu.SemaphoreType.DMA((parts,))]
+    return [
+        pltpu.VMEM((parts, ranks, chunk.width), BF),
+        pltpu.VMEM((parts, SEGS * ranks, chunk.seg), BF),
+        pltpu.SemaphoreType.DMA((2, parts)),
+    ]
 
 
 def pack_kernel(chunks, parts, me_ref, basis_ref, *rest):
@@ -86,12 +105,14 @@
     work = [
         Packing(
             chunk, parts, me_ref[0], basis_ref, outs[i * parts : (i + 1) * parts],
-            *scratch[2 * i : 2 * i + 2]
+            *scratch[3 * i : 3 * i + 3]
         )
         for i, chunk in enumerate(chunks)
     ]
     for w in work:
         w.finish()
+    for w in work:
+        w.wait()
 
 
 def pack(me, basis, chunks, parts):
@@ -104,7 +125,7 @@
         functools.partial(pack_kernel, chunks, parts),
         out_shape=shapes,
         in_specs=[SMEM, ANY],
-        out_specs=[VMEM] * len(shapes),
+        out_specs=[ANY] * len(shapes),
         scratch_shapes=scratch,
         compiler_params=params(60),
         cost_estimate=cost(1, 4 * parts * ranks * sum(chunk.width for chunk in chunks)),
@@ -368,7 +389,7 @@
             copy.wait()
 
 
-def cuts(low, high, step=3):
+def cuts(low, high, step):
     marks = list(range(low, high, step))
     return list(zip(marks, marks[1:] + [high]))
 
@@ -428,12 +449,12 @@
     return vsum, rsum
 
 
-def finished_planes(terms, cells, z0, carry, links, outs, out, low, high, ends):
+def finished_planes(terms, cells, z0, carry, links, outs, out, low, high, ends, step):
     ready = []
     for z in ends:
         carry = one_plane(terms, cells, z, z0, carry, links.get(z), outs(z))
         ready.append((z, z + 1))
-    for first, end in cuts(low, high):
+    for first, end in cuts(low, high, step):
         carry = lax.fori_loop(
             first, end, lambda z, c: one_plane(terms, cells, z, z0, c, None, outs(first)), carry
         )
@@ -459,7 +480,7 @@
     zero = jnp.zeros((NP, LANES), F32)
     links = {0: (link_ref, 0, 1), planes - 1: (link_ref, tiles, -1)}
     carry, ready = finished_planes(
-        terms, cells, 0, (zero, zero), links, outs, out, 1, split, (0, planes - 1)
+        terms, cells, 0, (zero, zero), links, outs, out, 1, split, (0, planes - 1), 3
     )
     edge_ref[0 : 2 * tiles] = cells[(split - 1) * tiles : (split + 1) * tiles]
     edge_ref[2 * tiles : 4 * tiles] = cells[(planes - 2) * tiles : planes * tiles]
@@ -483,7 +504,7 @@
     outs = lambda z: (vec_buf, res_buf, split * WID * WID)
     out = Output((vec_ref, res_ref), (vec_buf, res_buf), sem, {None: split})
     carry = (early_ref[0], early_ref[1])
-    carry, ready = finished_planes(terms, cells, z0, carry, {}, outs, out, split, planes - 1, ())
+    carry, ready = finished_planes(terms, cells, z0, carry, {}, outs, out, split, planes - 1, (), 1)
     vsum, rsum = carry
     vrow = jnp.broadcast_to(jnp.sum(vsum, axis=1, keepdims=True), (NP, LANES))
     rrow = jnp.broadcast_to(jnp.sum(rsum, axis=1, keepdims=True), (NP, LANES))

time: 90.2 us -> 89.4 us (level)
  Pallas kernels: 20.7 us -> 19.6 us
  transfers between devices with their start and end apart: 21 -> 21, of which waited for: 4 -> 4; matrix products, arithmetic and copies ran while one was open for 0% -> 0% of each run, Pallas kernels for 17% -> 16%
where the time goes in v4:
time: 89.4 us; the launch traced here: 89.2 us
  starting transfers between devices  40.8 us (46%)
  Pallas kernels  19.6 us (22%)
  blocking collectives  19.1 us (21%)
  waiting for transfers between devices  7.12 us (8%)
  between operations  1.81 us (2%)
    ppermute x21, starting transfers between devices, from_behind(): return lax.ppermute(value, axis, pairs)  40.8 us
    all_to_all x1, blocking collectives, on_device(): total = lax.all_to_all(sums, 'rows', 0, 0, tiled=True).sum(axis=(0, 1))  19.1 us
    ppermute x21, waiting for transfers between devices, from_behind(): return lax.ppermute(value, axis, pairs)  7.12 us
    pallas_call x2, Pallas kernels, pack(): pl.pallas_call(functools.partial(pack_kernel, chunks, parts), out_shape=s...  5.2 us
    pallas_call x1, Pallas kernels, part_one(): pl.pallas_call(functools.partial(part_one_kernel, chunks, parts, planes,...  3.68 us
    pallas_call x1, Pallas kernels, part_two(): pl.pallas_call(functools.partial(part_two_kernel, chunk, parts, planes, s...  2.85 us
    pallas_call x3, Pallas kernels, mix(): pl.pallas_call(functools.partial(mix_kernel, parts, lane, seg), out_shape...  2.65 us
    pallas_call x1, Pallas kernels, one_hots(): pl.pallas_call(functools.partial(one_hot_kernel, low), out_shape=(hot, ho...  2.34 us
  transfers between devices with their start and end apart: 21, of which 4 were waited for; matrix products, arithmetic and copies ran while one was open for 0% of the time, Pallas kernels for 16%

profile of v4, /device:TPU:1, one launch (start us, length us, event | category | flops | bytes accessed | tf_op | source)
XLA Modules:
  0.0 89.2 jit_solution(9062849413614218212)
XLA Ops:
  0.6 2.1 %pack.3 = (bf16[200,512]{1,0:T(8,128)(2,1)}, bf16[200,512]{1,0:T(8,128)(2,1)}, bf16[200,512]{1,0:T(8,128)(2,1)}, bf16[200,512]{1,0:T(8,128)(2,1)}) custom-call(s32[1]{0:T(128)} %bitcast.me_ref, bf16[25,65536]{1,0:T(8,128)(2,1)} %basis_ref.3), custom_call_target="tpu_custom_call" | custom-call | flops 1 | bytes 1638400 | tf_op jit(solution)/shard_map/pack/pallas_call | solution.py:124
  2.7 2.1 %collective-permute-start.6 = (bf16[200,512]{1,0:T(8,128)(2,1)}, bf16[200,512]{1,0:T(8,128)(2,1)S(1)}, u32[]{:S(2)}, u32[]{:S(2)}) collective-permute-start(bf16[200,512]{1,0:T(8,128)(2,1)} %get-tuple-element.48), channel_id=1, source_target_pairs={{0,1},{1,2},{2,3},{3,0},{4,5},{5,6},{6,7},{7,4},{8,9},{9,10},{10,1... | collective-permute-start | bytes 614408 | tf_op jit(solution)/shard_map/ppermute | solution.py:22
  4.8 2.5 %collective-permute-start.7 = (bf16[200,512]{1,0:T(8,128)(2,1)}, bf16[200,512]{1,0:T(8,128)(2,1)S(1)}, u32[]{:S(2)}, u32[]{:S(2)}) collective-permute-start(bf16[200,512]{1,0:T(8,128)(2,1)} %get-tuple-element.49), channel_id=1, source_target_pairs={{0,2},{1,3},{2,0},{3,1},{4,6},{5,7},{6,4},{7,5},{8,10},{9,11},{10,... | collective-permute-start | bytes 614408 | tf_op jit(solution)/shard_map/ppermute | solution.py:22
  7.3 1.2 %collective-permute-start.8 = (bf16[200,512]{1,0:T(8,128)(2,1)}, bf16[200,512]{1,0:T(8,128)(2,1)S(1)}, u32[]{:S(2)}, u32[]{:S(2)}) collective-permute-start(bf16[200,512]{1,0:T(8,128)(2,1)} %get-tuple-element.50), channel_id=1, source_target_pairs={{0,3},{1,0},{2,1},{3,2},{4,7},{5,4},{6,5},{7,6},{8,11},{9,8},{10,9... | collective-permute-start | bytes 614408 | tf_op jit(solution)/shard_map/ppermute | solution.py:22
  8.4 3.1 %pack.2 = (bf16[200,768]{1,0:T(8,128)(2,1)}, bf16[200,768]{1,0:T(8,128)(2,1)}, bf16[200,768]{1,0:T(8,128)(2,1)}, bf16[200,768]{1,0:T(8,128)(2,1)}, bf16[200,768]...) custom-call(s32[1]{0:T(128)} %bitcast.me_ref, ...), custom_call_target="tpu_custom_call" | custom-call | flops 1 | bytes 4915200 | tf_op jit(solution)/shard_map/pack/pallas_call | solution.py:124
  12.9 0.9 spread.1.l_ref
  13.8 2.6 %collective-permute-done.7.rest_2_ = bf16[200,512]{1,0:T(8,128)(2,1)S(1)} collective-permute-done((bf16[200,512]{1,0:T(8,128)(2,1)}, bf16[200,512]{1,0:T(8,128)(2,1)S(1)}, u32[]{:S(2)}, u32[]{:S(2)}) %collective-permute-start.7) | collective-permute-done | bytes 204832 | tf_op jit(solution)/shard_map/ppermute | solution.py:22
  16.4 0.7 mix.4
  17.0 2.2 %collective-permute-start.10 = (bf16[80,512]{1,0:T(8,128)(2,1)S(1)}, bf16[80,512]{1,0:T(8,128)(2,1)S(1)}, u32[]{:S(2)}, u32[]{:S(2)}) collective-permute-start(bf16[80,512]{1,0:T(8,128)(2,1)S(1)} %get-tuple-element.53), channel_id=1, source_target_pairs={{0,2},{1,3},{2,0},{3,1},{4,6},{5,7},{6,4},{7,5},{8,10},{9,11},{10,... | collective-permute-start | bytes 245768 | tf_op jit(solution)/shard_map/ppermute | solution.py:22
  19.3 1.5 %collective-permute-start.11 = (bf16[80,512]{1,0:T(8,128)(2,1)S(1)}, bf16[80,512]{1,0:T(8,128)(2,1)S(1)}, u32[]{:S(2)}, u32[]{:S(2)}) collective-permute-start(bf16[80,512]{1,0:T(8,128)(2,1)S(1)} %get-tuple-element.54), channel_id=1, source_target_pairs={{0,3},{1,0},{2,1},{3,2},{4,7},{5,4},{6,5},{7,6},{8,11},{9,8},{10,9... | collective-permute-start | bytes 245768 | tf_op jit(solution)/shard_map/ppermute | solution.py:22
  20.8 3.8 %collective-permute-start.20 = (s32[1,8320]{1,0:T(1,128)S(1)}, s32[1,8320]{1,0:T(1,128)S(1)}, u32[]{:S(2)}, u32[]{:S(2)}) collective-permute-start(s32[1,8320]{1,0:T(1,128)S(1)} %reshape_add_fusion), channel_id=1, source_target_pairs={{0,4},{4,8},{8,12},{12,16},{16,20},{20,24},{24,28},{28,32},{32,36}... | collective-permute-start | bytes 99848 | tf_op jit(solution)/shard_map/ppermute | solution.py:22
  24.6 1.0 %collective-permute-done.20.down_ref = s32[1,8320]{1,0:T(1,128)S(1)} collective-permute-done((s32[1,8320]{1,0:T(1,128)S(1)}, s32[1,8320]{1,0:T(1,128)S(1)}, u32[]{:S(2)}, u32[]{:S(2)}) %collective-permute-start.20) | collective-permute-done | bytes 33312 | tf_op jit(solution)/shard_map/ppermute | solution.py:22
  25.7 1.7 %collective-permute-start.13 = (bf16[200,768]{1,0:T(8,128)(2,1)S(1)}, bf16[200,768]{1,0:T(8,128)(2,1)S(1)}, u32[]{:S(2)}, u32[]{:S(2)}) collective-permute-start(bf16[200,768]{1,0:T(8,128)(2,1)S(1)} %copy-done.14), channel_id=1, source_target_pairs={{0,2},{1,3},{2,0},{3,1},{4,6},{5,7},{6,4},{7,5},{8,10},{9,11},{10,... | collective-permute-start | bytes 921608 | tf_op jit(solution)/shard_map/ppermute | solution.py:22
  27.4 0.9 collective-permute-start.14
  28.2 0.6 collective-permute-start
  28.9 1.6 %collective-permute-start.1 = (bf16[200,768]{1,0:T(8,128)(2,1)S(1)}, bf16[200,768]{1,0:T(8,128)(2,1)S(1)}, u32[]{:S(2)}, u32[]{:S(2)}) collective-permute-start(bf16[200,768]{1,0:T(8,128)(2,1)S(1)} %copy-done.11), channel_id=1, source_target_pairs={{0,2},{1,3},{2,0},{3,1},{4,6},{5,7},{6,4},{7,5},{8,10},{9,11},{10,... | collective-permute-start | bytes 921608 | tf_op jit(solution)/shard_map/ppermute | solution.py:22
  30.4 2.0 %collective-permute-start.2 = (bf16[200,768]{1,0:T(8,128)(2,1)S(1)}, bf16[200,768]{1,0:T(8,128)(2,1)S(1)}, u32[]{:S(2)}, u32[]{:S(2)}) collective-permute-start(bf16[200,768]{1,0:T(8,128)(2,1)S(1)} %copy-done.10), channel_id=1, source_target_pairs={{0,3},{1,0},{2,1},{3,2},{4,7},{5,4},{6,5},{7,6},{8,11},{9,8},{10,9... | collective-permute-start | bytes 921608 | tf_op jit(solution)/shard_map/ppermute | solution.py:22
  33.0 6.7 %collective-permute-start.18 = (bf16[80,512]{1,0:T(8,128)(2,1)S(1)}, bf16[80,512]{1,0:T(8,128)(2,1)S(1)}, u32[]{:S(2)}, u32[]{:S(2)}) collective-permute-start(bf16[80,512]{1,0:T(8,128)(2,1)S(1)} %get-tuple-element.63), channel_id=1, source_target_pairs={{0,4},{4,8},{8,12},{12,16},{16,20},{20,24},{24,28},{28,32},{32,36}... | collective-permute-start | bytes 245768 | tf_op jit(solution)/shard_map/ppermute | solution.py:22
  39.7 3.0 %collective-permute-done.14.rest_3_ = bf16[200,768]{1,0:T(8,128)(2,1)S(1)} collective-permute-done((bf16[200,768]{1,0:T(8,128)(2,1)S(1)}, bf16[200,768]{1,0:T(8,128)(2,1)S(1)}, u32[]{:S(2)}, u32[]{:S(2)}) %collective-permute-start.14) | collective-permute-done | bytes 307232 | tf_op jit(solution)/shard_map/ppermute | solution.py:22
  42.6 5.5 %collective-permute-start.19 = (bf16[80,512]{1,0:T(8,128)(2,1)S(1)}, bf16[80,512]{1,0:T(8,128)(2,1)S(1)}, u32[]{:S(2)}, u32[]{:S(2)}) collective-permute-start(bf16[80,512]{1,0:T(8,128)(2,1)S(1)} %get-tuple-element.64), channel_id=1, source_target_pairs={{0,124},{4,0},{8,4},{12,8},{16,12},{20,16},{24,20},{28,24},{32,28}... | collective-permute-start | bytes 245768 | tf_op jit(solution)/shard_map/ppermute | solution.py:22
  48.2 2.3 %one_hots.1 = (bf16[2,256,4096]{2,1,0:T(8,128)(2,1)S(1)}, bf16[2,4096,256]{2,1,0:T(8,128)(2,1)S(1)}, s32[4,4096]{1,0:T(4,128)S(1)}) custom-call(s32[1,8320]{1,0:T(1,128)S(1)} %collective-permute-done.20.down_ref, s32[1,4096]{1,0:T(1,128)S(1)} %copy-done.4, s32[1,4096]{1,0:T(1,128)S(1)} %copy-done.3, s32[1,1]{1,0:T(1,128)} %bitcast.9.count_ref), custom_call_target="tpu_custom_call" | custom-call | flops 41943040 | bytes 8388608 | tf_op jit(solution)/shard_map/one_hots/pallas_call | solution.py:255
  50.6 1.0 %mix.5 = (bf16[80,768]{1,0:T(8,128)(2,1)S(1)}, bf16[80,768]{1,0:T(8,128)(2,1)S(1)}, bf16[80,768]{1,0:T(8,128)(2,1)S(1)}, bf16[80,768]{1,0:T(8,128)(2,1)S(1)}) custom-call(bf16[4,320,200]{2,1,0:T(8,128)(2,1)S(1)} %spread.1.l_ref, bf16[200,768]{1,0:T(8,128)(2,1)S(1)} %kept.3.rest_0_, bf16[200,768]{1,0:T(8,128)(2,1)S(1)} %collective-permute-done.12.rest_1_, ...), custom_call_target="tpu_custom_call" | custom-call | flops 393216000 | bytes 1720320 | tf_op jit(solution)/shard_map/mix/pallas_call | solution.py:206
  51.6 1.7 %collective-permute-start.15 = (bf16[80,768]{1,0:T(8,128)(2,1)S(1)}, bf16[80,768]{1,0:T(8,128)(2,1)S(1)}, u32[]{:S(2)}, u32[]{:S(2)}) collective-permute-start(bf16[80,768]{1,0:T(8,128)(2,1)S(1)} %get-tuple-element.60), channel_id=1, source_target_pairs={{0,1},{1,2},{2,3},{3,0},{4,5},{5,6},{6,7},{7,4},{8,9},{9,10},{10,1... | collective-permute-start | bytes 368648 | tf_op jit(solution)/shard_map/ppermute | solution.py:22
  53.3 2.2 %collective-permute-start.16 = (bf16[80,768]{1,0:T(8,128)(2,1)S(1)}, bf16[80,768]{1,0:T(8,128)(2,1)S(1)}, u32[]{:S(2)}, u32[]{:S(2)}) collective-permute-start(bf16[80,768]{1,0:T(8,128)(2,1)S(1)} %get-tuple-element.61), channel_id=1, source_target_pairs={{0,2},{1,3},{2,0},{3,1},{4,6},{5,7},{6,4},{7,5},{8,10},{9,11},{10,... | collective-permute-start | bytes 368648 | tf_op jit(solution)/shard_map/ppermute | solution.py:22
  55.6 1.2 %collective-permute-start.17 = (bf16[80,768]{1,0:T(8,128)(2,1)S(1)}, bf16[80,768]{1,0:T(8,128)(2,1)S(1)}, u32[]{:S(2)}, u32[]{:S(2)}) collective-permute-start(bf16[80,768]{1,0:T(8,128)(2,1)S(1)} %get-tuple-element.62), channel_id=1, source_target_pairs={{0,3},{1,0},{2,1},{3,2},{4,7},{5,4},{6,5},{7,6},{8,11},{9,8},{10,9... | collective-permute-start | bytes 368648 | tf_op jit(solution)/shard_map/ppermute | solution.py:22
  56.8 1.0 %mix.3 = (bf16[80,768]{1,0:T(8,128)(2,1)S(1)}, bf16[80,768]{1,0:T(8,128)(2,1)S(1)}, bf16[80,768]{1,0:T(8,128)(2,1)S(1)}, bf16[80,768]{1,0:T(8,128)(2,1)S(1)}) custom-call(bf16[4,320,200]{2,1,0:T(8,128)(2,1)S(1)} %spread.1.l_ref, bf16[200,768]{1,0:T(8,128)(2,1)S(1)} %kept.2.rest_0_, bf16[200,768]{1,0:T(8,128)(2,1)S(1)} %collective-permute-done.rest_1_, ...), custom_call_target="tpu_custom_call" | custom-call | flops 393216000 | bytes 1720320 | tf_op jit(solution)/shard_map/mix/pallas_call | solution.py:206
  58.1 0.9 %collective-permute-start.4 = (bf16[80,768]{1,0:T(8,128)(2,1)S(1)}, bf16[80,768]{1,0:T(8,128)(2,1)S(1)}, u32[]{:S(2)}, u32[]{:S(2)}) collective-permute-start(bf16[80,768]{1,0:T(8,128)(2,1)S(1)} %get-tuple-element.45), channel_id=1, source_target_pairs={{0,2},{1,3},{2,0},{3,1},{4,6},{5,7},{6,4},{7,5},{8,10},{9,11},{10,... | collective-permute-start | bytes 368648 | tf_op jit(solution)/shard_map/ppermute | solution.py:22
  59.0 1.9 %links.1.rest_8_ = f32[64,16,128]{2,1,0:T(8,128)S(1)} custom-call(bf16[80,512]{1,0:T(8,128)(2,1)S(1)} %collective-permute-done.18.below_ref, bf16[80,512]{1,0:T(8,128)(2,1)S(1)} %collective-permute-done.19.above_ref, bf16[2,256,4096]{2,1,0:T(8,128)(2,1)S(1)} %get-tuple-element.65.g_ref, bf16[2,4096,256]{2,1,0:T(8,128)(2,1)S(1)} %get-tuple-element.66.s_ref, ...), custom_call_target="tpu_custom_call" | custom-call | flops 1342177280 | bytes 327680 | tf_op jit(solution)/shard_map/links/pallas_call | solution.py:317
  61.0 1.8 %collective-permute-start.5 = (bf16[80,768]{1,0:T(8,128)(2,1)S(1)}, bf16[80,768]{1,0:T(8,128)(2,1)S(1)}, u32[]{:S(2)}, u32[]{:S(2)}) collective-permute-start(bf16[80,768]{1,0:T(8,128)(2,1)S(1)} %get-tuple-element.46), channel_id=1, source_target_pairs={{0,3},{1,0},{2,1},{3,2},{4,7},{5,4},{6,5},{7,6},{8,11},{9,8},{10,9... | collective-permute-start | bytes 368648 | tf_op jit(solution)/shard_map/ppermute | solution.py:22
  62.8 3.7 %part_one.1 = (bf16[10,65536]{1,0:T(8,128)(2,1)}, bf16[10,65536]{1,0:T(8,128)(2,1)}, f32[128,16,128]{2,1,0:T(8,128)S(1)}, f32[2,16,128]{2,1,0:T(8,128)S(1)}) custom-call(s32[1]{0:T(128)} %bitcast.me_ref, bf16[80,512]{1,0:T(8,128)(2,1)S(1)} %get-tuple-element.51.rest_0_, bf16[80,512]{1,0:T(8,128)(2,1)S(1)} %collective-permute-done.9.rest_1_, ...), custom_call_target="tpu_custom_call" | custom-call | flops 2097152000 | bytes 4194304 | tf_op jit(solution)/shard_map/part_one/pallas_call | solution.py:536
  66.6 2.9 %part_two.1 = (bf16[10,65536]{1,0:T(8,128)(2,1)}, bf16[10,65536]{1,0:T(8,128)(2,1)}, f32[32,1,128]{2,1,0:T(1,128)S(1)}) custom-call(s32[1]{0:T(128)} %bitcast.me_ref, bf16[80,768]{1,0:T(8,128)(2,1)S(1)} %get-tuple-element.43.rest_0_, bf16[80,768]{1,0:T(8,128)(2,1)S(1)} %collective-permute-done.3.rest_1_, ...), custom_call_target="tpu_custom_call", output_to_operand_aliasing={{0}: (11, {}), {1}: (12, {})} | custom-call | flops 2097152000 | bytes 4194304 | tf_op jit(solution)/shard_map/part_two/pallas_call | solution.py:558
  69.4 19.1 %all_to_all.5 = f32[32,1,128]{2,1,0:T(1,128)S(1)} all-to-all(f32[32,1,128]{2,1,0:T(1,128)S(1)} %get-tuple-element.74), channel_id=1, replica_groups=mesh['rows'=32,'vecs'=4] {'rows'}, dimensions={0} | all-to-all | bytes 32768 | tf_op jit(solution)/shard_map/all_to_all | solution.py:643
  (59 shorter events, 2.1 us)
Async XLA Ops:
  2.7 11.1 %collective-permute-start.6 = (bf16[200,512]{1,0:T(8,128)(2,1)}, bf16[200,512]{1,0:T(8,128)(2,1)S(1)}, u32[]{:S(2)}, u32[]{:S(2)}) collective-permute-start(bf16[200,512]{1,0:T(8,128)(2,1)} %get-tuple-element.48), channel_id=1, source_target_pairs={{0,1},{1,2},{2,3},{3,0},{4,5},{5,6},{6,7},{7,4},{8,9},{9,10},{10,1... | collective-permute-start | bytes 614408 | tf_op jit(solution)/shard_map/ppermute | solution.py:22
  4.8 11.5 %collective-permute-start.7 = (bf16[200,512]{1,0:T(8,128)(2,1)}, bf16[200,512]{1,0:T(8,128)(2,1)S(1)}, u32[]{:S(2)}, u32[]{:S(2)}) collective-permute-start(bf16[200,512]{1,0:T(8,128)(2,1)} %get-tuple-element.49), channel_id=1, source_target_pairs={{0,2},{1,3},{2,0},{3,1},{4,6},{5,7},{6,4},{7,5},{8,10},{9,11},{10,... | collective-permute-start | bytes 614408 | tf_op jit(solution)/shard_map/ppermute | solution.py:22
  7.3 5.6 %copy-start.5 = (bf16[100,40]{0,1:T(8,128)(2,1)S(1)}, bf16[100,40]{0,1:T(8,128)(2,1)}, u32[]{:S(2)}) copy-start(bf16[100,40]{0,1:T(8,128)(2,1)} %param.10) | copy-start | bytes 24004
  7.3 9.1 %copy-start.2 = (bf16[200,512]{1,0:T(8,128)(2,1)S(1)}, bf16[200,512]{1,0:T(8,128)(2,1)}, u32[]{:S(2)}) copy-start(bf16[200,512]{1,0:T(8,128)(2,1)} %get-tuple-element.47.rest_0_) | copy-start | bytes 614404
  7.3 9.1 %collective-permute-start.8 = (bf16[200,512]{1,0:T(8,128)(2,1)}, bf16[200,512]{1,0:T(8,128)(2,1)S(1)}, u32[]{:S(2)}, u32[]{:S(2)}) collective-permute-start(bf16[200,512]{1,0:T(8,128)(2,1)} %get-tuple-element.50), channel_id=1, source_target_pairs={{0,3},{1,0},{2,1},{3,2},{4,7},{5,4},{6,5},{7,6},{8,11},{9,8},{10,9... | collective-permute-start | bytes 614408 | tf_op jit(solution)/shard_map/ppermute | solution.py:22
  11.6 9.2 %copy-start.3 = (s32[1,4096]{1,0:T(1,128)S(1)}, s32[1,4096]{1,0:T(1,128)}, u32[]{:S(2)}) copy-start(s32[1,4096]{1,0:T(1,128)} %upper_ref.1) | copy-start | bytes 49156
  11.6 9.2 %copy-start.4 = (s32[1,4096]{1,0:T(1,128)S(1)}, s32[1,4096]{1,0:T(1,128)}, u32[]{:S(2)}) copy-start(s32[1,4096]{1,0:T(1,128)} %lower_ref.1) | copy-start | bytes 49156
  11.6 14.1 %copy-start.14 = (bf16[200,768]{1,0:T(8,128)(2,1)S(1)}, bf16[200,768]{1,0:T(8,128)(2,1)}, u32[]{:S(2)}) copy-start(bf16[200,768]{1,0:T(8,128)(2,1)} %get-tuple-element.57) | copy-start | bytes 921604
  11.6 15.8 %copy-start.13 = (bf16[200,768]{1,0:T(8,128)(2,1)S(1)}, bf16[200,768]{1,0:T(8,128)(2,1)}, u32[]{:S(2)}) copy-start(bf16[200,768]{1,0:T(8,128)(2,1)} %get-tuple-element.58) | copy-start | bytes 921604
  11.6 16.6 %copy-start.12 = (bf16[200,768]{1,0:T(8,128)(2,1)S(1)}, bf16[200,768]{1,0:T(8,128)(2,1)}, u32[]{:S(2)}) copy-start(bf16[200,768]{1,0:T(8,128)(2,1)} %get-tuple-element.40) | copy-start | bytes 921604
  11.6 17.3 %copy-start.11 = (bf16[200,768]{1,0:T(8,128)(2,1)S(1)}, bf16[200,768]{1,0:T(8,128)(2,1)}, u32[]{:S(2)}) copy-start(bf16[200,768]{1,0:T(8,128)(2,1)} %get-tuple-element.41) | copy-start | bytes 921604
  11.6 18.8 %copy-start.10 = (bf16[200,768]{1,0:T(8,128)(2,1)S(1)}, bf16[200,768]{1,0:T(8,128)(2,1)}, u32[]{:S(2)}) copy-start(bf16[200,768]{1,0:T(8,128)(2,1)} %get-tuple-element.42) | copy-start | bytes 921604
  11.6 36.6 %copy-start.1 = (bf16[200,768]{1,0:T(8,128)(2,1)S(1)}, bf16[200,768]{1,0:T(8,128)(2,1)}, u32[]{:S(2)}) copy-start(bf16[200,768]{1,0:T(8,128)(2,1)} %get-tuple-element.55.from_ref) | copy-start | bytes 921604
  11.6 36.6 %copy-start = (bf16[200,768]{1,0:T(8,128)(2,1)S(1)}, bf16[200,768]{1,0:T(8,128)(2,1)}, u32[]{:S(2)}) copy-start(bf16[200,768]{1,0:T(8,128)(2,1)} %get-tuple-element.39.from_ref) | copy-start | bytes 921604
  11.6 18.8 %collective-permute-start.12 = (bf16[200,768]{1,0:T(8,128)(2,1)}, bf16[200,768]{1,0:T(8,128)(2,1)S(1)}, u32[]{:S(2)}, u32[]{:S(2)}) collective-permute-start(bf16[200,768]{1,0:T(8,128)(2,1)} %get-tuple-element.56), channel_id=1, source_target_pairs={{0,1},{1,2},{2,3},{3,0},{4,5},{5,6},{6,7},{7,4},{8,9},{9,10},{10,1... | collective-permute-start | bytes 921608 | tf_op jit(solution)/shard_map/ppermute | solution.py:22
  17.0 10.3 %collective-permute-start.10 = (bf16[80,512]{1,0:T(8,128)(2,1)S(1)}, bf16[80,512]{1,0:T(8,128)(2,1)S(1)}, u32[]{:S(2)}, u32[]{:S(2)}) collective-permute-start(bf16[80,512]{1,0:T(8,128)(2,1)S(1)} %get-tuple-element.53), channel_id=1, source_target_pairs={{0,2},{1,3},{2,0},{3,1},{4,6},{5,7},{6,4},{7,5},{8,10},{9,11},{10,... | collective-permute-start | bytes 245768 | tf_op jit(solution)/shard_map/ppermute | solution.py:22
  19.3 9.0 %collective-permute-start.11 = (bf16[80,512]{1,0:T(8,128)(2,1)S(1)}, bf16[80,512]{1,0:T(8,128)(2,1)S(1)}, u32[]{:S(2)}, u32[]{:S(2)}) collective-permute-start(bf16[80,512]{1,0:T(8,128)(2,1)S(1)} %get-tuple-element.54), channel_id=1, source_target_pairs={{0,3},{1,0},{2,1},{3,2},{4,7},{5,4},{6,5},{7,6},{8,11},{9,8},{10,9... | collective-permute-start | bytes 245768 | tf_op jit(solution)/shard_map/ppermute | solution.py:22
  20.7 8.1 %collective-permute-start.9 = (bf16[80,512]{1,0:T(8,128)(2,1)S(1)}, bf16[80,512]{1,0:T(8,128)(2,1)S(1)}, u32[]{:S(2)}, u32[]{:S(2)}) collective-permute-start(bf16[80,512]{1,0:T(8,128)(2,1)S(1)} %get-tuple-element.52), channel_id=1, source_target_pairs={{0,1},{1,2},{2,3},{3,0},{4,5},{5,6},{6,7},{7,4},{8,9},{9,10},{10,1... | collective-permute-start | bytes 245768 | tf_op jit(solution)/shard_map/ppermute | solution.py:22
  20.8 4.9 %collective-permute-start.20 = (s32[1,8320]{1,0:T(1,128)S(1)}, s32[1,8320]{1,0:T(1,128)S(1)}, u32[]{:S(2)}, u32[]{:S(2)}) collective-permute-start(s32[1,8320]{1,0:T(1,128)S(1)} %reshape_add_fusion), channel_id=1, source_target_pairs={{0,4},{4,8},{8,12},{12,16},{16,20},{20,24},{24,28},{28,32},{32,36}... | collective-permute-start | bytes 99848 | tf_op jit(solution)/shard_map/ppermute | solution.py:22
  25.7 7.3 %collective-permute-start.13 = (bf16[200,768]{1,0:T(8,128)(2,1)S(1)}, bf16[200,768]{1,0:T(8,128)(2,1)S(1)}, u32[]{:S(2)}, u32[]{:S(2)}) collective-permute-start(bf16[200,768]{1,0:T(8,128)(2,1)S(1)} %copy-done.14), channel_id=1, source_target_pairs={{0,2},{1,3},{2,0},{3,1},{4,6},{5,7},{6,4},{7,5},{8,10},{9,11},{10,... | collective-permute-start | bytes 921608 | tf_op jit(solution)/shard_map/ppermute | solution.py:22
  27.4 15.3 %collective-permute-start.14 = (bf16[200,768]{1,0:T(8,128)(2,1)S(1)}, bf16[200,768]{1,0:T(8,128)(2,1)S(1)}, u32[]{:S(2)}, u32[]{:S(2)}) collective-permute-start(bf16[200,768]{1,0:T(8,128)(2,1)S(1)} %copy-done.13), channel_id=1, source_target_pairs={{0,3},{1,0},{2,1},{3,2},{4,7},{5,4},{6,5},{7,6},{8,11},{9,8},{10,9... | collective-permute-start | bytes 921608 | tf_op jit(solution)/shard_map/ppermute | solution.py:22
  28.2 23.4 %collective-permute-start = (bf16[200,768]{1,0:T(8,128)(2,1)S(1)}, bf16[200,768]{1,0:T(8,128)(2,1)S(1)}, u32[]{:S(2)}, u32[]{:S(2)}) collective-permute-start(bf16[200,768]{1,0:T(8,128)(2,1)S(1)} %copy-done.12), channel_id=1, source_target_pairs={{0,1},{1,2},{2,3},{3,0},{4,5},{5,6},{6,7},{7,4},{8,9},{9,10},{10,1... | collective-permute-start | bytes 921608 | tf_op jit(solution)/shard_map/ppermute | solution.py:22
  28.9 24.5 %collective-permute-start.1 = (bf16[200,768]{1,0:T(8,128)(2,1)S(1)}, bf16[200,768]{1,0:T(8,128)(2,1)S(1)}, u32[]{:S(2)}, u32[]{:S(2)}) collective-permute-start(bf16[200,768]{1,0:T(8,128)(2,1)S(1)} %copy-done.11), channel_id=1, source_target_pairs={{0,2},{1,3},{2,0},{3,1},{4,6},{5,7},{6,4},{7,5},{8,10},{9,11},{10,... | collective-permute-start | bytes 921608 | tf_op jit(solution)/shard_map/ppermute | solution.py:22
  30.4 25.1 %collective-permute-start.2 = (bf16[200,768]{1,0:T(8,128)(2,1)S(1)}, bf16[200,768]{1,0:T(8,128)(2,1)S(1)}, u32[]{:S(2)}, u32[]{:S(2)}) collective-permute-start(bf16[200,768]{1,0:T(8,128)(2,1)S(1)} %copy-done.10), channel_id=1, source_target_pairs={{0,3},{1,0},{2,1},{3,2},{4,7},{5,4},{6,5},{7,6},{8,11},{9,8},{10,9... | collective-permute-start | bytes 921608 | tf_op jit(solution)/shard_map/ppermute | solution.py:22
  33.0 24.8 %collective-permute-start.18 = (bf16[80,512]{1,0:T(8,128)(2,1)S(1)}, bf16[80,512]{1,0:T(8,128)(2,1)S(1)}, u32[]{:S(2)}, u32[]{:S(2)}) collective-permute-start(bf16[80,512]{1,0:T(8,128)(2,1)S(1)} %get-tuple-element.63), channel_id=1, source_target_pairs={{0,4},{4,8},{8,12},{12,16},{16,20},{20,24},{24,28},{28,32},{32,36}... | collective-permute-start | bytes 245768 | tf_op jit(solution)/shard_map/ppermute | solution.py:22
  42.6 15.5 %collective-permute-start.19 = (bf16[80,512]{1,0:T(8,128)(2,1)S(1)}, bf16[80,512]{1,0:T(8,128)(2,1)S(1)}, u32[]{:S(2)}, u32[]{:S(2)}) collective-permute-start(bf16[80,512]{1,0:T(8,128)(2,1)S(1)} %get-tuple-element.64), channel_id=1, source_target_pairs={{0,124},{4,0},{8,4},{12,8},{16,12},{20,16},{24,20},{28,24},{32,28}... | collective-permute-start | bytes 245768 | tf_op jit(solution)/shard_map/ppermute | solution.py:22
  51.6 9.4 %collective-permute-start.15 = (bf16[80,768]{1,0:T(8,128)(2,1)S(1)}, bf16[80,768]{1,0:T(8,128)(2,1)S(1)}, u32[]{:S(2)}, u32[]{:S(2)}) collective-permute-start(bf16[80,768]{1,0:T(8,128)(2,1)S(1)} %get-tuple-element.60), channel_id=1, source_target_pairs={{0,1},{1,2},{2,3},{3,0},{4,5},{5,6},{6,7},{7,4},{8,9},{9,10},{10,1... | collective-permute-start | bytes 368648 | tf_op jit(solution)/shard_map/ppermute | solution.py:22
  53.3 9.5 %collective-permute-start.16 = (bf16[80,768]{1,0:T(8,128)(2,1)S(1)}, bf16[80,768]{1,0:T(8,128)(2,1)S(1)}, u32[]{:S(2)}, u32[]{:S(2)}) collective-permute-start(bf16[80,768]{1,0:T(8,128)(2,1)S(1)} %get-tuple-element.61), channel_id=1, source_target_pairs={{0,2},{1,3},{2,0},{3,1},{4,6},{5,7},{6,4},{7,5},{8,10},{9,11},{10,... | collective-permute-start | bytes 368648 | tf_op jit(solution)/shard_map/ppermute | solution.py:22
  55.6 7.2 %collective-permute-start.17 = (bf16[80,768]{1,0:T(8,128)(2,1)S(1)}, bf16[80,768]{1,0:T(8,128)(2,1)S(1)}, u32[]{:S(2)}, u32[]{:S(2)}) collective-permute-start(bf16[80,768]{1,0:T(8,128)(2,1)S(1)} %get-tuple-element.62), channel_id=1, source_target_pairs={{0,3},{1,0},{2,1},{3,2},{4,7},{5,4},{6,5},{7,6},{8,11},{9,8},{10,9... | collective-permute-start | bytes 368648 | tf_op jit(solution)/shard_map/ppermute | solution.py:22
  57.8 8.8 %collective-permute-start.3 = (bf16[80,768]{1,0:T(8,128)(2,1)S(1)}, bf16[80,768]{1,0:T(8,128)(2,1)S(1)}, u32[]{:S(2)}, u32[]{:S(2)}) collective-permute-start(bf16[80,768]{1,0:T(8,128)(2,1)S(1)} %get-tuple-element.44), channel_id=1, source_target_pairs={{0,1},{1,2},{2,3},{3,0},{4,5},{5,6},{6,7},{7,4},{8,9},{9,10},{10,1... | collective-permute-start | bytes 368648 | tf_op jit(solution)/shard_map/ppermute | solution.py:22
  58.1 8.4 %collective-permute-start.4 = (bf16[80,768]{1,0:T(8,128)(2,1)S(1)}, bf16[80,768]{1,0:T(8,128)(2,1)S(1)}, u32[]{:S(2)}, u32[]{:S(2)}) collective-permute-start(bf16[80,768]{1,0:T(8,128)(2,1)S(1)} %get-tuple-element.45), channel_id=1, source_target_pairs={{0,2},{1,3},{2,0},{3,1},{4,6},{5,7},{6,4},{7,5},{8,10},{9,11},{10,... | collective-permute-start | bytes 368648 | tf_op jit(solution)/shard_map/ppermute | solution.py:22
  61.0 5.6 %collective-permute-start.5 = (bf16[80,768]{1,0:T(8,128)(2,1)S(1)}, bf16[80,768]{1,0:T(8,128)(2,1)S(1)}, u32[]{:S(2)}, u32[]{:S(2)}) collective-permute-start(bf16[80,768]{1,0:T(8,128)(2,1)S(1)} %get-tuple-element.46), channel_id=1, source_target_pairs={{0,3},{1,0},{2,1},{3,2},{4,7},{5,4},{6,5},{7,6},{8,11},{9,8},{10,9... | collective-permute-start | bytes 368648 | tf_op jit(solution)/shard_map/ppermute | solution.py:22
  (4 other events, 15.2 us)

commit v5 on v4

--- a/solution.py
+++ b/solution.py
@@ -480,7 +480,7 @@
     zero = jnp.zeros((NP, LANES), F32)
     links = {0: (link_ref, 0, 1), planes - 1: (link_ref, tiles, -1)}
     carry, ready = finished_planes(
-        terms, cells, 0, (zero, zero), links, outs, out, 1, split, (0, planes - 1), 3
+        terms, cells, 0, (zero, zero), links, outs, out, 1, split, (0, planes - 1), 1
     )
     edge_ref[0 : 2 * tiles] = cells[(split - 1) * tiles : (split + 1) * tiles]
     edge_ref[2 * tiles : 4 * tiles] = cells[(planes - 2) * tiles : planes * tiles]
@@ -525,7 +525,7 @@
         pltpu.VMEM((planes * tiles, NP, LANES), F32),
         pltpu.VMEM((vecs, kept_planes * WID * WID), BF),
         pltpu.VMEM((vecs, kept_planes * WID * WID), BF),
-        pltpu.SemaphoreType.DMA((16,)),
+        pltpu.SemaphoreType.DMA((24,)),
     ]
 
 
@@ -605,7 +605,7 @@
     planes = rows_local // (WID * WID)
     me = lax.axis_index("vecs").astype(jnp.int32)[None]
     ends = Chunk(None, 4, parts, planes)
-    middle = (planes - 4) // 2 + 2
+    middle = (planes - 4) // 2 + 4
     one = Chunk(2, middle - 2, parts, planes)
     two = Chunk(middle, planes - 2 - middle, parts, planes)
     wide_count = jnp.broadcast_to(link_count[:, None], (1, LANES))

time: 89.4 us -> 87.1 us (0.974)
  waiting for transfers between devices: 7.12 us -> 14.7 us
  starting transfers between devices: 40.8 us -> 33.3 us
  blocking collectives: 19.1 us -> 17.5 us
    ppermute x21, waiting for transfers between devices: 7.12 us -> 14.7 us  [from_behind(): return lax.ppermute(value, axis, pairs)]
    ppermute x21, starting transfers between devices: 40.8 us -> 33.3 us  [from_behind(): return lax.ppermute(value, axis, pairs)]
    all_to_all x1, blocking collectives: 19.1 us -> 17.5 us  [on_device(): total = lax.all_to_all(sums, 'rows', 0, 0, tiled=True).sum(axis=(0, 1))]
  transfers between devices with their start and end apart: 21 -> 21, of which waited for: 4 -> 5; matrix products, arithmetic and copies ran while one was open for 0% -> 0% of each run, Pallas kernels for 16% -> 17%
where the time goes in v5:
time: 87.1 us; the launch traced here: 86.9 us
  starting transfers between devices  33.3 us (38%)
  Pallas kernels  19.1 us (22%)
  blocking collectives  17.5 us (20%)
  waiting for transfers between devices  14.7 us (17%)
  between operations  1.59 us (2%)
    ppermute x21, starting transfers between devices, from_behind(): return lax.ppermute(value, axis, pairs)  33.3 us
    all_to_all x1, blocking collectives, on_device(): total = lax.all_to_all(sums, 'rows', 0, 0, tiled=True).sum(axis=(0, 1))  17.5 us
    ppermute x21, waiting for transfers between devices, from_behind(): return lax.ppermute(value, axis, pairs)  14.7 us
    pallas_call x2, Pallas kernels, pack(): pl.pallas_call(functools.partial(pack_kernel, chunks, parts), out_shape=s...  5.21 us
    pallas_call x1, Pallas kernels, part_one(): pl.pallas_call(functools.partial(part_one_kernel, chunks, parts, planes,...  3.46 us
    pallas_call x3, Pallas kernels, mix(): pl.pallas_call(functools.partial(mix_kernel, parts, lane, seg), out_shape...  2.7 us
    pallas_call x1, Pallas kernels, part_two(): pl.pallas_call(functools.partial(part_two_kernel, chunk, parts, planes, s...  2.46 us
    pallas_call x1, Pallas kernels, one_hots(): pl.pallas_call(functools.partial(one_hot_kernel, low), out_shape=(hot, ho...  2.34 us
  transfers between devices with their start and end apart: 21, of which 5 were waited for; matrix products, arithmetic and copies ran while one was open for 0% of the time, Pallas kernels for 17%

profile of v5, /device:TPU:1, one launch (start us, length us, event | category | flops | bytes accessed | tf_op | source)
XLA Modules:
  0.0 86.9 jit_solution(16145228831119038691)
XLA Ops:
  0.6 2.1 %pack.3 = (bf16[200,512]{1,0:T(8,128)(2,1)}, bf16[200,512]{1,0:T(8,128)(2,1)}, bf16[200,512]{1,0:T(8,128)(2,1)}, bf16[200,512]{1,0:T(8,128)(2,1)}) custom-call(s32[1]{0:T(128)} %bitcast.me_ref, bf16[25,65536]{1,0:T(8,128)(2,1)} %basis_ref.3), custom_call_target="tpu_custom_call" | custom-call | flops 1 | bytes 1638400 | tf_op jit(solution)/shard_map/pack/pallas_call | solution.py:124
  2.8 2.1 %collective-permute-start.6 = (bf16[200,512]{1,0:T(8,128)(2,1)}, bf16[200,512]{1,0:T(8,128)(2,1)S(1)}, u32[]{:S(2)}, u32[]{:S(2)}) collective-permute-start(bf16[200,512]{1,0:T(8,128)(2,1)} %get-tuple-element.48), channel_id=1, source_target_pairs={{0,1},{1,2},{2,3},{3,0},{4,5},{5,6},{6,7},{7,4},{8,9},{9,10},{10,1... | collective-permute-start | bytes 614408 | tf_op jit(solution)/shard_map/ppermute | solution.py:22
  4.9 2.5 %collective-permute-start.7 = (bf16[200,512]{1,0:T(8,128)(2,1)}, bf16[200,512]{1,0:T(8,128)(2,1)S(1)}, u32[]{:S(2)}, u32[]{:S(2)}) collective-permute-start(bf16[200,512]{1,0:T(8,128)(2,1)} %get-tuple-element.49), channel_id=1, source_target_pairs={{0,2},{1,3},{2,0},{3,1},{4,6},{5,7},{6,4},{7,5},{8,10},{9,11},{10,... | collective-permute-start | bytes 614408 | tf_op jit(solution)/shard_map/ppermute | solution.py:22
  7.3 1.2 %collective-permute-start.8 = (bf16[200,512]{1,0:T(8,128)(2,1)}, bf16[200,512]{1,0:T(8,128)(2,1)S(1)}, u32[]{:S(2)}, u32[]{:S(2)}) collective-permute-start(bf16[200,512]{1,0:T(8,128)(2,1)} %get-tuple-element.50), channel_id=1, source_target_pairs={{0,3},{1,0},{2,1},{3,2},{4,7},{5,4},{6,5},{7,6},{8,11},{9,8},{10,9... | collective-permute-start | bytes 614408 | tf_op jit(solution)/shard_map/ppermute | solution.py:22
  8.5 3.1 %pack.2 = (bf16[200,1024]{1,0:T(8,128)(2,1)}, bf16[200,1024]{1,0:T(8,128)(2,1)}, bf16[200,1024]{1,0:T(8,128)(2,1)}, bf16[200,1024]{1,0:T(8,128)(2,1)}, bf16[200,...) custom-call(s32[1]{0:T(128)} %bitcast.me_ref, ...), custom_call_target="tpu_custom_call" | custom-call | flops 1 | bytes 4915200 | tf_op jit(solution)/shard_map/pack/pallas_call | solution.py:124
  11.6 0.4 collective-permute-start.12
  12.0 0.9 %collective-permute-start.13 = (bf16[200,1024]{1,0:T(8,128)(2,1)}, bf16[200,1024]{1,0:T(8,128)(2,1)S(1)}, u32[]{:S(2)}, u32[]{:S(2)}) collective-permute-start(bf16[200,1024]{1,0:T(8,128)(2,1)} %get-tuple-element.57), channel_id=1, source_target_pairs={{0,2},{1,3},{2,0},{3,1},{4,6},{5,7},{6,4},{7,5},{8,10},{9,11},{10,... | collective-permute-start | bytes 1228808 | tf_op jit(solution)/shard_map/ppermute | solution.py:22
  13.6 0.9 spread.1.l_ref
  14.5 1.6 %collective-permute-start.14 = (bf16[200,1024]{1,0:T(8,128)(2,1)}, bf16[200,1024]{1,0:T(8,128)(2,1)S(1)}, u32[]{:S(2)}, u32[]{:S(2)}) collective-permute-start(bf16[200,1024]{1,0:T(8,128)(2,1)} %get-tuple-element.58), channel_id=1, source_target_pairs={{0,3},{1,0},{2,1},{3,2},{4,7},{5,4},{6,5},{7,6},{8,11},{9,8},{10,9... | collective-permute-start | bytes 1228808 | tf_op jit(solution)/shard_map/ppermute | solution.py:22
  16.4 0.7 mix.4
  17.1 2.2 %collective-permute-start.10 = (bf16[80,512]{1,0:T(8,128)(2,1)S(1)}, bf16[80,512]{1,0:T(8,128)(2,1)S(1)}, u32[]{:S(2)}, u32[]{:S(2)}) collective-permute-start(bf16[80,512]{1,0:T(8,128)(2,1)S(1)} %get-tuple-element.53), channel_id=1, source_target_pairs={{0,2},{1,3},{2,0},{3,1},{4,6},{5,7},{6,4},{7,5},{8,10},{9,11},{10,... | collective-permute-start | bytes 245768 | tf_op jit(solution)/shard_map/ppermute | solution.py:22
  19.4 4.7 %collective-permute-start.20 = (s32[1,8320]{1,0:T(1,128)S(1)}, s32[1,8320]{1,0:T(1,128)S(1)}, u32[]{:S(2)}, u32[]{:S(2)}) collective-permute-start(s32[1,8320]{1,0:T(1,128)S(1)} %reshape_add_fusion), channel_id=1, source_target_pairs={{0,4},{4,8},{8,12},{12,16},{16,20},{20,24},{24,28},{28,32},{32,36}... | collective-permute-start | bytes 99848 | tf_op jit(solution)/shard_map/ppermute | solution.py:22
  24.0 1.0 %collective-permute-done.20.down_ref = s32[1,8320]{1,0:T(1,128)S(1)} collective-permute-done((s32[1,8320]{1,0:T(1,128)S(1)}, s32[1,8320]{1,0:T(1,128)S(1)}, u32[]{:S(2)}, u32[]{:S(2)}) %collective-permute-start.20) | collective-permute-done | bytes 33312 | tf_op jit(solution)/shard_map/ppermute | solution.py:22
  25.4 10.3 %collective-permute-done.10.rest_2_ = bf16[80,512]{1,0:T(8,128)(2,1)S(1)} collective-permute-done((bf16[80,512]{1,0:T(8,128)(2,1)S(1)}, bf16[80,512]{1,0:T(8,128)(2,1)S(1)}, u32[]{:S(2)}, u32[]{:S(2)}) %collective-permute-start.10) | collective-permute-done | bytes 81952 | tf_op jit(solution)/shard_map/ppermute | solution.py:22
  35.7 1.3 %collective-permute-start.9 = (bf16[80,512]{1,0:T(8,128)(2,1)S(1)}, bf16[80,512]{1,0:T(8,128)(2,1)S(1)}, u32[]{:S(2)}, u32[]{:S(2)}) collective-permute-start(bf16[80,512]{1,0:T(8,128)(2,1)S(1)} %get-tuple-element.52), channel_id=1, source_target_pairs={{0,1},{1,2},{2,3},{3,0},{4,5},{5,6},{6,7},{7,4},{8,9},{9,10},{10,1... | collective-permute-start | bytes 245768 | tf_op jit(solution)/shard_map/ppermute | solution.py:22
  37.0 1.2 %collective-permute-start = (bf16[200,512]{1,0:T(8,128)(2,1)S(1)}, bf16[200,512]{1,0:T(8,128)(2,1)S(1)}, u32[]{:S(2)}, u32[]{:S(2)}) collective-permute-start(bf16[200,512]{1,0:T(8,128)(2,1)S(1)} %copy-done.12), channel_id=1, source_target_pairs={{0,1},{1,2},{2,3},{3,0},{4,5},{5,6},{6,7},{7,4},{8,9},{9,10},{10,1... | collective-permute-start | bytes 614408 | tf_op jit(solution)/shard_map/ppermute | solution.py:22
  38.2 2.0 %collective-permute-done.9.rest_1_ = bf16[80,512]{1,0:T(8,128)(2,1)S(1)} collective-permute-done((bf16[80,512]{1,0:T(8,128)(2,1)S(1)}, bf16[80,512]{1,0:T(8,128)(2,1)S(1)}, u32[]{:S(2)}, u32[]{:S(2)}) %collective-permute-start.9) | collective-permute-done | bytes 81952 | tf_op jit(solution)/shard_map/ppermute | solution.py:22
  40.2 1.4 %collective-permute-start.1 = (bf16[200,512]{1,0:T(8,128)(2,1)S(1)}, bf16[200,512]{1,0:T(8,128)(2,1)S(1)}, u32[]{:S(2)}, u32[]{:S(2)}) collective-permute-start(bf16[200,512]{1,0:T(8,128)(2,1)S(1)} %copy-done.11), channel_id=1, source_target_pairs={{0,2},{1,3},{2,0},{3,1},{4,6},{5,7},{6,4},{7,5},{8,10},{9,11},{10,... | collective-permute-start | bytes 614408 | tf_op jit(solution)/shard_map/ppermute | solution.py:22
  41.6 1.1 %collective-permute-start.2 = (bf16[200,512]{1,0:T(8,128)(2,1)S(1)}, bf16[200,512]{1,0:T(8,128)(2,1)S(1)}, u32[]{:S(2)}, u32[]{:S(2)}) collective-permute-start(bf16[200,512]{1,0:T(8,128)(2,1)S(1)} %copy-done.10), channel_id=1, source_target_pairs={{0,3},{1,0},{2,1},{3,2},{4,7},{5,4},{6,5},{7,6},{8,11},{9,8},{10,9... | collective-permute-start | bytes 614408 | tf_op jit(solution)/shard_map/ppermute | solution.py:22
  42.8 6.0 %collective-permute-start.18 = (bf16[80,512]{1,0:T(8,128)(2,1)S(1)}, bf16[80,512]{1,0:T(8,128)(2,1)S(1)}, u32[]{:S(2)}, u32[]{:S(2)}) collective-permute-start(bf16[80,512]{1,0:T(8,128)(2,1)S(1)} %get-tuple-element.63), channel_id=1, source_target_pairs={{0,4},{4,8},{8,12},{12,16},{16,20},{20,24},{24,28},{28,32},{32,36}... | collective-permute-start | bytes 245768 | tf_op jit(solution)/shard_map/ppermute | solution.py:22
  48.8 1.4 %mix.5 = (bf16[80,1024]{1,0:T(8,128)(2,1)S(1)}, bf16[80,1024]{1,0:T(8,128)(2,1)S(1)}, bf16[80,1024]{1,0:T(8,128)(2,1)S(1)}, bf16[80,1024]{1,0:T(8,128)(2,1)S(1)}) custom-call(bf16[4,320,200]{2,1,0:T(8,128)(2,1)S(1)} %spread.1.l_ref, bf16[200,1024]{1,0:T(8,128)(2,1)S(1)} %kept.3.rest_0_, bf16[200,1024]{1,0:T(8,128)(2,1)S(1)} %collective-permute-done.12.rest_1_, ...), custom_call_target="tpu_custom_call" | custom-call | flops 524288000 | bytes 2293760 | tf_op jit(solution)/shard_map/mix/pallas_call | solution.py:206
  50.3 1.1 %collective-permute-done.1.rest_2_ = bf16[200,512]{1,0:T(8,128)(2,1)S(1)} collective-permute-done((bf16[200,512]{1,0:T(8,128)(2,1)S(1)}, bf16[200,512]{1,0:T(8,128)(2,1)S(1)}, u32[]{:S(2)}, u32[]{:S(2)}) %collective-permute-start.1) | collective-permute-done | bytes 204832 | tf_op jit(solution)/shard_map/ppermute | solution.py:22
  51.6 1.8 %collective-permute-start.17 = (bf16[80,1024]{1,0:T(8,128)(2,1)S(1)}, bf16[80,1024]{1,0:T(8,128)(2,1)S(1)}, u32[]{:S(2)}, u32[]{:S(2)}) collective-permute-start(bf16[80,1024]{1,0:T(8,128)(2,1)S(1)} %get-tuple-element.62), channel_id=1, source_target_pairs={{0,3},{1,0},{2,1},{3,2},{4,7},{5,4},{6,5},{7,6},{8,11},{9,8},{10,9... | collective-permute-start | bytes 491528 | tf_op jit(solution)/shard_map/ppermute | solution.py:22
  53.4 2.3 %one_hots.1 = (bf16[2,256,4096]{2,1,0:T(8,128)(2,1)S(1)}, bf16[2,4096,256]{2,1,0:T(8,128)(2,1)S(1)}, s32[4,4096]{1,0:T(4,128)S(1)}) custom-call(s32[1,8320]{1,0:T(1,128)S(1)} %collective-permute-done.20.down_ref, s32[1,4096]{1,0:T(1,128)S(1)} %copy-done.4, s32[1,4096]{1,0:T(1,128)S(1)} %copy-done.3, s32[1,1]{1,0:T(1,128)} %bitcast.9.count_ref), custom_call_target="tpu_custom_call" | custom-call | flops 41943040 | bytes 8388608 | tf_op jit(solution)/shard_map/one_hots/pallas_call | solution.py:255
  55.8 0.7 mix.3
  56.7 2.3 %collective-permute-start.4 = (bf16[80,512]{1,0:T(8,128)(2,1)S(1)}, bf16[80,512]{1,0:T(8,128)(2,1)S(1)}, u32[]{:S(2)}, u32[]{:S(2)}) collective-permute-start(bf16[80,512]{1,0:T(8,128)(2,1)S(1)} %get-tuple-element.45), channel_id=1, source_target_pairs={{0,2},{1,3},{2,0},{3,1},{4,6},{5,7},{6,4},{7,5},{8,10},{9,11},{10,... | collective-permute-start | bytes 245768 | tf_op jit(solution)/shard_map/ppermute | solution.py:22
  58.9 1.9 %links.1.rest_8_ = f32[64,16,128]{2,1,0:T(8,128)S(1)} custom-call(bf16[80,512]{1,0:T(8,128)(2,1)S(1)} %collective-permute-done.18.below_ref, bf16[80,512]{1,0:T(8,128)(2,1)S(1)} %collective-permute-done.19.above_ref, bf16[2,256,4096]{2,1,0:T(8,128)(2,1)S(1)} %get-tuple-element.65.g_ref, bf16[2,4096,256]{2,1,0:T(8,128)(2,1)S(1)} %get-tuple-element.66.s_ref, ...), custom_call_target="tpu_custom_call" | custom-call | flops 1342177280 | bytes 327680 | tf_op jit(solution)/shard_map/links/pallas_call | solution.py:317
  60.9 1.8 %collective-permute-start.5 = (bf16[80,512]{1,0:T(8,128)(2,1)S(1)}, bf16[80,512]{1,0:T(8,128)(2,1)S(1)}, u32[]{:S(2)}, u32[]{:S(2)}) collective-permute-start(bf16[80,512]{1,0:T(8,128)(2,1)S(1)} %get-tuple-element.46), channel_id=1, source_target_pairs={{0,3},{1,0},{2,1},{3,2},{4,7},{5,4},{6,5},{7,6},{8,11},{9,8},{10,9... | collective-permute-start | bytes 245768 | tf_op jit(solution)/shard_map/ppermute | solution.py:22
  62.8 3.5 %part_one.1 = (bf16[10,65536]{1,0:T(8,128)(2,1)}, bf16[10,65536]{1,0:T(8,128)(2,1)}, f32[128,16,128]{2,1,0:T(8,128)S(1)}, f32[2,16,128]{2,1,0:T(8,128)S(1)}) custom-call(s32[1]{0:T(128)} %bitcast.me_ref, bf16[80,512]{1,0:T(8,128)(2,1)S(1)} %get-tuple-element.51.rest_0_, bf16[80,512]{1,0:T(8,128)(2,1)S(1)} %collective-permute-done.9.rest_1_, ...), custom_call_target="tpu_custom_call" | custom-call | flops 2097152000 | bytes 4194304 | tf_op jit(solution)/shard_map/part_one/pallas_call | solution.py:536
  66.3 2.5 %part_two.1 = (bf16[10,65536]{1,0:T(8,128)(2,1)}, bf16[10,65536]{1,0:T(8,128)(2,1)}, f32[32,1,128]{2,1,0:T(1,128)S(1)}) custom-call(s32[1]{0:T(128)} %bitcast.me_ref, bf16[80,512]{1,0:T(8,128)(2,1)S(1)} %get-tuple-element.43.rest_0_, bf16[80,512]{1,0:T(8,128)(2,1)S(1)} %collective-permute-done.3.rest_1_, ...), custom_call_target="tpu_custom_call", output_to_operand_aliasing={{0}: (11, {}), {1}: (12, {})} | custom-call | flops 2097152000 | bytes 4194304 | tf_op jit(solution)/shard_map/part_two/pallas_call | solution.py:558
  68.7 17.5 %all_to_all.5 = f32[32,1,128]{2,1,0:T(1,128)S(1)} all-to-all(f32[32,1,128]{2,1,0:T(1,128)S(1)} %get-tuple-element.74), channel_id=1, replica_groups=mesh['rows'=32,'vecs'=4] {'rows'}, dimensions={0} | all-to-all | bytes 32768 | tf_op jit(solution)/shard_map/all_to_all | solution.py:643
  86.3 0.6 rsqrt_multiply_fusion
  (55 shorter events, 1.5 us)
Async XLA Ops:
  2.8 11.7 %collective-permute-start.6 = (bf16[200,512]{1,0:T(8,128)(2,1)}, bf16[200,512]{1,0:T(8,128)(2,1)S(1)}, u32[]{:S(2)}, u32[]{:S(2)}) collective-permute-start(bf16[200,512]{1,0:T(8,128)(2,1)} %get-tuple-element.48), channel_id=1, source_target_pairs={{0,1},{1,2},{2,3},{3,0},{4,5},{5,6},{6,7},{7,4},{8,9},{9,10},{10,1... | collective-permute-start | bytes 614408 | tf_op jit(solution)/shard_map/ppermute | solution.py:22
  4.9 11.5 %collective-permute-start.7 = (bf16[200,512]{1,0:T(8,128)(2,1)}, bf16[200,512]{1,0:T(8,128)(2,1)S(1)}, u32[]{:S(2)}, u32[]{:S(2)}) collective-permute-start(bf16[200,512]{1,0:T(8,128)(2,1)} %get-tuple-element.49), channel_id=1, source_target_pairs={{0,2},{1,3},{2,0},{3,1},{4,6},{5,7},{6,4},{7,5},{8,10},{9,11},{10,... | collective-permute-start | bytes 614408 | tf_op jit(solution)/shard_map/ppermute | solution.py:22
  7.3 6.3 %copy-start.5 = (bf16[100,40]{0,1:T(8,128)(2,1)S(1)}, bf16[100,40]{0,1:T(8,128)(2,1)}, u32[]{:S(2)}) copy-start(bf16[100,40]{0,1:T(8,128)(2,1)} %param.10) | copy-start | bytes 24004
  7.3 9.1 %copy-start.2 = (bf16[200,512]{1,0:T(8,128)(2,1)S(1)}, bf16[200,512]{1,0:T(8,128)(2,1)}, u32[]{:S(2)}) copy-start(bf16[200,512]{1,0:T(8,128)(2,1)} %get-tuple-element.47.rest_0_) | copy-start | bytes 614404
  7.3 9.1 %collective-permute-start.8 = (bf16[200,512]{1,0:T(8,128)(2,1)}, bf16[200,512]{1,0:T(8,128)(2,1)S(1)}, u32[]{:S(2)}, u32[]{:S(2)}) collective-permute-start(bf16[200,512]{1,0:T(8,128)(2,1)} %get-tuple-element.50), channel_id=1, source_target_pairs={{0,3},{1,0},{2,1},{3,2},{4,7},{5,4},{6,5},{7,6},{8,11},{9,8},{10,9... | collective-permute-start | bytes 614408 | tf_op jit(solution)/shard_map/ppermute | solution.py:22
  11.6 7.8 %copy-start.3 = (s32[1,4096]{1,0:T(1,128)S(1)}, s32[1,4096]{1,0:T(1,128)}, u32[]{:S(2)}) copy-start(s32[1,4096]{1,0:T(1,128)} %upper_ref.1) | copy-start | bytes 49156
  11.6 7.7 %copy-start.4 = (s32[1,4096]{1,0:T(1,128)S(1)}, s32[1,4096]{1,0:T(1,128)}, u32[]{:S(2)}) copy-start(s32[1,4096]{1,0:T(1,128)} %lower_ref.1) | copy-start | bytes 49156
  11.6 25.4 %copy-start.12 = (bf16[200,512]{1,0:T(8,128)(2,1)S(1)}, bf16[200,512]{1,0:T(8,128)(2,1)}, u32[]{:S(2)}) copy-start(bf16[200,512]{1,0:T(8,128)(2,1)} %get-tuple-element.40) | copy-start | bytes 614404
  11.6 28.6 %copy-start.11 = (bf16[200,512]{1,0:T(8,128)(2,1)S(1)}, bf16[200,512]{1,0:T(8,128)(2,1)}, u32[]{:S(2)}) copy-start(bf16[200,512]{1,0:T(8,128)(2,1)} %get-tuple-element.41) | copy-start | bytes 614404
  11.6 30.0 %copy-start.10 = (bf16[200,512]{1,0:T(8,128)(2,1)S(1)}, bf16[200,512]{1,0:T(8,128)(2,1)}, u32[]{:S(2)}) copy-start(bf16[200,512]{1,0:T(8,128)(2,1)} %get-tuple-element.42) | copy-start | bytes 614404
  11.6 31.1 %copy-start = (bf16[200,1024]{1,0:T(8,128)(2,1)S(1)}, bf16[200,1024]{1,0:T(8,128)(2,1)}, u32[]{:S(2)}) copy-start(bf16[200,1024]{1,0:T(8,128)(2,1)} %get-tuple-element.55.from_ref) | copy-start | bytes 1228804
  11.6 30.0 %collective-permute-start.12 = (bf16[200,1024]{1,0:T(8,128)(2,1)}, bf16[200,1024]{1,0:T(8,128)(2,1)S(1)}, u32[]{:S(2)}, u32[]{:S(2)}) collective-permute-start(bf16[200,1024]{1,0:T(8,128)(2,1)} %get-tuple-element.56), channel_id=1, source_target_pairs={{0,1},{1,2},{2,3},{3,0},{4,5},{5,6},{6,7},{7,4},{8,9},{9,10},{10,1... | collective-permute-start | bytes 1228808 | tf_op jit(solution)/shard_map/ppermute | solution.py:22
  12.0 30.8 %collective-permute-start.13 = (bf16[200,1024]{1,0:T(8,128)(2,1)}, bf16[200,1024]{1,0:T(8,128)(2,1)S(1)}, u32[]{:S(2)}, u32[]{:S(2)}) collective-permute-start(bf16[200,1024]{1,0:T(8,128)(2,1)} %get-tuple-element.57), channel_id=1, source_target_pairs={{0,2},{1,3},{2,0},{3,1},{4,6},{5,7},{6,4},{7,5},{8,10},{9,11},{10,... | collective-permute-start | bytes 1228808 | tf_op jit(solution)/shard_map/ppermute | solution.py:22
  14.5 34.3 %collective-permute-start.14 = (bf16[200,1024]{1,0:T(8,128)(2,1)}, bf16[200,1024]{1,0:T(8,128)(2,1)S(1)}, u32[]{:S(2)}, u32[]{:S(2)}) collective-permute-start(bf16[200,1024]{1,0:T(8,128)(2,1)} %get-tuple-element.58), channel_id=1, source_target_pairs={{0,3},{1,0},{2,1},{3,2},{4,7},{5,4},{6,5},{7,6},{8,11},{9,8},{10,9... | collective-permute-start | bytes 1228808 | tf_op jit(solution)/shard_map/ppermute | solution.py:22
  17.1 36.3 %copy-start.1 = (bf16[200,512]{1,0:T(8,128)(2,1)S(1)}, bf16[200,512]{1,0:T(8,128)(2,1)}, u32[]{:S(2)}) copy-start(bf16[200,512]{1,0:T(8,128)(2,1)} %get-tuple-element.39.from_ref) | copy-start | bytes 614404
  17.1 18.6 %collective-permute-start.10 = (bf16[80,512]{1,0:T(8,128)(2,1)S(1)}, bf16[80,512]{1,0:T(8,128)(2,1)S(1)}, u32[]{:S(2)}, u32[]{:S(2)}) collective-permute-start(bf16[80,512]{1,0:T(8,128)(2,1)S(1)} %get-tuple-element.53), channel_id=1, source_target_pairs={{0,2},{1,3},{2,0},{3,1},{4,6},{5,7},{6,4},{7,5},{8,10},{9,11},{10,... | collective-permute-start | bytes 245768 | tf_op jit(solution)/shard_map/ppermute | solution.py:22
  19.4 5.7 %collective-permute-start.20 = (s32[1,8320]{1,0:T(1,128)S(1)}, s32[1,8320]{1,0:T(1,128)S(1)}, u32[]{:S(2)}, u32[]{:S(2)}) collective-permute-start(s32[1,8320]{1,0:T(1,128)S(1)} %reshape_add_fusion), channel_id=1, source_target_pairs={{0,4},{4,8},{8,12},{12,16},{16,20},{20,24},{24,28},{28,32},{32,36}... | collective-permute-start | bytes 99848 | tf_op jit(solution)/shard_map/ppermute | solution.py:22
  25.0 12.0 %collective-permute-start.11 = (bf16[80,512]{1,0:T(8,128)(2,1)S(1)}, bf16[80,512]{1,0:T(8,128)(2,1)S(1)}, u32[]{:S(2)}, u32[]{:S(2)}) collective-permute-start(bf16[80,512]{1,0:T(8,128)(2,1)S(1)} %get-tuple-element.54), channel_id=1, source_target_pairs={{0,3},{1,0},{2,1},{3,2},{4,7},{5,4},{6,5},{7,6},{8,11},{9,8},{10,9... | collective-permute-start | bytes 245768 | tf_op jit(solution)/shard_map/ppermute | solution.py:22
  35.7 4.5 %collective-permute-start.9 = (bf16[80,512]{1,0:T(8,128)(2,1)S(1)}, bf16[80,512]{1,0:T(8,128)(2,1)S(1)}, u32[]{:S(2)}, u32[]{:S(2)}) collective-permute-start(bf16[80,512]{1,0:T(8,128)(2,1)S(1)} %get-tuple-element.52), channel_id=1, source_target_pairs={{0,1},{1,2},{2,3},{3,0},{4,5},{5,6},{6,7},{7,4},{8,9},{9,10},{10,1... | collective-permute-start | bytes 245768 | tf_op jit(solution)/shard_map/ppermute | solution.py:22
  37.0 13.2 %collective-permute-start = (bf16[200,512]{1,0:T(8,128)(2,1)S(1)}, bf16[200,512]{1,0:T(8,128)(2,1)S(1)}, u32[]{:S(2)}, u32[]{:S(2)}) collective-permute-start(bf16[200,512]{1,0:T(8,128)(2,1)S(1)} %copy-done.12), channel_id=1, source_target_pairs={{0,1},{1,2},{2,3},{3,0},{4,5},{5,6},{6,7},{7,4},{8,9},{9,10},{10,1... | collective-permute-start | bytes 614408 | tf_op jit(solution)/shard_map/ppermute | solution.py:22
  40.2 11.2 %collective-permute-start.1 = (bf16[200,512]{1,0:T(8,128)(2,1)S(1)}, bf16[200,512]{1,0:T(8,128)(2,1)S(1)}, u32[]{:S(2)}, u32[]{:S(2)}) collective-permute-start(bf16[200,512]{1,0:T(8,128)(2,1)S(1)} %copy-done.11), channel_id=1, source_target_pairs={{0,2},{1,3},{2,0},{3,1},{4,6},{5,7},{6,4},{7,5},{8,10},{9,11},{10,... | collective-permute-start | bytes 614408 | tf_op jit(solution)/shard_map/ppermute | solution.py:22
  41.6 10.0 %collective-permute-start.2 = (bf16[200,512]{1,0:T(8,128)(2,1)S(1)}, bf16[200,512]{1,0:T(8,128)(2,1)S(1)}, u32[]{:S(2)}, u32[]{:S(2)}) collective-permute-start(bf16[200,512]{1,0:T(8,128)(2,1)S(1)} %copy-done.10), channel_id=1, source_target_pairs={{0,3},{1,0},{2,1},{3,2},{4,7},{5,4},{6,5},{7,6},{8,11},{9,8},{10,9... | collective-permute-start | bytes 614408 | tf_op jit(solution)/shard_map/ppermute | solution.py:22
  42.8 13.6 %collective-permute-start.18 = (bf16[80,512]{1,0:T(8,128)(2,1)S(1)}, bf16[80,512]{1,0:T(8,128)(2,1)S(1)}, u32[]{:S(2)}, u32[]{:S(2)}) collective-permute-start(bf16[80,512]{1,0:T(8,128)(2,1)S(1)} %get-tuple-element.63), channel_id=1, source_target_pairs={{0,4},{4,8},{8,12},{12,16},{16,20},{20,24},{24,28},{28,32},{32,36}... | collective-permute-start | bytes 245768 | tf_op jit(solution)/shard_map/ppermute | solution.py:22
  48.8 7.9 %collective-permute-start.19 = (bf16[80,512]{1,0:T(8,128)(2,1)S(1)}, bf16[80,512]{1,0:T(8,128)(2,1)S(1)}, u32[]{:S(2)}, u32[]{:S(2)}) collective-permute-start(bf16[80,512]{1,0:T(8,128)(2,1)S(1)} %get-tuple-element.64), channel_id=1, source_target_pairs={{0,124},{4,0},{8,4},{12,8},{16,12},{20,16},{24,20},{28,24},{32,28}... | collective-permute-start | bytes 245768 | tf_op jit(solution)/shard_map/ppermute | solution.py:22
  50.2 10.7 %collective-permute-start.15 = (bf16[80,1024]{1,0:T(8,128)(2,1)S(1)}, bf16[80,1024]{1,0:T(8,128)(2,1)S(1)}, u32[]{:S(2)}, u32[]{:S(2)}) collective-permute-start(bf16[80,1024]{1,0:T(8,128)(2,1)S(1)} %get-tuple-element.60), channel_id=1, source_target_pairs={{0,1},{1,2},{2,3},{3,0},{4,5},{5,6},{6,7},{7,4},{8,9},{9,10},{10,1... | collective-permute-start | bytes 491528 | tf_op jit(solution)/shard_map/ppermute | solution.py:22
  51.4 11.4 %collective-permute-start.16 = (bf16[80,1024]{1,0:T(8,128)(2,1)S(1)}, bf16[80,1024]{1,0:T(8,128)(2,1)S(1)}, u32[]{:S(2)}, u32[]{:S(2)}) collective-permute-start(bf16[80,1024]{1,0:T(8,128)(2,1)S(1)} %get-tuple-element.61), channel_id=1, source_target_pairs={{0,2},{1,3},{2,0},{3,1},{4,6},{5,7},{6,4},{7,5},{8,10},{9,11},{10,... | collective-permute-start | bytes 491528 | tf_op jit(solution)/shard_map/ppermute | solution.py:22
  51.6 11.1 %collective-permute-start.17 = (bf16[80,1024]{1,0:T(8,128)(2,1)S(1)}, bf16[80,1024]{1,0:T(8,128)(2,1)S(1)}, u32[]{:S(2)}, u32[]{:S(2)}) collective-permute-start(bf16[80,1024]{1,0:T(8,128)(2,1)S(1)} %get-tuple-element.62), channel_id=1, source_target_pairs={{0,3},{1,0},{2,1},{3,2},{4,7},{5,4},{6,5},{7,6},{8,11},{9,8},{10,9... | collective-permute-start | bytes 491528 | tf_op jit(solution)/shard_map/ppermute | solution.py:22
  56.5 9.8 %collective-permute-start.3 = (bf16[80,512]{1,0:T(8,128)(2,1)S(1)}, bf16[80,512]{1,0:T(8,128)(2,1)S(1)}, u32[]{:S(2)}, u32[]{:S(2)}) collective-permute-start(bf16[80,512]{1,0:T(8,128)(2,1)S(1)} %get-tuple-element.44), channel_id=1, source_target_pairs={{0,1},{1,2},{2,3},{3,0},{4,5},{5,6},{6,7},{7,4},{8,9},{9,10},{10,1... | collective-permute-start | bytes 245768 | tf_op jit(solution)/shard_map/ppermute | solution.py:22
  56.7 9.6 %collective-permute-start.4 = (bf16[80,512]{1,0:T(8,128)(2,1)S(1)}, bf16[80,512]{1,0:T(8,128)(2,1)S(1)}, u32[]{:S(2)}, u32[]{:S(2)}) collective-permute-start(bf16[80,512]{1,0:T(8,128)(2,1)S(1)} %get-tuple-element.45), channel_id=1, source_target_pairs={{0,2},{1,3},{2,0},{3,1},{4,6},{5,7},{6,4},{7,5},{8,10},{9,11},{10,... | collective-permute-start | bytes 245768 | tf_op jit(solution)/shard_map/ppermute | solution.py:22
  58.9 3.8 %copy-start.8 = (f32[65536]{0:T(1024)S(1)}, f32[65536]{0:T(1024)}, u32[]{:S(2)}) copy-start(f32[65536]{0:T(1024)} %param.14) | copy-start | bytes 786436
  58.9 3.8 %copy-start.9 = (f32[10]{0:T(128)S(1)}, f32[10]{0:T(128)}, u32[]{:S(2)}) copy-start(f32[10]{0:T(128)} %param.11) | copy-start | bytes 124
  60.9 5.4 %collective-permute-start.5 = (bf16[80,512]{1,0:T(8,128)(2,1)S(1)}, bf16[80,512]{1,0:T(8,128)(2,1)S(1)}, u32[]{:S(2)}, u32[]{:S(2)}) collective-permute-start(bf16[80,512]{1,0:T(8,128)(2,1)S(1)} %get-tuple-element.46), channel_id=1, source_target_pairs={{0,3},{1,0},{2,1},{3,2},{4,7},{5,4},{6,5},{7,6},{8,11},{9,8},{10,9... | collective-permute-start | bytes 245768 | tf_op jit(solution)/shard_map/ppermute | solution.py:22
  (2 other events, 7.6 us)
